TPU v7x, 1024 devices: a whole 4x4x32 slice. The times are simulated.
1024 devices in a mesh: blk: 8 (over y, core), uly: 4 (over x), dp: 32 (over z).
Axes of the slice: x: 4, y: 4, z: 32, core: 2. Of those that a mesh axis runs over, the one named last changes fastest.
Arguments:
- tokens: bfloat16 [8192, 4096], P(('uly', 'dp')), may hold values from -6 to 6
- expert_ids: int32 [8192, 8], P(('uly', 'dp')), may hold values from 0 to 127, all different within a row; in each aligned block of 64 rows (0 to 63, 64 to 127, ...) at most 5 rows name the same one
- route_weight: float32 [8192, 8], P(('uly', 'dp')), may hold values from 0.05 to 0.5
- w_gate: bfloat16 [128, 4096, 1024], P(('uly', 'dp'), None, 'blk'), may hold values from -0.09375 to 0.09375
- w_up: bfloat16 [128, 4096, 1024], P(('uly', 'dp'), None, 'blk'), may hold values from -0.09375 to 0.09375
- w_down: bfloat16 [128, 1024, 4096], P(('uly', 'dp'), 'blk'), may hold values from -0.1875 to 0.1875
Outputs:
- mixed: bfloat16 [8192, 4096], P(('uly', 'dp'), 'blk')
Inputs may be any that keep to these rules, and one draw needn't show every extreme that they name: `expert_ids`: each row names 8 different experts. In each aligned block of 64 rows (the rows of one device) no expert is named by more than 5 rows, and in some block one expert is named by exactly 5 rows.
All inputs are finite; a program needn't handle non-finite values.
Results may differ from a plain program's by a relative error of at most 0.015.
Values may be sent and summed in bfloat16 or wider, within the bound.
No kernel may reach another device: no remote copies, remote signals or barrier semaphores. Data moves between devices by JAX's collectives and lax.ppermute only.
A program may use at most 32 MiB of HBM per device.

v0:
```python
import jax
import jax.numpy as jnp
from jax import lax
from jax.sharding import PartitionSpec as P


def routing_tables(expert_ids, route_weight, groups, local_count, capacity):
    tokens_here, picks_count = expert_ids.shape
    experts = groups * local_count
    labels = lax.broadcasted_iota(jnp.int32, (1, 1, experts), 2)
    onehot = (expert_ids[:, :, None] == labels).astype(jnp.int32)
    chosen = jnp.sum(onehot, axis=1)
    before = jnp.cumsum(chosen, axis=0) - chosen
    slot_of = jnp.sum(onehot * before[:, None, :], axis=2)
    places = lax.broadcasted_iota(jnp.int32, (1, 1, capacity), 2)
    slot_hot = (slot_of[:, :, None] == places).astype(jnp.float32)
    expert_hot = onehot.astype(jnp.float32).reshape(tokens_here, picks_count, groups, local_count)
    placing = jnp.einsum("tkgl,tkc->gclt", expert_hot, slot_hot)
    placing = placing.reshape(groups * capacity * local_count, tokens_here)
    mixing = jnp.einsum("tkgl,tkc,tk->tgcl", expert_hot, slot_hot, route_weight)
    mixing = mixing.reshape(tokens_here, groups * capacity * local_count)
    return (placing.astype(jnp.bfloat16), mixing)


def local(tokens, expert_ids, route_weight, w_gate, w_up, w_down):
    ulysses_size = lax.axis_size("uly")
    data_size = lax.axis_size("dp")
    cycle_size = lax.axis_size("blk")
    tokens_here, model_width = tokens.shape
    local_count = w_gate.shape[0]
    groups = ulysses_size * data_size
    experts = groups * local_count
    picks_count = expert_ids.shape[1]
    capacity = min(tokens_here, max(2, 5 * tokens_here * picks_count // (4 * experts)))
    placing, mixing = routing_tables(expert_ids, route_weight, groups, local_count, capacity)
    slice_width = model_width // cycle_size
    rows_total = groups * capacity
    cycle_index = lax.axis_index("blk")
    own_part = lax.dynamic_slice_in_dim(tokens, cycle_index * slice_width, slice_width, 1)
    outgoing = jnp.dot(placing, own_part, preferred_element_type=jnp.float32).astype(jnp.bfloat16)
    outgoing = outgoing.reshape(ulysses_size, data_size, capacity, local_count, slice_width)
    arrived = lax.all_to_all(
        lax.all_to_all(outgoing, "uly", split_axis=0, concat_axis=0, tiled=True),
        "dp",
        split_axis=1,
        concat_axis=1,
        tiled=True,
    )
    arrived = arrived.reshape(rows_total, local_count, slice_width)
    portion = lax.all_gather(arrived, "blk", axis=2, tiled=True)
    gate_more = jnp.einsum("rlw,lwf->rlf", portion, w_gate, preferred_element_type=jnp.float32)
    up_more = jnp.einsum("rlw,lwf->rlf", portion, w_up, preferred_element_type=jnp.float32)
    hidden = (jax.nn.silu(gate_more) * up_more).astype(jnp.bfloat16)
    partial_value = jnp.einsum("lfd,rlf->drl", w_down, hidden, preferred_element_type=jnp.float32)
    summed = lax.psum_scatter(
        partial_value.reshape(slice_width * lax.axis_size("blk"), rows_total * local_count).astype(
            jnp.bfloat16
        ),
        "blk",
        scatter_dimension=0,
        tiled=True,
    )
    returned = summed.reshape(slice_width, ulysses_size, data_size, capacity, local_count)
    returned_rows = lax.all_to_all(
        lax.all_to_all(returned, "uly", split_axis=1, concat_axis=1, tiled=True),
        "dp",
        split_axis=2,
        concat_axis=2,
        tiled=True,
    )
    returned_rows = returned_rows.reshape(slice_width, rows_total * local_count).astype(jnp.float32)
    mixed = lax.dot_general(
        mixing, returned_rows, (((1,), (1,)), ((), ())), precision=lax.Precision.HIGHEST
    )
    return mixed.astype(jnp.bfloat16)


def solution(mesh):
    return jax.shard_map(
        local,
        mesh=mesh,
        in_specs=(
            P(("uly", "dp"), None),
            P(("uly", "dp"), None),
            P(("uly", "dp"), None),
            P(("uly", "dp"), None, "blk"),
            P(("uly", "dp"), None, "blk"),
            P(("uly", "dp"), "blk", None),
        ),
        out_specs=P(("uly", "dp"), "blk"),
        check_vma=False,
    )
```

profile of v0, /device:TPU:25, one launch (start us, length us, event | category | flops | bytes accessed | tf_op | source)
XLA Modules:
  0.0 361.1 jit_solution(10190874067728886654)
XLA Ops:
  6.5 0.0 copy-start
  6.5 0.0 all-gather.2.cloned.1.call-start
  6.5 0.9 copy.13
  7.4 0.1 convert_reduce_fusion
  7.6 0.1 reduce_window_sum.11
  7.7 1.2 select_reduce_fusion
  8.9 0.3 fusion.22
  9.2 0.2 copy.16
  9.4 0.1 convert_element_type.52
  9.5 1.1 convolution_convert_fusion.1
  10.7 0.3 reshape.57
  10.9 0.2 copy.17
  11.2 13.8 %all_to_all.20 = bf16[4,32,5,1,512]{4,1,3,2,0:T(8,128)(2,1)S(1)} all-to-all(bf16[4,32,5,1,512]{4,1,3,2,0:T(8,128)(2,1)S(1)} %copy.17), channel_id=1, replica_groups=mesh['blk'=8,'uly'=4,'dp'=32] {'uly'}, dimensions={0} | all-to-all | bytes 1310720 | tf_op jit(solution)/shard_map/all_to_all | solution.py:43
  25.0 0.5 copy.18
  25.5 103.9 %all_to_all.21 = bf16[4,32,5,1,512]{4,0,3,2,1:T(4,128)(2,1)S(1)} all-to-all(bf16[4,32,5,1,512]{4,0,3,2,1:T(4,128)(2,1)S(1)} %copy.18), channel_id=1, replica_groups=mesh['blk'=8,'uly'=4,'dp'=32] {'dp'}, dimensions={1} | all-to-all | bytes 1310720 | tf_op jit(solution)/shard_map/all_to_all | solution.py:42
  129.5 0.2 copy.19
  129.7 0.0 copy-start.1
  129.7 1.1 reshape.58
  130.8 0.0 all-gather.2.cloned.1.call-update
  130.8 0.0 reduce-scatter.2.cloned.1.call-start
  130.9 33.0 %all-gather.2.cloned.1.call-done = bf16[640,1,4096]{2,0,1:T(8,128)(2,1)} async-done(((bf16[640,1,512]{2,0,1:T(8,128)(2,1)}), bf16[640,1,4096]{2,0,1:T(8,128)(2,1)}) %all-gather.2.cloned.1.call-update) | async-done | bytes 5242896 | tf_op jit(solution)/shard_map/all_gather | solution.py:50
  163.8 4.3 %fusion.5 = f32[640,1,128]{2,0,1:T(8,128)S(1)} fusion(bf16[640,1,4096]{2,0,1:T(8,128)(2,1)} %all-gather.2.cloned.1.call-done, bf16[1,4096,128]{2,1,0:T(8,128)(2,1)} %param.9), kind=kOutput, calls=%fused_computation.7 | convolution fusion | flops 671088640 | bytes 6619136 | tf_op jit(solution)/shard_map/rlw,lwf->rlf/dot_general | solution.py:51
  168.1 0.0 copy-done
  168.2 0.0 copy-done.1
  168.2 10.4 %fusion = bf16[4096,640]{0,1:T(8,128)(2,1)} fusion(bf16[640,1,4096]{2,0,1:T(8,128)(2,1)} %all-gather.2.cloned.1.call-done, bf16[1,128,4096]{2,1,0:T(8,128)(2,1)S(1)} %copy-done, bf16[1,4096,128]{2,1,0:T(8,128)(2,1)S(1)} %copy-done.1, f32[640,1,128]{2,0,1:T(8,128)S(1)} %fusion.5), kind=kOutput, calls=%fused_computation.1 | convolution fusion | flops 1345290240 | bytes 12910592 | tf_op jit(solution)/shard_map/lfd,rlf->drl/dot_general | solution.py:54
  178.5 0.0 copy-start.2
  178.5 0.0 reduce-scatter.2.cloned.1.call-update
  178.6 60.6 %reduce-scatter.2.cloned.1.call-done = bf16[512,640]{0,1:T(8,128)(2,1)} async-done(((bf16[4096,640]{0,1:T(8,128)(2,1)}), bf16[512,640]{0,1:T(8,128)(2,1)}) %reduce-scatter.2.cloned.1.call-update) | async-done | bytes 655376 | tf_op jit(solution)/shard_map/reduce_scatter | solution.py:55
  239.1 1.3 reshape.64
  240.4 0.2 copy.20
  240.7 11.9 %all_to_all.22 = bf16[512,4,32,5,1]{0,2,4,3,1:T(8,128)(2,1)S(1)} all-to-all(bf16[512,4,32,5,1]{0,2,4,3,1:T(8,128)(2,1)S(1)} %copy.20), channel_id=1, replica_groups=mesh['blk'=8,'uly'=4,'dp'=32] {'uly'}, dimensions={1} | all-to-all | bytes 1310720 | tf_op jit(solution)/shard_map/all_to_all | solution.py:65
  252.6 1.3 copy.21
  253.9 22.6 %all-to-all-start.3 = ((bf16[512,4,32,5,1]{0,1,4,3,2:T(4,128)(2,1)}), bf16[512,4,32,5,1]{0,1,4,3,2:T(4,128)(2,1)S(1)}, u32[]{:S(2)}, u32[]{:S(2)}) async-start(bf16[512,4,32,5,1]{0,1,4,3,2:T(4,128)(2,1)} %copy.21), calls=%async_computation.4 | async-start | bytes 1310720 | tf_op jit(solution)/shard_map/all_to_all | solution.py:64
  276.5 0.0 copy-done.2
  276.5 0.1 copy.14
  276.6 0.3 convolution_bitcast_fusion
  276.9 0.3 copy.15
  277.2 75.5 %all-to-all-done.3 = bf16[512,4,32,5,1]{0,1,4,3,2:T(4,128)(2,1)S(1)} async-done(((bf16[512,4,32,5,1]{0,1,4,3,2:T(4,128)(2,1)}), bf16[512,4,32,5,1]{0,1,4,3,2:T(4,128)(2,1)S(1)}, u32[]{:S(2)}, u32[]{:S(2)}) %all-to-all-start.3) | async-done | bytes 655392 | tf_op jit(solution)/shard_map/all_to_all | solution.py:64
  352.7 0.2 copy.22
  352.9 0.3 reshape.65
  353.2 1.1 convolution_convert_fusion.3
  (2 shorter events, 0.1 us)
Async XLA Ops:
  6.5 161.6 %copy-start = (bf16[1,128,4096]{2,1,0:T(8,128)(2,1)S(1)}, bf16[1,128,4096]{2,1,0:T(8,128)(2,1)}, u32[]{:S(2)}) copy-start(bf16[1,128,4096]{2,1,0:T(8,128)(2,1)} %param.11) | copy-start | bytes 3145732
  6.5 157.3 %all-gather.2.cloned.1.call-start = ((), (), s32[]{:S(2)}) async-start(), calls=%async_computation.5 | async-start | bytes 5898240 | tf_op jit(solution)/shard_map/all_gather | solution.py:50
  129.7 38.5 %copy-start.1 = (bf16[1,4096,128]{2,1,0:T(8,128)(2,1)S(1)}, bf16[1,4096,128]{2,1,0:T(8,128)(2,1)}, u32[]{:S(2)}) copy-start(bf16[1,4096,128]{2,1,0:T(8,128)(2,1)} %param.10) | copy-start | bytes 3145732
  130.8 108.3 %reduce-scatter.2.cloned.1.call-start = ((), (), s32[]{:S(2)}) async-start(), calls=%async_computation.6 | async-start | bytes 5898240 | tf_op jit(solution)/shard_map/reduce_scatter | solution.py:55
  178.5 98.0 %copy-start.2 = (f32[64,8]{0,1:T(8,128)S(1)}, f32[64,8]{0,1:T(8,128)}, u32[]{:S(2)}) copy-start(f32[64,8]{0,1:T(8,128)} %param.8) | copy-start | bytes 6148
  253.9 98.8 %all-to-all-start.3 = ((bf16[512,4,32,5,1]{0,1,4,3,2:T(4,128)(2,1)}), bf16[512,4,32,5,1]{0,1,4,3,2:T(4,128)(2,1)S(1)}, u32[]{:S(2)}, u32[]{:S(2)}) async-start(bf16[512,4,32,5,1]{0,1,4,3,2:T(4,128)(2,1)} %copy.21), calls=%async_computation.4 | async-start | bytes 1310720 | tf_op jit(solution)/shard_map/all_to_all | solution.py:64
Sparse Core Ops, SparseCore 0:
  130.9 32.8 all-gather.1
  178.7 60.3 reduce-scatter.1
where the time goes:
time: 362 us; the launch traced here: 361 us
  waiting for transfers between devices  169 us (47%)
  blocking collectives  130 us (36%)
  starting transfers between devices  22.6 us (6%)
  matrix products  17.5 us (5%)
  between operations  13.6 us (4%)
  local copies, waits for them, and re-layouts  7.25 us (2%)
    all_to_all x1, blocking collectives, local(): lax.all_to_all(lax.all_to_all(outgoing, 'uly', split_axis=0, concat_axis=...  104 us
    all_to_all x1, waiting for transfers between devices, local(): lax.all_to_all(lax.all_to_all(returned, 'uly', split_axis=1, concat_axis=...  75.5 us
    reduce_scatter x1, waiting for transfers between devices, local(): lax.psum_scatter(partial_value.reshape(slice_width * lax.axis_size('blk')...  60.6 us
    all_gather x1, waiting for transfers between devices, local(): portion = lax.all_gather(arrived, 'blk', axis=2, tiled=True)  33 us
    all_to_all x1, starting transfers between devices, local(): lax.all_to_all(lax.all_to_all(returned, 'uly', split_axis=1, concat_axis=...  22.6 us
    all_to_all x1, blocking collectives, local(): lax.all_to_all(outgoing, 'uly', split_axis=0, concat_axis=0, tiled=True)  13.8 us
    all_to_all x1, blocking collectives, local(): lax.all_to_all(returned, 'uly', split_axis=1, concat_axis=1, tiled=True)  11.9 us
    dot_general x1, matrix products, local(): jnp.einsum('lfd,rlf->drl', w_down, hidden, preferred_element_type=jnp.flo...  10.4 us
  transfers between devices with their start and end apart: 3, of which 3 were waited for; matrix products, arithmetic and copies ran while one was open for 0% of the time, Pallas kernels for 0%

commit v1 on v0

v1 whole, which is shorter than its diff:
```python
import jax
import jax.numpy as jnp
import numpy as np
from jax import lax
from jax.sharding import PartitionSpec as P

CAPACITY = 5
STEPS = 4
FORWARD = ((16, 9, 8, 1), (15, 10, 7, 2), (14, 11, 6, 3), (13, 12, 5, 4))
BACKWARD = ((15, 8, 7, 0), (14, 9, 6, 1), (13, 10, 5, 2), (12, 11, 4, 3))


def shift_table(n_blk, n_dp):
    rows = []
    for b in range(n_blk):
        if b % 2 == 0:
            rows.append([s for s in FORWARD[b // 2]])
        else:
            rows.append([(-s) % n_dp for s in BACKWARD[b // 2]])
    return np.array(rows, np.int32)


def move(value, shifts, step, sign, n_blk, n_dp):
    pairs = []
    for b in range(n_blk):
        s = sign * int(shifts[b, step])
        for z in range(n_dp):
            pairs.append((b * n_dp + z, b * n_dp + (z + s) % n_dp))
    return lax.ppermute(value, ("blk", "dp"), pairs)


def local(tokens, expert_ids, route_weight, w_gate, w_up, w_down):
    n_uly = lax.axis_size("uly")
    n_dp = lax.axis_size("dp")
    n_blk = lax.axis_size("blk")
    tokens_here, width = tokens.shape
    part = width // n_blk
    shifts = shift_table(n_blk, n_dp)
    b = lax.axis_index("blk")
    z = lax.axis_index("dp")

    w_down_full = lax.all_gather(w_down[0], "blk", axis=0, tiled=True)

    own_shifts = lax.dynamic_slice_in_dim(jnp.asarray(shifts), b, 1, 0)[0]
    z_of = (z + own_shifts) % n_dp
    experts = (jnp.arange(n_uly, dtype=jnp.int32)[:, None] * n_dp + z_of[None, :]).reshape(-1)
    hit = expert_ids[:, :, None] == experts[None, None, :]
    chosen = jnp.sum(hit.astype(jnp.float32), axis=1)
    weight = jnp.sum(jnp.where(hit, route_weight[:, :, None], 0.0), axis=1)
    row_i = lax.broadcasted_iota(jnp.int32, (tokens_here, tokens_here), 0)
    col_i = lax.broadcasted_iota(jnp.int32, (tokens_here, tokens_here), 1)
    earlier = (col_i < row_i).astype(jnp.float32)
    before = jnp.dot(earlier, chosen, preferred_element_type=jnp.float32)
    places = jnp.arange(CAPACITY, dtype=jnp.float32)
    at = (before.reshape(tokens_here, n_uly, 1, STEPS) == places[None, None, :, None]).astype(jnp.float32)
    placing = (at * chosen.reshape(tokens_here, n_uly, 1, STEPS)).astype(jnp.bfloat16)
    mixing = at * weight.reshape(tokens_here, n_uly, 1, STEPS)

    rows = n_uly * CAPACITY * STEPS
    outgoing = lax.dot_general(
        placing.reshape(tokens_here, rows), tokens, (((0,), (0,)), ((), ())), preferred_element_type=jnp.float32
    ).astype(jnp.bfloat16)
    outgoing = outgoing.reshape(n_uly, CAPACITY, STEPS, width)
    crossed = lax.all_to_all(outgoing, "uly", split_axis=0, concat_axis=0, tiled=True)
    arrived = []
    for j in range(STEPS):
        chunk = jnp.transpose(crossed[:, :, j, :], (1, 0, 2))
        arrived.append(move(chunk, shifts, j, 1, n_blk, n_dp))
    mine = jnp.stack(arrived).reshape(rows, width)
    mine, w_down_full = lax.optimization_barrier((mine, w_down_full))
    everyone = lax.all_gather(mine, "blk", axis=0, tiled=True)
    gate = jnp.dot(everyone, w_gate[0], preferred_element_type=jnp.float32)
    up = jnp.dot(everyone, w_up[0], preferred_element_type=jnp.float32)
    hidden = (jax.nn.silu(gate) * up).astype(jnp.bfloat16)
    hidden = hidden.reshape(n_blk, rows, hidden.shape[1])
    hidden = lax.all_to_all(hidden, "blk", split_axis=0, concat_axis=0, tiled=True)
    hidden = jnp.transpose(hidden, (1, 0, 2)).reshape(rows, -1)
    answer = jnp.dot(hidden, w_down_full, preferred_element_type=jnp.float32).astype(jnp.bfloat16)
    answer = answer.reshape(STEPS, CAPACITY, n_uly, width)
    back = [move(answer[j], shifts, j, -1, n_blk, n_dp) for j in range(STEPS)]
    back = jnp.transpose(jnp.stack(back), (2, 1, 0, 3))
    home = lax.all_to_all(back, "uly", split_axis=0, concat_axis=0, tiled=True).reshape(rows, width)
    mixed = jnp.dot(mixing.reshape(tokens_here, rows), home.astype(jnp.float32), precision=lax.Precision.HIGHEST)
    mixed = mixed.astype(jnp.bfloat16).reshape(tokens_here, n_blk, part)
    mixed = lax.all_to_all(jnp.transpose(mixed, (1, 0, 2)), "blk", split_axis=0, concat_axis=0, tiled=True)
    return jnp.sum(mixed.astype(jnp.float32), axis=0).astype(jnp.bfloat16)


def solution(mesh):
    return jax.shard_map(
        local,
        mesh=mesh,
        in_specs=(
            P(("uly", "dp"), None),
            P(("uly", "dp"), None),
            P(("uly", "dp"), None),
            P(("uly", "dp"), None, "blk"),
            P(("uly", "dp"), None, "blk"),
            P(("uly", "dp"), "blk", None),
        ),
        out_specs=P(("uly", "dp"), "blk"),
        check_vma=False,
    )
```

time: 362 us -> 311 us (0.86)
  blocking collectives: 130 us -> 68.3 us
  starting transfers between devices: 22.6 us -> 65.5 us
  waiting for transfers between devices: 169 us -> 140 us
  matrix products: 17.5 us -> 12.5 us
    ppermute x0 -> x8, waiting for transfers between devices: none -> 80.8 us  [move(): return lax.ppermute(value, ('blk', 'dp'), pairs)]
    all_to_all x1 -> x0, waiting for transfers between devices: 75.5 us -> none  [local(): lax.all_to_all(lax.all_to_all(returned, 'uly', split_axis=1, concat_axis=...]
    ppermute x0 -> x8, starting transfers between devices: none -> 65.5 us  [move(): return lax.ppermute(value, ('blk', 'dp'), pairs)]
    all_to_all x2 -> x3, blocking collectives: 116 us -> 54.5 us  [the longest x1 34.4 us: local(): lax.all_to_all(jnp.transpose(mixed, (1, 0, 2)), 'blk', split_axis=0, conc...]
    reduce_scatter x1 -> x0, waiting for transfers between devices: 60.6 us -> none  [local(): lax.psum_scatter(partial_value.reshape(slice_width * lax.axis_size('blk')...]
    all_gather x1 -> x2, waiting for transfers between devices: 33 us -> 58.3 us  [the longest x1 58.3 us: local(): everyone = lax.all_gather(mine, 'blk', axis=0, tiled=True)]
    all_to_all x1 -> x0, starting transfers between devices: 22.6 us -> none  [local(): lax.all_to_all(lax.all_to_all(returned, 'uly', split_axis=1, concat_axis=...]
    dot_general x6, matrix products: 17.5 us -> 12.5 us  [the longest x1 4.15 us: local(): up = jnp.dot(everyone, w_up[0], preferred_element_type=jnp.float32)]
  transfers between devices with their start and end apart: 3 -> 10, of which waited for: 3 -> 5; matrix products, arithmetic and copies ran while one was open for 0% -> 2% of each run, Pallas kernels for 0% -> 0%
where the time goes in v1:
time: 311 us; the launch traced here: 308 us
  waiting for transfers between devices  140 us (45%)
  blocking collectives  68.3 us (22%)
  starting transfers between devices  65.5 us (21%)
  between operations  13.6 us (4%)
  matrix products  12.5 us (4%)
  local copies, waits for them, and re-layouts  4.72 us (2%)
  other arithmetic  3.47 us (1%)
    ppermute x8, waiting for transfers between devices, move(): return lax.ppermute(value, ('blk', 'dp'), pairs)  80.8 us
    ppermute x8, starting transfers between devices, move(): return lax.ppermute(value, ('blk', 'dp'), pairs)  65.5 us
    all_gather x1, waiting for transfers between devices, local(): everyone = lax.all_gather(mine, 'blk', axis=0, tiled=True)  58.3 us
    all_to_all x1, blocking collectives, local(): lax.all_to_all(jnp.transpose(mixed, (1, 0, 2)), 'blk', split_axis=0, conc...  34.4 us
    all_to_all x1, blocking collectives, local(): lax.all_to_all(outgoing, 'uly', split_axis=0, concat_axis=0, tiled=True)  13.8 us
    all_to_all x1, blocking collectives, local(): lax.all_to_all(back, 'uly', split_axis=0, concat_axis=0, tiled=True)  11.1 us
    all_to_all x1, blocking collectives, local(): lax.all_to_all(hidden, 'blk', split_axis=0, concat_axis=0, tiled=True)  8.96 us
  transfers between devices with their start and end apart: 10, of which 5 were waited for; matrix products, arithmetic and copies ran while one was open for 2% of the time, Pallas kernels for 0%

profile of v1, /device:TPU:25, one launch (start us, length us, event | category | flops | bytes accessed | tf_op | source)
XLA Modules:
  0.0 307.9 jit_solution(10142285890561670986)
XLA Ops:
  6.5 0.0 copy-start
  6.5 0.0 all-gather.6.cloned.1.call-start
  6.5 0.7 all-gather.6.cloned.1.call-update
  7.3 0.0 all-gather.4.cloned.1.call-start
  7.3 0.7 fusion.18
  8.0 0.1 broadcast_add_fusion
  8.1 0.1 add.51
  8.2 0.1 eq.47
  8.3 0.8 fusion.8
  9.1 0.1 fusion.11
  9.3 1.4 convolution_convert_fusion.1
  10.7 0.2 reshape.64
  10.9 13.8 %all_to_all.20 = bf16[4,5,4,4096]{3,2,1,0:T(4,128)(2,1)S(1)} all-to-all(bf16[4,5,4,4096]{3,2,1,0:T(4,128)(2,1)S(1)} %reshape.64), channel_id=1, replica_groups=mesh['blk'=8,'uly'=4,'dp'=32] {'uly'}, dimensions={0} | all-to-all | bytes 1310720 | tf_op jit(solution)/shard_map/all_to_all | solution.py:64
  24.8 1.4 fusion.23
  26.2 0.2 copy.84
  26.4 0.2 copy.83
  26.7 0.2 copy.85
  26.9 0.2 copy.82
  27.1 19.7 %collective-permute-start.2 = (bf16[5,4,4096]{2,1,0:T(4,128)(2,1)S(1)}, bf16[5,4,4096]{2,1,0:T(4,128)(2,1)S(1)}, u32[]{:S(2)}, u32[]{:S(2)}) collective-permute-start(bf16[5,4,4096]{2,1,0:T(4,128)(2,1)S(1)} %bitcast.95), channel_id=1, source_target_pairs={{0,8},{1,9},{2,10},{3,11},{4,12},{5,13},{6,14},{7,15},{8,16},{9,17... | collective-permute-start | bytes 491528 | tf_op jit(solution)/shard_map/ppermute | solution.py:29
  46.8 4.7 %collective-permute-start.3 = (bf16[5,4,4096]{2,1,0:T(4,128)(2,1)S(1)}, bf16[5,4,4096]{2,1,0:T(4,128)(2,1)S(1)}, u32[]{:S(2)}, u32[]{:S(2)}) collective-permute-start(bf16[5,4,4096]{2,1,0:T(4,128)(2,1)S(1)} %bitcast.94), channel_id=1, source_target_pairs={{0,1},{1,2},{2,3},{3,4},{4,5},{5,6},{6,7},{7,8},{8,9},{9,10},{10,1... | collective-permute-start | bytes 491528 | tf_op jit(solution)/shard_map/ppermute | solution.py:29
  51.6 7.9 %collective-permute-start.1 = (bf16[5,4,4096]{2,1,0:T(4,128)(2,1)S(1)}, bf16[5,4,4096]{2,1,0:T(4,128)(2,1)S(1)}, u32[]{:S(2)}, u32[]{:S(2)}) collective-permute-start(bf16[5,4,4096]{2,1,0:T(4,128)(2,1)S(1)} %bitcast.93), channel_id=1, source_target_pairs={{0,9},{1,10},{2,11},{3,12},{4,13},{5,14},{6,15},{7,16},{8,17},{9,1... | collective-permute-start | bytes 491528 | tf_op jit(solution)/shard_map/ppermute | solution.py:29
  59.5 2.4 collective-permute-start
  61.9 0.0 collective-permute-done.2
  61.9 0.0 collective-permute-done.3
  61.9 20.0 %collective-permute-done.1 = bf16[5,4,4096]{2,1,0:T(4,128)(2,1)S(1)} collective-permute-done((bf16[5,4,4096]{2,1,0:T(4,128)(2,1)S(1)}, bf16[5,4,4096]{2,1,0:T(4,128)(2,1)S(1)}, u32[]{:S(2)}, u32[]{:S(2)}) %collective-permute-start.1) | collective-permute-done | bytes 163872 | tf_op jit(solution)/shard_map/ppermute | solution.py:29
  81.9 25.4 %collective-permute-done = bf16[5,4,4096]{2,1,0:T(4,128)(2,1)S(1)} collective-permute-done((bf16[5,4,4096]{2,1,0:T(4,128)(2,1)S(1)}, bf16[5,4,4096]{2,1,0:T(4,128)(2,1)S(1)}, u32[]{:S(2)}, u32[]{:S(2)}) %collective-permute-start) | collective-permute-done | bytes 163872 | tf_op jit(solution)/shard_map/ppermute | solution.py:29
  107.3 0.0 copy-start.1
  107.3 0.6 pad_maximum_fusion
  107.9 1.0 reshape.65
  108.9 0.0 all-gather.6.cloned.1.call-done
  108.9 0.0 all-gather.4.cloned.1.call-update
  109.0 58.3 %all-gather.4.cloned.1.call-done = bf16[640,4096]{1,0:T(8,128)(2,1)} async-done(((bf16[80,4096]{1,0:T(8,128)(2,1)}), bf16[640,4096]{1,0:T(8,128)(2,1)}) %all-gather.4.cloned.1.call-update) | async-done | bytes 5242896 | tf_op jit(solution)/shard_map/all_gather | solution.py:71
  167.3 0.0 copy-done
  167.3 0.0 slice-start
  167.3 4.1 %fusion.3 = f32[640,128]{1,0:T(8,128)S(1)} fusion(bf16[640,4096]{1,0:T(8,128)(2,1)} %all-gather.4.cloned.1.call-done, bf16[1,4096,128]{2,1,0:T(8,128)(2,1)S(1)} %copy-done), kind=kOutput, calls=%fused_computation.7 | convolution fusion | flops 671088640 | bytes 6619136 | tf_op jit(solution)/shard_map/dot_general | solution.py:72
  171.4 0.0 copy-done.1
  171.4 0.0 slice-start.1
  171.4 4.2 %fusion.1 = bf16[640,128]{1,0:T(8,128)(2,1)S(1)} fusion(bf16[640,4096]{1,0:T(8,128)(2,1)} %all-gather.4.cloned.1.call-done, bf16[1,4096,128]{2,1,0:T(8,128)(2,1)S(1)} %copy-done.1, f32[640,128]{1,0:T(8,128)S(1)} %fusion.3), kind=kOutput, calls=%fused_computation.5 | convolution fusion | flops 671580160 | bytes 6782976 | tf_op jit(solution)/shard_map/dot_general | solution.py:73
  175.6 9.0 %all_to_all.21 = bf16[8,80,128]{2,1,0:T(8,128)(2,1)S(1)} all-to-all(bf16[8,80,128]{2,1,0:T(8,128)(2,1)S(1)} %bitcast.91), channel_id=1, replica_groups=mesh['blk'=8,'uly'=4,'dp'=32] {'blk'}, dimensions={0} | all-to-all | bytes 327680 | tf_op jit(solution)/shard_map/all_to_all | solution.py:76
  184.6 0.0 slice-done
  184.6 0.0 slice-done.1
  184.6 1.6 convolution_convert_fusion
  186.1 0.1 fusion.22
  186.2 0.1 squeeze.41
  186.3 0.1 squeeze.44
  186.4 0.1 squeeze.43
  186.5 0.1 squeeze.42
  186.6 15.5 %collective-permute-start.5 = (bf16[5,4,4096]{2,1,0:T(4,128)(2,1)S(1)}, bf16[5,4,4096]{2,1,0:T(4,128)(2,1)S(1)}, u32[]{:S(2)}, u32[]{:S(2)}) collective-permute-start(bf16[5,4,4096]{2,1,0:T(4,128)(2,1)S(1)} %squeeze.42), channel_id=1, source_target_pairs={{0,23},{1,24},{2,25},{3,26},{4,27},{5,28},{6,29},{7,30},{8,31},{9,... | collective-permute-start | bytes 491528 | tf_op jit(solution)/shard_map/ppermute | solution.py:29
  202.1 7.4 %collective-permute-start.6 = (bf16[5,4,4096]{2,1,0:T(4,128)(2,1)S(1)}, bf16[5,4,4096]{2,1,0:T(4,128)(2,1)S(1)}, u32[]{:S(2)}, u32[]{:S(2)}) collective-permute-start(bf16[5,4,4096]{2,1,0:T(4,128)(2,1)S(1)} %squeeze.43), channel_id=1, source_target_pairs={{0,24},{1,25},{2,26},{3,27},{4,28},{5,29},{6,30},{7,31},{8,0},{9,1... | collective-permute-start | bytes 491528 | tf_op jit(solution)/shard_map/ppermute | solution.py:29
  209.4 4.6 %collective-permute-start.7 = (bf16[5,4,4096]{2,1,0:T(4,128)(2,1)S(1)}, bf16[5,4,4096]{2,1,0:T(4,128)(2,1)S(1)}, u32[]{:S(2)}, u32[]{:S(2)}) collective-permute-start(bf16[5,4,4096]{2,1,0:T(4,128)(2,1)S(1)} %squeeze.44), channel_id=1, source_target_pairs={{0,31},{1,0},{2,1},{3,2},{4,3},{5,4},{6,5},{7,6},{8,7},{9,8},{10,9... | collective-permute-start | bytes 491528 | tf_op jit(solution)/shard_map/ppermute | solution.py:29
  214.0 3.3 %collective-permute-start.4 = (bf16[5,4,4096]{2,1,0:T(4,128)(2,1)S(1)}, bf16[5,4,4096]{2,1,0:T(4,128)(2,1)S(1)}, u32[]{:S(2)}, u32[]{:S(2)}) collective-permute-start(bf16[5,4,4096]{2,1,0:T(4,128)(2,1)S(1)} %squeeze.41), channel_id=1, source_target_pairs={{0,16},{1,17},{2,18},{3,19},{4,20},{5,21},{6,22},{7,23},{8,24},{9,... | collective-permute-start | bytes 491528 | tf_op jit(solution)/shard_map/ppermute | solution.py:29
  217.3 0.0 collective-permute-done.5
  217.4 15.0 %collective-permute-done.6 = bf16[5,4,4096]{2,1,0:T(4,128)(2,1)S(1)} collective-permute-done((bf16[5,4,4096]{2,1,0:T(4,128)(2,1)S(1)}, bf16[5,4,4096]{2,1,0:T(4,128)(2,1)S(1)}, u32[]{:S(2)}, u32[]{:S(2)}) %collective-permute-start.6) | collective-permute-done | bytes 163872 | tf_op jit(solution)/shard_map/ppermute | solution.py:29
  232.3 0.0 collective-permute-done.7
  232.3 20.3 %collective-permute-done.4 = bf16[5,4,4096]{2,1,0:T(4,128)(2,1)S(1)} collective-permute-done((bf16[5,4,4096]{2,1,0:T(4,128)(2,1)S(1)}, bf16[5,4,4096]{2,1,0:T(4,128)(2,1)S(1)}, u32[]{:S(2)}, u32[]{:S(2)}) %collective-permute-start.4) | collective-permute-done | bytes 163872 | tf_op jit(solution)/shard_map/ppermute | solution.py:29
  252.7 0.6 maximum_bitcast_fusion
  253.2 0.5 copy.64
  253.8 11.1 %all_to_all.22 = bf16[4,5,4,4096]{3,2,1,0:T(4,128)(2,1)S(1)} all-to-all(bf16[4,5,4,4096]{3,2,1,0:T(4,128)(2,1)S(1)} %copy.64), channel_id=1, replica_groups=mesh['blk'=8,'uly'=4,'dp'=32] {'uly'}, dimensions={0} | all-to-all | bytes 1310720 | tf_op jit(solution)/shard_map/all_to_all | solution.py:82
  264.9 1.1 fusion
  266.0 34.4 %all_to_all.23 = bf16[8,64,512]{2,1,0:T(8,128)(2,1)S(1)} all-to-all(bf16[8,64,512]{2,1,0:T(8,128)(2,1)S(1)} %bitcast.80), channel_id=1, replica_groups=mesh['blk'=8,'uly'=4,'dp'=32] {'blk'}, dimensions={0} | all-to-all | bytes 1048576 | tf_op jit(solution)/shard_map/all_to_all | solution.py:85
  300.4 0.7 reduce_sum.32
  (6 shorter events, 0.1 us)
Async XLA Ops:
  6.5 160.7 %copy-start = (bf16[1,4096,128]{2,1,0:T(8,128)(2,1)S(1)}, bf16[1,4096,128]{2,1,0:T(8,128)(2,1)}, u32[]{:S(2)}) copy-start(bf16[1,4096,128]{2,1,0:T(8,128)(2,1)} %param.10) | copy-start | bytes 3145732
  6.5 102.4 %all-gather.6.cloned.1.call-start = ((), (), s32[]{:S(2)}) async-start(), calls=%async_computation.5 | async-start | bytes 9437184 | tf_op jit(solution)/shard_map/all_gather | solution.py:42
  7.3 160.0 %all-gather.4.cloned.1.call-start = ((), (), s32[]{:S(2)}) async-start(), calls=%async_computation.4 | async-start | bytes 5898240 | tf_op jit(solution)/shard_map/all_gather | solution.py:71
  27.1 34.8 %collective-permute-start.2 = (bf16[5,4,4096]{2,1,0:T(4,128)(2,1)S(1)}, bf16[5,4,4096]{2,1,0:T(4,128)(2,1)S(1)}, u32[]{:S(2)}, u32[]{:S(2)}) collective-permute-start(bf16[5,4,4096]{2,1,0:T(4,128)(2,1)S(1)} %bitcast.95), channel_id=1, source_target_pairs={{0,8},{1,9},{2,10},{3,11},{4,12},{5,13},{6,14},{7,15},{8,16},{9,17... | collective-permute-start | bytes 491528 | tf_op jit(solution)/shard_map/ppermute | solution.py:29
  46.8 15.0 %collective-permute-start.3 = (bf16[5,4,4096]{2,1,0:T(4,128)(2,1)S(1)}, bf16[5,4,4096]{2,1,0:T(4,128)(2,1)S(1)}, u32[]{:S(2)}, u32[]{:S(2)}) collective-permute-start(bf16[5,4,4096]{2,1,0:T(4,128)(2,1)S(1)} %bitcast.94), channel_id=1, source_target_pairs={{0,1},{1,2},{2,3},{3,4},{4,5},{5,6},{6,7},{7,8},{8,9},{9,10},{10,1... | collective-permute-start | bytes 491528 | tf_op jit(solution)/shard_map/ppermute | solution.py:29
  51.6 30.3 %collective-permute-start.1 = (bf16[5,4,4096]{2,1,0:T(4,128)(2,1)S(1)}, bf16[5,4,4096]{2,1,0:T(4,128)(2,1)S(1)}, u32[]{:S(2)}, u32[]{:S(2)}) collective-permute-start(bf16[5,4,4096]{2,1,0:T(4,128)(2,1)S(1)} %bitcast.93), channel_id=1, source_target_pairs={{0,9},{1,10},{2,11},{3,12},{4,13},{5,14},{6,15},{7,16},{8,17},{9,1... | collective-permute-start | bytes 491528 | tf_op jit(solution)/shard_map/ppermute | solution.py:29
  59.5 47.8 %collective-permute-start = (bf16[5,4,4096]{2,1,0:T(4,128)(2,1)S(1)}, bf16[5,4,4096]{2,1,0:T(4,128)(2,1)S(1)}, u32[]{:S(2)}, u32[]{:S(2)}) collective-permute-start(bf16[5,4,4096]{2,1,0:T(4,128)(2,1)S(1)} %bitcast.92), channel_id=1, source_target_pairs={{0,16},{1,17},{2,18},{3,19},{4,20},{5,21},{6,22},{7,23},{8,24},{9,... | collective-permute-start | bytes 491528 | tf_op jit(solution)/shard_map/ppermute | solution.py:29
  107.3 64.1 %copy-start.1 = (bf16[1,4096,128]{2,1,0:T(8,128)(2,1)S(1)}, bf16[1,4096,128]{2,1,0:T(8,128)(2,1)}, u32[]{:S(2)}) copy-start(bf16[1,4096,128]{2,1,0:T(8,128)(2,1)} %param.11) | copy-start | bytes 3145732
  167.3 17.3 %slice-start = ((s8[8388608]{0:T(1024)(128)(4,1)}), s8[4194304]{0:T(1024)(128)(4,1)S(1)}, s32[]{:S(2)}) async-start(s8[8388608]{0:T(1024)(128)(4,1)} %bitcast.77), calls=%async_computation.6 | async-start | bytes 8388608
  171.4 13.1 %slice-start.1 = ((s8[8388608]{0:T(1024)(128)(4,1)}), s8[4194304]{0:T(1024)(128)(4,1)S(1)}, s32[]{:S(2)}) async-start(s8[8388608]{0:T(1024)(128)(4,1)} %bitcast.77), calls=%async_computation.7 | async-start | bytes 8388608
  186.6 30.8 %collective-permute-start.5 = (bf16[5,4,4096]{2,1,0:T(4,128)(2,1)S(1)}, bf16[5,4,4096]{2,1,0:T(4,128)(2,1)S(1)}, u32[]{:S(2)}, u32[]{:S(2)}) collective-permute-start(bf16[5,4,4096]{2,1,0:T(4,128)(2,1)S(1)} %squeeze.42), channel_id=1, source_target_pairs={{0,23},{1,24},{2,25},{3,26},{4,27},{5,28},{6,29},{7,30},{8,31},{9,... | collective-permute-start | bytes 491528 | tf_op jit(solution)/shard_map/ppermute | solution.py:29
  202.1 30.2 %collective-permute-start.6 = (bf16[5,4,4096]{2,1,0:T(4,128)(2,1)S(1)}, bf16[5,4,4096]{2,1,0:T(4,128)(2,1)S(1)}, u32[]{:S(2)}, u32[]{:S(2)}) collective-permute-start(bf16[5,4,4096]{2,1,0:T(4,128)(2,1)S(1)} %squeeze.43), channel_id=1, source_target_pairs={{0,24},{1,25},{2,26},{3,27},{4,28},{5,29},{6,30},{7,31},{8,0},{9,1... | collective-permute-start | bytes 491528 | tf_op jit(solution)/shard_map/ppermute | solution.py:29
  209.4 22.9 %collective-permute-start.7 = (bf16[5,4,4096]{2,1,0:T(4,128)(2,1)S(1)}, bf16[5,4,4096]{2,1,0:T(4,128)(2,1)S(1)}, u32[]{:S(2)}, u32[]{:S(2)}) collective-permute-start(bf16[5,4,4096]{2,1,0:T(4,128)(2,1)S(1)} %squeeze.44), channel_id=1, source_target_pairs={{0,31},{1,0},{2,1},{3,2},{4,3},{5,4},{6,5},{7,6},{8,7},{9,8},{10,9... | collective-permute-start | bytes 491528 | tf_op jit(solution)/shard_map/ppermute | solution.py:29
  214.0 38.6 %collective-permute-start.4 = (bf16[5,4,4096]{2,1,0:T(4,128)(2,1)S(1)}, bf16[5,4,4096]{2,1,0:T(4,128)(2,1)S(1)}, u32[]{:S(2)}, u32[]{:S(2)}) collective-permute-start(bf16[5,4,4096]{2,1,0:T(4,128)(2,1)S(1)} %squeeze.41), channel_id=1, source_target_pairs={{0,16},{1,17},{2,18},{3,19},{4,20},{5,21},{6,22},{7,23},{8,24},{9,... | collective-permute-start | bytes 491528 | tf_op jit(solution)/shard_map/ppermute | solution.py:29
Sparse Core Ops, SparseCore 0:
  10.1 73.2 all-gather.5
  109.1 58.1 all-gather.3

commit v2 on v1

--- a/solution.py
+++ b/solution.py
@@ -6,17 +6,20 @@
 
 CAPACITY = 5
 STEPS = 4
-FORWARD = ((16, 9, 8, 1), (15, 10, 7, 2), (14, 11, 6, 3), (13, 12, 5, 4))
-BACKWARD = ((15, 8, 7, 0), (14, 9, 6, 1), (13, 10, 5, 2), (12, 11, 4, 3))
+DISTANCES = ((9, 8, 1), (15, 10, 7, 2), (14, 11, 6, 3), (13, 12, 5, 4))
 
 
 def shift_table(n_blk, n_dp):
+    half = n_dp // 2
     rows = []
     for b in range(n_blk):
-        if b % 2 == 0:
-            rows.append([s for s in FORWARD[b // 2]])
-        else:
-            rows.append([(-s) % n_dp for s in BACKWARD[b // 2]])
+        sign = 1 if b % 2 == 0 else -1
+        steps = [(sign * s) % n_dp for s in DISTANCES[b // 2]]
+        if b == 0:
+            steps = [half] + steps
+        if b == 1:
+            steps = steps + [0]
+        rows.append(steps)
     return np.array(rows, np.int32)
 
 

time: 311 us -> 297 us (0.955)
  blocking collectives: 68.3 us -> 55.4 us
  waiting for transfers between devices: 140 us -> 129 us
  starting transfers between devices: 65.5 us -> 75.1 us
    all_to_all x1, blocking collectives: 34.4 us -> 21.2 us  [local(): lax.all_to_all(jnp.transpose(mixed, (1, 0, 2)), 'blk', split_axis=0, conc...]
    ppermute x8, starting transfers between devices: 65.5 us -> 75.1 us  [move(): return lax.ppermute(value, ('blk', 'dp'), pairs)]
    ppermute x8, waiting for transfers between devices: 80.8 us -> 74.9 us  [move(): return lax.ppermute(value, ('blk', 'dp'), pairs)]
    all_gather x1, waiting for transfers between devices: 58.3 us -> 53.3 us  [local(): everyone = lax.all_gather(mine, 'blk', axis=0, tiled=True)]
  transfers between devices with their start and end apart: 10 -> 10, of which waited for: 5 -> 7; matrix products, arithmetic and copies ran while one was open for 2% -> 3% of each run, Pallas kernels for 0% -> 0%
where the time goes in v2:
time: 297 us; the launch traced here: 294 us
  waiting for transfers between devices  129 us (43%)
  starting transfers between devices  75.1 us (25%)
  blocking collectives  55.4 us (19%)
  between operations  13.6 us (5%)
  matrix products  12.4 us (4%)
  local copies, waits for them, and re-layouts  4.72 us (2%)
  other arithmetic  3.47 us (1%)
    ppermute x8, starting transfers between devices, move(): return lax.ppermute(value, ('blk', 'dp'), pairs)  75.1 us
    ppermute x8, waiting for transfers between devices, move(): return lax.ppermute(value, ('blk', 'dp'), pairs)  74.9 us
    all_gather x1, waiting for transfers between devices, local(): everyone = lax.all_gather(mine, 'blk', axis=0, tiled=True)  53.3 us
    all_to_all x1, blocking collectives, local(): lax.all_to_all(jnp.transpose(mixed, (1, 0, 2)), 'blk', split_axis=0, conc...  21.2 us
    all_to_all x1, blocking collectives, local(): lax.all_to_all(outgoing, 'uly', split_axis=0, concat_axis=0, tiled=True)  13.8 us
    all_to_all x1, blocking collectives, local(): lax.all_to_all(back, 'uly', split_axis=0, concat_axis=0, tiled=True)  11.5 us
    all_to_all x1, blocking collectives, local(): lax.all_to_all(hidden, 'blk', split_axis=0, concat_axis=0, tiled=True)  8.96 us
  transfers between devices with their start and end apart: 10, of which 7 were waited for; matrix products, arithmetic and copies ran while one was open for 3% of the time, Pallas kernels for 0%

profile of v2, /device:TPU:25, one launch (start us, length us, event | category | flops | bytes accessed | tf_op | source)
XLA Modules:
  0.0 293.8 jit_solution(9942107456393570784)
XLA Ops:
  6.5 0.0 copy-start
  6.5 0.0 all-gather.6.cloned.1.call-start
  6.5 0.7 all-gather.6.cloned.1.call-update
  7.3 0.0 all-gather.4.cloned.1.call-start
  7.3 0.7 fusion.18
  8.0 0.1 broadcast_add_fusion
  8.1 0.1 add.51
  8.2 0.1 eq.47
  8.3 0.8 fusion.8
  9.1 0.1 fusion.11
  9.3 1.4 convolution_convert_fusion.1
  10.7 0.2 reshape.64
  10.9 13.8 %all_to_all.20 = bf16[4,5,4,4096]{3,2,1,0:T(4,128)(2,1)S(1)} all-to-all(bf16[4,5,4,4096]{3,2,1,0:T(4,128)(2,1)S(1)} %reshape.64), channel_id=1, replica_groups=mesh['blk'=8,'uly'=4,'dp'=32] {'uly'}, dimensions={0} | all-to-all | bytes 1310720 | tf_op jit(solution)/shard_map/all_to_all | solution.py:67
  24.8 1.4 fusion.23
  26.2 0.2 copy.84
  26.4 0.2 copy.83
  26.7 0.2 copy.85
  26.9 0.2 copy.82
  27.1 21.4 %collective-permute-start.2 = (bf16[5,4,4096]{2,1,0:T(4,128)(2,1)S(1)}, bf16[5,4,4096]{2,1,0:T(4,128)(2,1)S(1)}, u32[]{:S(2)}, u32[]{:S(2)}) collective-permute-start(bf16[5,4,4096]{2,1,0:T(4,128)(2,1)S(1)} %bitcast.95), channel_id=1, source_target_pairs={{0,8},{1,9},{2,10},{3,11},{4,12},{5,13},{6,14},{7,15},{8,16},{9,17... | collective-permute-start | bytes 491528 | tf_op jit(solution)/shard_map/ppermute | solution.py:32
  48.5 5.2 %collective-permute-start.3 = (bf16[5,4,4096]{2,1,0:T(4,128)(2,1)S(1)}, bf16[5,4,4096]{2,1,0:T(4,128)(2,1)S(1)}, u32[]{:S(2)}, u32[]{:S(2)}) collective-permute-start(bf16[5,4,4096]{2,1,0:T(4,128)(2,1)S(1)} %bitcast.94), channel_id=1, source_target_pairs={{0,1},{1,2},{2,3},{3,4},{4,5},{5,6},{6,7},{7,8},{8,9},{9,10},{10,1... | collective-permute-start | bytes 491528 | tf_op jit(solution)/shard_map/ppermute | solution.py:32
  53.7 6.2 %collective-permute-start.1 = (bf16[5,4,4096]{2,1,0:T(4,128)(2,1)S(1)}, bf16[5,4,4096]{2,1,0:T(4,128)(2,1)S(1)}, u32[]{:S(2)}, u32[]{:S(2)}) collective-permute-start(bf16[5,4,4096]{2,1,0:T(4,128)(2,1)S(1)} %bitcast.93), channel_id=1, source_target_pairs={{0,9},{1,10},{2,11},{3,12},{4,13},{5,14},{6,15},{7,16},{8,17},{9,1... | collective-permute-start | bytes 491528 | tf_op jit(solution)/shard_map/ppermute | solution.py:32
  59.9 11.8 %collective-permute-start = (bf16[5,4,4096]{2,1,0:T(4,128)(2,1)S(1)}, bf16[5,4,4096]{2,1,0:T(4,128)(2,1)S(1)}, u32[]{:S(2)}, u32[]{:S(2)}) collective-permute-start(bf16[5,4,4096]{2,1,0:T(4,128)(2,1)S(1)} %bitcast.92), channel_id=1, source_target_pairs={{0,16},{1,17},{2,18},{3,19},{4,20},{5,21},{6,22},{7,23},{8,24},{9,... | collective-permute-start | bytes 491528 | tf_op jit(solution)/shard_map/ppermute | solution.py:32
  71.8 0.0 collective-permute-done.2
  71.8 23.9 %collective-permute-done.3 = bf16[5,4,4096]{2,1,0:T(4,128)(2,1)S(1)} collective-permute-done((bf16[5,4,4096]{2,1,0:T(4,128)(2,1)S(1)}, bf16[5,4,4096]{2,1,0:T(4,128)(2,1)S(1)}, u32[]{:S(2)}, u32[]{:S(2)}) %collective-permute-start.3) | collective-permute-done | bytes 163872 | tf_op jit(solution)/shard_map/ppermute | solution.py:32
  95.7 4.4 %collective-permute-done.1 = bf16[5,4,4096]{2,1,0:T(4,128)(2,1)S(1)} collective-permute-done((bf16[5,4,4096]{2,1,0:T(4,128)(2,1)S(1)}, bf16[5,4,4096]{2,1,0:T(4,128)(2,1)S(1)}, u32[]{:S(2)}, u32[]{:S(2)}) %collective-permute-start.1) | collective-permute-done | bytes 163872 | tf_op jit(solution)/shard_map/ppermute | solution.py:32
  100.0 4.1 %collective-permute-done = bf16[5,4,4096]{2,1,0:T(4,128)(2,1)S(1)} collective-permute-done((bf16[5,4,4096]{2,1,0:T(4,128)(2,1)S(1)}, bf16[5,4,4096]{2,1,0:T(4,128)(2,1)S(1)}, u32[]{:S(2)}, u32[]{:S(2)}) %collective-permute-start) | collective-permute-done | bytes 163872 | tf_op jit(solution)/shard_map/ppermute | solution.py:32
  104.1 0.0 copy-start.1
  104.1 0.6 pad_maximum_fusion
  104.7 1.0 reshape.65
  105.7 0.0 all-gather.6.cloned.1.call-done
  105.7 0.0 all-gather.4.cloned.1.call-update
  105.7 53.3 %all-gather.4.cloned.1.call-done = bf16[640,4096]{1,0:T(8,128)(2,1)} async-done(((bf16[80,4096]{1,0:T(8,128)(2,1)}), bf16[640,4096]{1,0:T(8,128)(2,1)}) %all-gather.4.cloned.1.call-update) | async-done | bytes 5242896 | tf_op jit(solution)/shard_map/all_gather | solution.py:74
  159.0 0.0 copy-done
  159.0 0.0 slice-start
  159.0 4.1 %fusion.3 = f32[640,128]{1,0:T(8,128)S(1)} fusion(bf16[640,4096]{1,0:T(8,128)(2,1)} %all-gather.4.cloned.1.call-done, bf16[1,4096,128]{2,1,0:T(8,128)(2,1)S(1)} %copy-done), kind=kOutput, calls=%fused_computation.7 | convolution fusion | flops 671088640 | bytes 6619136 | tf_op jit(solution)/shard_map/dot_general | solution.py:75
  163.2 0.0 copy-done.1
  163.2 0.0 slice-start.1
  163.2 4.2 %fusion.1 = bf16[640,128]{1,0:T(8,128)(2,1)S(1)} fusion(bf16[640,4096]{1,0:T(8,128)(2,1)} %all-gather.4.cloned.1.call-done, bf16[1,4096,128]{2,1,0:T(8,128)(2,1)S(1)} %copy-done.1, f32[640,128]{1,0:T(8,128)S(1)} %fusion.3), kind=kOutput, calls=%fused_computation.5 | convolution fusion | flops 671580160 | bytes 6782976 | tf_op jit(solution)/shard_map/dot_general | solution.py:76
  167.4 9.0 %all_to_all.21 = bf16[8,80,128]{2,1,0:T(8,128)(2,1)S(1)} all-to-all(bf16[8,80,128]{2,1,0:T(8,128)(2,1)S(1)} %bitcast.91), channel_id=1, replica_groups=mesh['blk'=8,'uly'=4,'dp'=32] {'blk'}, dimensions={0} | all-to-all | bytes 327680 | tf_op jit(solution)/shard_map/all_to_all | solution.py:79
  176.3 0.0 slice-done
  176.3 0.0 slice-done.1
  176.3 1.6 convolution_convert_fusion
  177.9 0.1 fusion.22
  178.0 0.1 squeeze.41
  178.1 0.1 squeeze.44
  178.2 0.1 squeeze.43
  178.2 0.1 squeeze.42
  178.3 17.7 %collective-permute-start.5 = (bf16[5,4,4096]{2,1,0:T(4,128)(2,1)S(1)}, bf16[5,4,4096]{2,1,0:T(4,128)(2,1)S(1)}, u32[]{:S(2)}, u32[]{:S(2)}) collective-permute-start(bf16[5,4,4096]{2,1,0:T(4,128)(2,1)S(1)} %squeeze.42), channel_id=1, source_target_pairs={{0,23},{1,24},{2,25},{3,26},{4,27},{5,28},{6,29},{7,30},{8,31},{9,... | collective-permute-start | bytes 491528 | tf_op jit(solution)/shard_map/ppermute | solution.py:32
  196.0 7.5 %collective-permute-start.6 = (bf16[5,4,4096]{2,1,0:T(4,128)(2,1)S(1)}, bf16[5,4,4096]{2,1,0:T(4,128)(2,1)S(1)}, u32[]{:S(2)}, u32[]{:S(2)}) collective-permute-start(bf16[5,4,4096]{2,1,0:T(4,128)(2,1)S(1)} %squeeze.43), channel_id=1, source_target_pairs={{0,24},{1,25},{2,26},{3,27},{4,28},{5,29},{6,30},{7,31},{8,0},{9,1... | collective-permute-start | bytes 491528 | tf_op jit(solution)/shard_map/ppermute | solution.py:32
  203.5 2.6 collective-permute-start.7
  206.1 2.8 collective-permute-start.4
  208.8 0.0 collective-permute-done.5
  208.8 20.8 %collective-permute-done.6 = bf16[5,4,4096]{2,1,0:T(4,128)(2,1)S(1)} collective-permute-done((bf16[5,4,4096]{2,1,0:T(4,128)(2,1)S(1)}, bf16[5,4,4096]{2,1,0:T(4,128)(2,1)S(1)}, u32[]{:S(2)}, u32[]{:S(2)}) %collective-permute-start.6) | collective-permute-done | bytes 163872 | tf_op jit(solution)/shard_map/ppermute | solution.py:32
  229.6 2.8 collective-permute-done.7
  232.4 19.0 %collective-permute-done.4 = bf16[5,4,4096]{2,1,0:T(4,128)(2,1)S(1)} collective-permute-done((bf16[5,4,4096]{2,1,0:T(4,128)(2,1)S(1)}, bf16[5,4,4096]{2,1,0:T(4,128)(2,1)S(1)}, u32[]{:S(2)}, u32[]{:S(2)}) %collective-permute-start.4) | collective-permute-done | bytes 163872 | tf_op jit(solution)/shard_map/ppermute | solution.py:32
  251.4 0.6 maximum_bitcast_fusion
  252.0 0.5 copy.64
  252.5 11.5 %all_to_all.22 = bf16[4,5,4,4096]{3,2,1,0:T(4,128)(2,1)S(1)} all-to-all(bf16[4,5,4,4096]{3,2,1,0:T(4,128)(2,1)S(1)} %copy.64), channel_id=1, replica_groups=mesh['blk'=8,'uly'=4,'dp'=32] {'uly'}, dimensions={0} | all-to-all | bytes 1310720 | tf_op jit(solution)/shard_map/all_to_all | solution.py:85
  264.0 1.1 fusion
  265.1 21.2 %all_to_all.23 = bf16[8,64,512]{2,1,0:T(8,128)(2,1)S(1)} all-to-all(bf16[8,64,512]{2,1,0:T(8,128)(2,1)S(1)} %bitcast.80), channel_id=1, replica_groups=mesh['blk'=8,'uly'=4,'dp'=32] {'blk'}, dimensions={0} | all-to-all | bytes 1048576 | tf_op jit(solution)/shard_map/all_to_all | solution.py:88
  286.2 0.7 reduce_sum.32
  (6 shorter events, 0.1 us)
Async XLA Ops:
  6.5 152.5 %copy-start = (bf16[1,4096,128]{2,1,0:T(8,128)(2,1)S(1)}, bf16[1,4096,128]{2,1,0:T(8,128)(2,1)}, u32[]{:S(2)}) copy-start(bf16[1,4096,128]{2,1,0:T(8,128)(2,1)} %param.10) | copy-start | bytes 3145732
  6.5 99.1 %all-gather.6.cloned.1.call-start = ((), (), s32[]{:S(2)}) async-start(), calls=%async_computation.5 | async-start | bytes 9437184 | tf_op jit(solution)/shard_map/all_gather | solution.py:45
  7.3 151.8 %all-gather.4.cloned.1.call-start = ((), (), s32[]{:S(2)}) async-start(), calls=%async_computation.4 | async-start | bytes 5898240 | tf_op jit(solution)/shard_map/all_gather | solution.py:74
  27.1 44.7 %collective-permute-start.2 = (bf16[5,4,4096]{2,1,0:T(4,128)(2,1)S(1)}, bf16[5,4,4096]{2,1,0:T(4,128)(2,1)S(1)}, u32[]{:S(2)}, u32[]{:S(2)}) collective-permute-start(bf16[5,4,4096]{2,1,0:T(4,128)(2,1)S(1)} %bitcast.95), channel_id=1, source_target_pairs={{0,8},{1,9},{2,10},{3,11},{4,12},{5,13},{6,14},{7,15},{8,16},{9,17... | collective-permute-start | bytes 491528 | tf_op jit(solution)/shard_map/ppermute | solution.py:32
  48.5 47.2 %collective-permute-start.3 = (bf16[5,4,4096]{2,1,0:T(4,128)(2,1)S(1)}, bf16[5,4,4096]{2,1,0:T(4,128)(2,1)S(1)}, u32[]{:S(2)}, u32[]{:S(2)}) collective-permute-start(bf16[5,4,4096]{2,1,0:T(4,128)(2,1)S(1)} %bitcast.94), channel_id=1, source_target_pairs={{0,1},{1,2},{2,3},{3,4},{4,5},{5,6},{6,7},{7,8},{8,9},{9,10},{10,1... | collective-permute-start | bytes 491528 | tf_op jit(solution)/shard_map/ppermute | solution.py:32
  53.7 46.3 %collective-permute-start.1 = (bf16[5,4,4096]{2,1,0:T(4,128)(2,1)S(1)}, bf16[5,4,4096]{2,1,0:T(4,128)(2,1)S(1)}, u32[]{:S(2)}, u32[]{:S(2)}) collective-permute-start(bf16[5,4,4096]{2,1,0:T(4,128)(2,1)S(1)} %bitcast.93), channel_id=1, source_target_pairs={{0,9},{1,10},{2,11},{3,12},{4,13},{5,14},{6,15},{7,16},{8,17},{9,1... | collective-permute-start | bytes 491528 | tf_op jit(solution)/shard_map/ppermute | solution.py:32
  59.9 44.2 %collective-permute-start = (bf16[5,4,4096]{2,1,0:T(4,128)(2,1)S(1)}, bf16[5,4,4096]{2,1,0:T(4,128)(2,1)S(1)}, u32[]{:S(2)}, u32[]{:S(2)}) collective-permute-start(bf16[5,4,4096]{2,1,0:T(4,128)(2,1)S(1)} %bitcast.92), channel_id=1, source_target_pairs={{0,16},{1,17},{2,18},{3,19},{4,20},{5,21},{6,22},{7,23},{8,24},{9,... | collective-permute-start | bytes 491528 | tf_op jit(solution)/shard_map/ppermute | solution.py:32
  104.1 59.1 %copy-start.1 = (bf16[1,4096,128]{2,1,0:T(8,128)(2,1)S(1)}, bf16[1,4096,128]{2,1,0:T(8,128)(2,1)}, u32[]{:S(2)}) copy-start(bf16[1,4096,128]{2,1,0:T(8,128)(2,1)} %param.11) | copy-start | bytes 3145732
  159.0 17.3 %slice-start = ((s8[8388608]{0:T(1024)(128)(4,1)}), s8[4194304]{0:T(1024)(128)(4,1)S(1)}, s32[]{:S(2)}) async-start(s8[8388608]{0:T(1024)(128)(4,1)} %bitcast.77), calls=%async_computation.6 | async-start | bytes 8388608
  163.2 13.1 %slice-start.1 = ((s8[8388608]{0:T(1024)(128)(4,1)}), s8[4194304]{0:T(1024)(128)(4,1)S(1)}, s32[]{:S(2)}) async-start(s8[8388608]{0:T(1024)(128)(4,1)} %bitcast.77), calls=%async_computation.7 | async-start | bytes 8388608
  178.3 30.5 %collective-permute-start.5 = (bf16[5,4,4096]{2,1,0:T(4,128)(2,1)S(1)}, bf16[5,4,4096]{2,1,0:T(4,128)(2,1)S(1)}, u32[]{:S(2)}, u32[]{:S(2)}) collective-permute-start(bf16[5,4,4096]{2,1,0:T(4,128)(2,1)S(1)} %squeeze.42), channel_id=1, source_target_pairs={{0,23},{1,24},{2,25},{3,26},{4,27},{5,28},{6,29},{7,30},{8,31},{9,... | collective-permute-start | bytes 491528 | tf_op jit(solution)/shard_map/ppermute | solution.py:32
  196.0 33.5 %collective-permute-start.6 = (bf16[5,4,4096]{2,1,0:T(4,128)(2,1)S(1)}, bf16[5,4,4096]{2,1,0:T(4,128)(2,1)S(1)}, u32[]{:S(2)}, u32[]{:S(2)}) collective-permute-start(bf16[5,4,4096]{2,1,0:T(4,128)(2,1)S(1)} %squeeze.43), channel_id=1, source_target_pairs={{0,24},{1,25},{2,26},{3,27},{4,28},{5,29},{6,30},{7,31},{8,0},{9,1... | collective-permute-start | bytes 491528 | tf_op jit(solution)/shard_map/ppermute | solution.py:32
  203.5 28.9 %collective-permute-start.7 = (bf16[5,4,4096]{2,1,0:T(4,128)(2,1)S(1)}, bf16[5,4,4096]{2,1,0:T(4,128)(2,1)S(1)}, u32[]{:S(2)}, u32[]{:S(2)}) collective-permute-start(bf16[5,4,4096]{2,1,0:T(4,128)(2,1)S(1)} %squeeze.44), channel_id=1, source_target_pairs={{0,31},{1,0},{2,1},{3,2},{4,3},{5,4},{6,5},{7,6},{8,7},{9,8},{10,9... | collective-permute-start | bytes 491528 | tf_op jit(solution)/shard_map/ppermute | solution.py:32
  206.1 45.3 %collective-permute-start.4 = (bf16[5,4,4096]{2,1,0:T(4,128)(2,1)S(1)}, bf16[5,4,4096]{2,1,0:T(4,128)(2,1)S(1)}, u32[]{:S(2)}, u32[]{:S(2)}) collective-permute-start(bf16[5,4,4096]{2,1,0:T(4,128)(2,1)S(1)} %squeeze.41), channel_id=1, source_target_pairs={{0,16},{1,17},{2,18},{3,19},{4,20},{5,21},{6,22},{7,23},{8,24},{9,... | collective-permute-start | bytes 491528 | tf_op jit(solution)/shard_map/ppermute | solution.py:32
Sparse Core Ops, SparseCore 0:
  10.1 73.2 all-gather.5
  105.8 53.1 all-gather.3

commit v3 on v2

v3 whole, which is shorter than its diff:
```python
import jax
import jax.numpy as jnp
import numpy as np
from jax import lax
from jax.sharding import PartitionSpec as P

CAPACITY = 5
DISTANCES = ((9, 8, 1), (15, 10, 7, 2), (14, 11, 6, 3), (13, 12, 5, 4))
CHUNKS = ((0, 3), (1, 2))
NEAR = (0, -1, 1, 2)


def shift_table(n_blk, n_dp):
    half = n_dp // 2
    rows = []
    for b in range(n_blk):
        sign = 1 if b % 2 == 0 else -1
        steps = [(sign * s) % n_dp for s in DISTANCES[b // 2]]
        if b == 0:
            steps = [half] + steps
        if b == 1:
            steps = steps + [0]
        rows.append(steps)
    return np.array(rows, np.int32)


def move(value, shifts, step, sign, n_blk, n_dp):
    pairs = []
    for b in range(n_blk):
        s = sign * int(shifts[b, step])
        for z in range(n_dp):
            pairs.append((b * n_dp + z, b * n_dp + (z + s) % n_dp))
    return lax.ppermute(value, ("blk", "dp"), pairs)


def chip_move(value, step, n_blk):
    chips = n_blk // 2
    return lax.ppermute(value, "blk", [(b, (b // 2 + step) % chips * 2 + b % 2) for b in range(n_blk)])


def core_swap(value, n_blk):
    return lax.ppermute(value, "blk", [(b, b ^ 1) for b in range(n_blk)])


def chip_gather(value, n_blk):
    half = value.shape[0] // 2
    below = chip_move(value, 1, n_blk)
    above = chip_move(value, -1, n_blk)
    far_low = chip_move(below[:half], 1, n_blk)
    far_high = chip_move(above[half:], -1, n_blk)
    own = jnp.concatenate([value, below, above, far_low, far_high], axis=0)
    return own, core_swap(own, n_blk)


def block(tokens, expert_ids, route_weight, w_gate, w_up, w_down):
    n_uly = lax.axis_size("uly")
    n_dp = lax.axis_size("dp")
    n_blk = lax.axis_size("blk")
    tokens_here, width = tokens.shape
    part = width // n_blk
    shifts = shift_table(n_blk, n_dp)
    b = lax.axis_index("blk")
    z = lax.axis_index("dp")

    down_own, down_other = chip_gather(w_down[0], n_blk)

    row_i = lax.broadcasted_iota(jnp.int32, (tokens_here, tokens_here), 0)
    col_i = lax.broadcasted_iota(jnp.int32, (tokens_here, tokens_here), 1)
    earlier = (col_i < row_i).astype(jnp.float32)
    places = jnp.arange(CAPACITY, dtype=jnp.float32)
    own_shifts = lax.dynamic_slice_in_dim(jnp.asarray(shifts), b, 1, 0)[0]
    order = [own_shifts[j] for steps in CHUNKS for j in steps]
    z_of = (z + jnp.stack(order)) % n_dp
    per = len(CHUNKS[0])
    rows = n_uly * CAPACITY * per
    x_of = jnp.arange(n_uly, dtype=jnp.int32) * n_dp
    experts = (x_of[None, :, None] + z_of.reshape(len(CHUNKS), 1, per)).reshape(-1)
    hit = expert_ids[:, :, None] == experts[None, None, :]
    chosen = jnp.sum(hit.astype(jnp.float32), axis=1)
    weight = jnp.sum(jnp.where(hit, route_weight[:, :, None], 0.0), axis=1)
    before = jnp.dot(earlier, chosen, preferred_element_type=jnp.float32)
    shape = (tokens_here, len(CHUNKS), n_uly, 1, per)
    at = (before.reshape(shape) == places[None, None, None, :, None]).astype(jnp.float32)
    placing = (at * chosen.reshape(shape)).astype(jnp.bfloat16).reshape(tokens_here, len(CHUNKS), rows)
    mixing = (at * weight.reshape(shape)).reshape(tokens_here, len(CHUNKS), rows)

    index_own = (b // 2 + jnp.array(NEAR, jnp.int32)) % (n_blk // 2) * 2 + b % 2
    index_other = index_own + 1 - 2 * (b % 2)

    outgoing = [
        lax.dot_general(placing[:, n], tokens, (((0,), (0,)), ((), ())), preferred_element_type=jnp.float32)
        .astype(jnp.bfloat16)
        .reshape(n_uly, CAPACITY, per, width)
        for n in range(len(CHUNKS))
    ]
    crossed = lax.all_to_all(jnp.stack(outgoing, axis=1), "uly", split_axis=0, concat_axis=0, tiled=True)
    gathered = []
    for n, steps in enumerate(CHUNKS):
        arrived = []
        for i, j in enumerate(steps):
            chunk = jnp.transpose(crossed[:, n, :, i, :], (1, 0, 2))
            arrived.append(move(chunk, shifts, j, 1, n_blk, n_dp))
        mine = jnp.stack(arrived).reshape(rows, n_blk, part)
        mine = jnp.transpose(mine, (1, 0, 2)).reshape(rows * n_blk, part)
        gathered.append(lax.all_gather(mine, "blk", axis=1, tiled=True))

    home = []
    answers = []
    for n, steps in enumerate(CHUNKS):
        everyone = gathered[n]
        if answers:
            everyone, _ = lax.optimization_barrier((everyone, answers[-1]))
        everyone = everyone.reshape(n_blk, rows, n_blk, part)
        everyone = jnp.transpose(everyone, (2, 1, 0, 3)).reshape(n_blk * rows, width)
        gate = jnp.dot(everyone, w_gate[0], preferred_element_type=jnp.float32)
        up = jnp.dot(everyone, w_up[0], preferred_element_type=jnp.float32)
        hidden = (jax.nn.silu(gate) * up).astype(jnp.bfloat16)
        units = hidden.shape[1]
        hidden = hidden.reshape(n_blk, rows, units)
        hidden = lax.all_to_all(hidden, "blk", split_axis=0, concat_axis=0, tiled=True)

        def pick(index):
            pieces = [lax.dynamic_index_in_dim(hidden, index[i], 0, keepdims=False) for i in range(len(NEAR))]
            return jnp.concatenate(pieces, axis=1)

        answer = jnp.dot(pick(index_own), down_own, preferred_element_type=jnp.float32)
        answer = answer + jnp.dot(pick(index_other), down_other, preferred_element_type=jnp.float32)
        answers.append(answer.astype(jnp.bfloat16).reshape(per, CAPACITY, n_uly, width))
    for n, steps in enumerate(CHUNKS):
        leaving = [answers[n][i] for i in range(per)]
        back = [move(leaving[i], shifts, j, -1, n_blk, n_dp) for i, j in enumerate(steps)]
        back = jnp.transpose(jnp.stack(back), (2, 1, 0, 3))
        home.append(lax.all_to_all(back, "uly", split_axis=0, concat_axis=0, tiled=True).reshape(rows, width))

    mixed = 0.0
    for n in range(len(CHUNKS)):
        mixed = mixed + jnp.dot(mixing[:, n], home[n].astype(jnp.float32), precision=lax.Precision.HIGHEST)
    mixed = mixed.astype(jnp.bfloat16).reshape(tokens_here, n_blk, part)
    mixed = lax.all_to_all(jnp.transpose(mixed, (1, 0, 2)), "blk", split_axis=0, concat_axis=0, tiled=True)
    return jnp.sum(mixed.astype(jnp.float32), axis=0).astype(jnp.bfloat16)


def solution(mesh):
    return jax.shard_map(
        block,
        mesh=mesh,
        in_specs=(
            P(("uly", "dp"), None),
            P(("uly", "dp"), None),
            P(("uly", "dp"), None),
            P(("uly", "dp"), None, "blk"),
            P(("uly", "dp"), None, "blk"),
            P(("uly", "dp"), "blk", None),
        ),
        out_specs=P(("uly", "dp"), "blk"),
        check_vma=False,
    )
```

time: 297 us -> 334 us (1.12)
  starting transfers between devices: 75.1 us -> 110 us
  local copies, waits for them, and re-layouts: 4.72 us -> 31.3 us
  waiting for transfers between devices: 129 us -> 105 us
  blocking collectives: 55.4 us -> 31.7 us
  between operations: 13.6 us -> 29.5 us
  matrix products: 12.4 us -> 16.5 us
    all_gather x2, waiting for transfers between devices: 53.3 us -> 0.02 us  [block(): gathered.append(lax.all_gather(mine, 'blk', axis=1, tiled=True))]
    all_to_all x4 -> x2, blocking collectives: 55.4 us -> 31.7 us  [the longest x1 17.8 us: block(): lax.all_to_all(jnp.transpose(mixed, (1, 0, 2)), 'blk', split_axis=0, conc...]
    all_to_all x0 -> x4, starting transfers between devices: none -> 18.3 us  [the longest x2 11.4 us: block(): lax.all_to_all(hidden, 'blk', split_axis=0, concat_axis=0, tiled=True)]
    ppermute x0 -> x5, starting transfers between devices: none -> 16.7 us  [the longest x4 13 us: chip_move(): lax.ppermute(value, 'blk', [(b, (b // 2 + step) % chips * 2 + b % 2) for...]
    unnamed x11 -> x18, local copies, waits for them, and re-layouts: 0.67 us -> 15.2 us
    ppermute x8, waiting for transfers between devices: 74.9 us -> 87.8 us  [move(): return lax.ppermute(value, ('blk', 'dp'), pairs)]
    ppermute x0 -> x5, waiting for transfers between devices: none -> 8.43 us  [the longest x4 8.43 us: chip_move(): lax.ppermute(value, 'blk', [(b, (b // 2 + step) % chips * 2 + b % 2) for...]
    all_to_all x0 -> x4, waiting for transfers between devices: none -> 8.31 us  [the longest x2 5.09 us: block(): lax.all_to_all(back, 'uly', split_axis=0, concat_axis=0, tiled=True)]
  transfers between devices with their start and end apart: 10 -> 19, of which waited for: 7 -> 8; matrix products, arithmetic and copies ran while one was open for 3% -> 11% of each run, Pallas kernels for 0% -> 0%
where the time goes in v3:
time: 334 us; the launch traced here: 330 us
  starting transfers between devices  110 us (33%)
  waiting for transfers between devices  105 us (31%)
  blocking collectives  31.7 us (9%)
  local copies, waits for them, and re-layouts  31.3 us (9%)
  between operations  29.5 us (9%)
  matrix products  16.5 us (5%)
  other arithmetic  6.69 us (2%)
    ppermute x8, waiting for transfers between devices, move(): return lax.ppermute(value, ('blk', 'dp'), pairs)  87.8 us
    ppermute x8, starting transfers between devices, move(): return lax.ppermute(value, ('blk', 'dp'), pairs)  75.1 us
    all_to_all x1, blocking collectives, block(): lax.all_to_all(jnp.transpose(mixed, (1, 0, 2)), 'blk', split_axis=0, conc...  17.8 us
    unnamed x18, local copies, waits for them, and re-layouts  15.2 us
    all_to_all x1, blocking collectives, block(): lax.all_to_all(jnp.stack(outgoing, axis=1), 'uly', split_axis=0, concat_a...  13.8 us
    ppermute x4, starting transfers between devices, chip_move(): lax.ppermute(value, 'blk', [(b, (b // 2 + step) % chips * 2 + b % 2) for...  13 us
    all_to_all x2, starting transfers between devices, block(): lax.all_to_all(hidden, 'blk', split_axis=0, concat_axis=0, tiled=True)  11.4 us
    ppermute x4, waiting for transfers between devices, chip_move(): lax.ppermute(value, 'blk', [(b, (b // 2 + step) % chips * 2 + b % 2) for...  8.43 us
  transfers between devices with their start and end apart: 19, of which 8 were waited for; matrix products, arithmetic and copies ran while one was open for 11% of the time, Pallas kernels for 0%

profile of v3, /device:TPU:25, one launch (start us, length us, event | category | flops | bytes accessed | tf_op | source)
XLA Modules:
  0.0 330.3 jit_solution(4950296457197222504)
XLA Ops:
  6.5 0.8 constant_dynamic-slice_fusion
  7.3 0.7 fusion.61
  8.0 3.2 add_subtract_fusion
  11.4 0.8 fusion.12
  12.6 1.3 convolution_convert_fusion
  13.9 1.3 convolution_convert_fusion.1
  15.6 0.9 pad_maximum_fusion
  16.6 13.8 %all_to_all.30 = bf16[4,2,5,2,4096]{4,3,2,1,0:T(2,128)(2,1)S(1)} all-to-all(bf16[4,2,5,2,4096]{4,3,2,1,0:T(2,128)(2,1)S(1)} %pad_maximum_fusion), channel_id=1, replica_groups=mesh['blk'=8,'uly'=4,'dp'=32] {'uly'}, dimensions={0} | all-to-all | bytes 1310720 | tf_op jit(solution)/shard_map/all_to_all | solution.py:96
  30.4 1.6 fusion.56
  32.5 19.7 %collective-permute-start.1 = (bf16[5,4,4096]{2,1,0:T(4,128)(2,1)S(1)}, bf16[5,4,4096]{2,1,0:T(4,128)(2,1)S(1)}, u32[]{:S(2)}, u32[]{:S(2)}) collective-permute-start(bf16[5,4,4096]{2,1,0:T(4,128)(2,1)S(1)} %bitcast.186), channel_id=1, source_target_pairs={{0,1},{1,2},{2,3},{3,4},{4,5},{5,6},{6,7},{7,8},{8,9},{9,10},{10,1... | collective-permute-start | bytes 491528 | tf_op jit(solution)/shard_map/ppermute | solution.py:33
  52.2 10.7 %collective-permute-start = (bf16[5,4,4096]{2,1,0:T(4,128)(2,1)S(1)}, bf16[5,4,4096]{2,1,0:T(4,128)(2,1)S(1)}, u32[]{:S(2)}, u32[]{:S(2)}) collective-permute-start(bf16[5,4,4096]{2,1,0:T(4,128)(2,1)S(1)} %bitcast.184), channel_id=1, source_target_pairs={{0,16},{1,17},{2,18},{3,19},{4,20},{5,21},{6,22},{7,23},{8,24},{9,... | collective-permute-start | bytes 491528 | tf_op jit(solution)/shard_map/ppermute | solution.py:33
  62.9 22.0 %collective-permute-done = bf16[5,4,4096]{2,1,0:T(4,128)(2,1)S(1)} collective-permute-done((bf16[5,4,4096]{2,1,0:T(4,128)(2,1)S(1)}, bf16[5,4,4096]{2,1,0:T(4,128)(2,1)S(1)}, u32[]{:S(2)}, u32[]{:S(2)}) %collective-permute-start) | collective-permute-done | bytes 163872 | tf_op jit(solution)/shard_map/ppermute | solution.py:33
  85.4 0.8 copy.82
  86.3 1.9 collective-permute-start.3
  88.2 4.6 %collective-permute-start.2 = (bf16[128,4096]{1,0:T(8,128)(2,1)}, bf16[128,4096]{1,0:T(8,128)(2,1)S(1)}, u32[]{:S(2)}, u32[]{:S(2)}) collective-permute-start(bf16[128,4096]{1,0:T(8,128)(2,1)} %bitcast.38), channel_id=1, source_target_pairs={{0,256},{128,384},{256,512},{384,640},{512,768},{640,896},{768,0},... | collective-permute-start | bytes 3145736 | tf_op jit(solution)/shard_map/ppermute | solution.py:38
  92.8 1.2 copy.107
  94.2 14.5 %collective-permute-start.10 = (bf16[5,4,4096]{2,1,0:T(4,128)(2,1)S(1)}, bf16[5,4,4096]{2,1,0:T(4,128)(2,1)S(1)}, u32[]{:S(2)}, u32[]{:S(2)}) collective-permute-start(bf16[5,4,4096]{2,1,0:T(4,128)(2,1)S(1)} %bitcast.185), channel_id=1, source_target_pairs={{0,8},{1,9},{2,10},{3,11},{4,12},{5,13},{6,14},{7,15},{8,16},{9,17... | collective-permute-start | bytes 491528 | tf_op jit(solution)/shard_map/ppermute | solution.py:33
  108.7 2.0 collective-permute-start.9
  110.7 2.3 constant_dynamic-update-slice_fusion.4
  113.0 19.7 %collective-permute-done.10 = bf16[5,4,4096]{2,1,0:T(4,128)(2,1)S(1)} collective-permute-done((bf16[5,4,4096]{2,1,0:T(4,128)(2,1)S(1)}, bf16[5,4,4096]{2,1,0:T(4,128)(2,1)S(1)}, u32[]{:S(2)}, u32[]{:S(2)}) %collective-permute-start.10) | collective-permute-done | bytes 163872 | tf_op jit(solution)/shard_map/ppermute | solution.py:33
  132.7 11.1 %collective-permute-done.9 = bf16[5,4,4096]{2,1,0:T(4,128)(2,1)S(1)} collective-permute-done((bf16[5,4,4096]{2,1,0:T(4,128)(2,1)S(1)}, bf16[5,4,4096]{2,1,0:T(4,128)(2,1)S(1)}, u32[]{:S(2)}, u32[]{:S(2)}) %collective-permute-start.9) | collective-permute-done | bytes 163872 | tf_op jit(solution)/shard_map/ppermute | solution.py:33
  144.1 1.0 reshape.119
  145.1 1.8 copy.87
  146.9 1.9 collective-permute-start.5
  148.9 4.6 %collective-permute-start.4 = (bf16[64,4096]{1,0:T(8,128)(2,1)S(1)}, bf16[64,4096]{1,0:T(8,128)(2,1)S(1)}, u32[]{:S(2)}, u32[]{:S(2)}) collective-permute-start(bf16[64,4096]{1,0:T(8,128)(2,1)S(1)} %slice.137), channel_id=1, source_target_pairs={{0,256},{128,384},{256,512},{384,640},{512,768},{640,896},{768,0},... | collective-permute-start | bytes 1572872 | tf_op jit(solution)/shard_map/ppermute | solution.py:38
  153.5 1.1 constant_dynamic-update-slice_fusion.3
  154.6 1.0 constant_dynamic-update-slice_fusion.2
  155.6 8.4 %collective-permute-done.4 = bf16[64,4096]{1,0:T(8,128)(2,1)S(1)} collective-permute-done((bf16[64,4096]{1,0:T(8,128)(2,1)S(1)}, bf16[64,4096]{1,0:T(8,128)(2,1)S(1)}, u32[]{:S(2)}, u32[]{:S(2)}) %collective-permute-start.4) | collective-permute-done | bytes 524320 | tf_op jit(solution)/shard_map/ppermute | solution.py:38
  164.0 0.9 constant_dynamic-update-slice_fusion.1
  164.9 0.9 constant_dynamic-update-slice_fusion
  165.7 3.7 %collective-permute-start.6 = (bf16[512,4096]{1,0:T(8,128)(2,1)}, bf16[512,4096]{1,0:T(8,128)(2,1)}, u32[]{:S(2)}, u32[]{:S(2)}) collective-permute-start(bf16[512,4096]{1,0:T(8,128)(2,1)} %constant_dynamic-update-slice_fusion), channel_id=1, source_target_pairs={{0,128},{128,0},{256,384},{384,256},{512,640},{640,512},{768,896},... | collective-permute-start | bytes 12582920 | tf_op jit(solution)/shard_map/ppermute | solution.py:42
  169.4 0.7 fusion.60
  175.5 0.7 fusion.59
  186.5 2.9 copy.97
  189.4 1.5 copy.83
  190.8 1.2 copy.98
  192.1 0.9 fusion.9
  193.0 1.5 fusion.3
  194.4 6.6 %all-to-all-start.1 = ((bf16[8,40,128]{2,1,0:T(8,128)(2,1)}), bf16[8,40,128]{2,1,0:T(8,128)(2,1)S(1)}, u32[]{:S(2)}, u32[]{:S(2)}) async-start(bf16[8,40,128]{2,1,0:T(8,128)(2,1)} %bitcast.29), calls=%async_computation.1 | async-start | bytes 163840 | tf_op jit(solution)/shard_map/all_to_all | solution.py:120
  201.1 2.9 copy.99
  204.0 1.5 copy.88
  205.4 1.2 copy.100
  206.6 0.9 fusion.7
  207.5 1.5 fusion.4
  209.0 4.8 %all-to-all-start.3 = ((bf16[8,40,128]{2,1,0:T(8,128)(2,1)}), bf16[8,40,128]{2,1,0:T(8,128)(2,1)S(1)}, u32[]{:S(2)}, u32[]{:S(2)}) async-start(bf16[8,40,128]{2,1,0:T(8,128)(2,1)} %bitcast.60), calls=%async_computation.3 | async-start | bytes 163840 | tf_op jit(solution)/shard_map/all_to_all | solution.py:120
  213.8 3.2 all-to-all-done.3
  217.1 3.2 fusion.20
  220.5 0.8 fusion.1
  221.6 2.2 collective-permute-start.8
  223.7 12.8 %collective-permute-start.7 = (bf16[5,4,4096]{2,1,0:T(4,128)(2,1)S(1)}, bf16[5,4,4096]{2,1,0:T(4,128)(2,1)S(1)}, u32[]{:S(2)}, u32[]{:S(2)}) collective-permute-start(bf16[5,4,4096]{2,1,0:T(4,128)(2,1)S(1)} %squeeze.153), channel_id=1, source_target_pairs={{0,16},{1,17},{2,18},{3,19},{4,20},{5,21},{6,22},{7,23},{8,24},{9,... | collective-permute-start | bytes 491528 | tf_op jit(solution)/shard_map/ppermute | solution.py:33
  236.6 3.0 fusion.35
  239.6 0.8 fusion.2
  240.7 4.0 %collective-permute-start.12 = (bf16[5,4,4096]{2,1,0:T(4,128)(2,1)S(1)}, bf16[5,4,4096]{2,1,0:T(4,128)(2,1)S(1)}, u32[]{:S(2)}, u32[]{:S(2)}) collective-permute-start(bf16[5,4,4096]{2,1,0:T(4,128)(2,1)S(1)} %squeeze.167), channel_id=1, source_target_pairs={{0,24},{1,25},{2,26},{3,27},{4,28},{5,29},{6,30},{7,31},{8,0},{9,1... | collective-permute-start | bytes 491528 | tf_op jit(solution)/shard_map/ppermute | solution.py:33
  244.7 9.1 %collective-permute-start.11 = (bf16[5,4,4096]{2,1,0:T(4,128)(2,1)S(1)}, bf16[5,4,4096]{2,1,0:T(4,128)(2,1)S(1)}, u32[]{:S(2)}, u32[]{:S(2)}) collective-permute-start(bf16[5,4,4096]{2,1,0:T(4,128)(2,1)S(1)} %squeeze.166), channel_id=1, source_target_pairs={{0,23},{1,24},{2,25},{3,26},{4,27},{5,28},{6,29},{7,30},{8,31},{9,... | collective-permute-start | bytes 491528 | tf_op jit(solution)/shard_map/ppermute | solution.py:33
  253.9 15.2 %collective-permute-done.7 = bf16[5,4,4096]{2,1,0:T(4,128)(2,1)S(1)} collective-permute-done((bf16[5,4,4096]{2,1,0:T(4,128)(2,1)S(1)}, bf16[5,4,4096]{2,1,0:T(4,128)(2,1)S(1)}, u32[]{:S(2)}, u32[]{:S(2)}) %collective-permute-start.7) | collective-permute-done | bytes 163872 | tf_op jit(solution)/shard_map/ppermute | solution.py:33
  269.3 1.1 copy.84
  270.4 3.5 %all-to-all-start.2 = ((bf16[4,5,2,4096]{3,2,1,0:T(2,128)(2,1)}), bf16[4,5,2,4096]{3,2,1,0:T(2,128)(2,1)S(1)}, u32[]{:S(2)}, u32[]{:S(2)}) async-start(bf16[4,5,2,4096]{3,2,1,0:T(2,128)(2,1)} %copy.84), calls=%async_computation.2 | async-start | bytes 655360 | tf_op jit(solution)/shard_map/all_to_all | solution.py:133
  273.9 19.7 %collective-permute-done.11 = bf16[5,4,4096]{2,1,0:T(4,128)(2,1)S(1)} collective-permute-done((bf16[5,4,4096]{2,1,0:T(4,128)(2,1)S(1)}, bf16[5,4,4096]{2,1,0:T(4,128)(2,1)S(1)}, u32[]{:S(2)}, u32[]{:S(2)}) %collective-permute-start.11) | collective-permute-done | bytes 163872 | tf_op jit(solution)/shard_map/ppermute | solution.py:33
  293.8 1.1 copy.89
  294.8 3.5 %all-to-all-start.4 = ((bf16[4,5,2,4096]{3,2,1,0:T(2,128)(2,1)}), bf16[4,5,2,4096]{3,2,1,0:T(2,128)(2,1)S(1)}, u32[]{:S(2)}, u32[]{:S(2)}) async-start(bf16[4,5,2,4096]{3,2,1,0:T(2,128)(2,1)} %copy.89), calls=%async_computation.4 | async-start | bytes 655360 | tf_op jit(solution)/shard_map/all_to_all | solution.py:133
  299.1 5.1 %all-to-all-done.4 = bf16[4,5,2,4096]{3,2,1,0:T(2,128)(2,1)S(1)} async-done(((bf16[4,5,2,4096]{3,2,1,0:T(2,128)(2,1)}), bf16[4,5,2,4096]{3,2,1,0:T(2,128)(2,1)S(1)}, u32[]{:S(2)}, u32[]{:S(2)}) %all-to-all-start.4) | async-done | bytes 327712 | tf_op jit(solution)/shard_map/all_to_all | solution.py:133
  304.3 0.6 fusion
  305.0 17.8 %all_to_all.31 = bf16[8,64,512]{2,1,0:T(8,128)(2,1)S(1)} all-to-all(bf16[8,64,512]{2,1,0:T(8,128)(2,1)S(1)} %bitcast.165), channel_id=1, replica_groups=mesh['blk'=8,'uly'=4,'dp'=32] {'blk'}, dimensions={0} | all-to-all | bytes 1048576 | tf_op jit(solution)/shard_map/all_to_all | solution.py:139
  322.8 0.7 reduce_sum.32
  (60 shorter events, 4.7 us)
Async XLA Ops:
  6.5 185.5 %copy-start = (bf16[1,4096,128]{2,1,0:T(8,128)(2,1)S(1)}, bf16[1,4096,128]{2,1,0:T(8,128)(2,1)}, u32[]{:S(2)}) copy-start(bf16[1,4096,128]{2,1,0:T(8,128)(2,1)} %param.11) | copy-start | bytes 3145732
  6.5 179.9 %all-gather.3.cloned.1.call-start = ((), (), s32[]{:S(2)}) async-start(), calls=%async_computation.6 | async-start | bytes 2949120 | tf_op jit(solution)/shard_map/all_gather | solution.py:105
  32.5 30.4 %collective-permute-start.1 = (bf16[5,4,4096]{2,1,0:T(4,128)(2,1)S(1)}, bf16[5,4,4096]{2,1,0:T(4,128)(2,1)S(1)}, u32[]{:S(2)}, u32[]{:S(2)}) collective-permute-start(bf16[5,4,4096]{2,1,0:T(4,128)(2,1)S(1)} %bitcast.186), channel_id=1, source_target_pairs={{0,1},{1,2},{2,3},{3,4},{4,5},{5,6},{6,7},{7,8},{8,9},{9,10},{10,1... | collective-permute-start | bytes 491528 | tf_op jit(solution)/shard_map/ppermute | solution.py:33
  52.2 32.7 %collective-permute-start = (bf16[5,4,4096]{2,1,0:T(4,128)(2,1)S(1)}, bf16[5,4,4096]{2,1,0:T(4,128)(2,1)S(1)}, u32[]{:S(2)}, u32[]{:S(2)}) collective-permute-start(bf16[5,4,4096]{2,1,0:T(4,128)(2,1)S(1)} %bitcast.184), channel_id=1, source_target_pairs={{0,16},{1,17},{2,18},{3,19},{4,20},{5,21},{6,22},{7,23},{8,24},{9,... | collective-permute-start | bytes 491528 | tf_op jit(solution)/shard_map/ppermute | solution.py:33
  86.2 114.8 %all-gather.5.cloned.1.call-start = ((), (), s32[]{:S(2)}) async-start(), calls=%async_computation.7 | async-start | bytes 2949120 | tf_op jit(solution)/shard_map/all_gather | solution.py:105
  86.3 60.6 %collective-permute-start.3 = (bf16[128,4096]{1,0:T(8,128)(2,1)}, bf16[128,4096]{1,0:T(8,128)(2,1)S(1)}, u32[]{:S(2)}, u32[]{:S(2)}) collective-permute-start(bf16[128,4096]{1,0:T(8,128)(2,1)} %bitcast.38), channel_id=1, source_target_pairs={{0,768},{128,896},{256,0},{384,128},{512,256},{640,384},{768,512},... | collective-permute-start | bytes 3145736 | tf_op jit(solution)/shard_map/ppermute | solution.py:38
  88.2 60.6 %collective-permute-start.2 = (bf16[128,4096]{1,0:T(8,128)(2,1)}, bf16[128,4096]{1,0:T(8,128)(2,1)S(1)}, u32[]{:S(2)}, u32[]{:S(2)}) collective-permute-start(bf16[128,4096]{1,0:T(8,128)(2,1)} %bitcast.38), channel_id=1, source_target_pairs={{0,256},{128,384},{256,512},{384,640},{512,768},{640,896},{768,0},... | collective-permute-start | bytes 3145736 | tf_op jit(solution)/shard_map/ppermute | solution.py:38
  94.2 38.5 %collective-permute-start.10 = (bf16[5,4,4096]{2,1,0:T(4,128)(2,1)S(1)}, bf16[5,4,4096]{2,1,0:T(4,128)(2,1)S(1)}, u32[]{:S(2)}, u32[]{:S(2)}) collective-permute-start(bf16[5,4,4096]{2,1,0:T(4,128)(2,1)S(1)} %bitcast.185), channel_id=1, source_target_pairs={{0,8},{1,9},{2,10},{3,11},{4,12},{5,13},{6,14},{7,15},{8,16},{9,17... | collective-permute-start | bytes 491528 | tf_op jit(solution)/shard_map/ppermute | solution.py:33
  108.7 35.2 %collective-permute-start.9 = (bf16[5,4,4096]{2,1,0:T(4,128)(2,1)S(1)}, bf16[5,4,4096]{2,1,0:T(4,128)(2,1)S(1)}, u32[]{:S(2)}, u32[]{:S(2)}) collective-permute-start(bf16[5,4,4096]{2,1,0:T(4,128)(2,1)S(1)} %bitcast.183), channel_id=1, source_target_pairs={{0,9},{1,10},{2,11},{3,12},{4,13},{5,14},{6,15},{7,16},{8,17},{9,1... | collective-permute-start | bytes 491528 | tf_op jit(solution)/shard_map/ppermute | solution.py:33
  146.9 17.9 %collective-permute-start.5 = (bf16[64,4096]{1,0:T(8,128)(2,1)S(1)}, bf16[64,4096]{1,0:T(8,128)(2,1)S(1)}, u32[]{:S(2)}, u32[]{:S(2)}) collective-permute-start(bf16[64,4096]{1,0:T(8,128)(2,1)S(1)} %slice.138), channel_id=1, source_target_pairs={{0,768},{128,896},{256,0},{384,128},{512,256},{640,384},{768,512},... | collective-permute-start | bytes 1572872 | tf_op jit(solution)/shard_map/ppermute | solution.py:38
  148.9 15.1 %collective-permute-start.4 = (bf16[64,4096]{1,0:T(8,128)(2,1)S(1)}, bf16[64,4096]{1,0:T(8,128)(2,1)S(1)}, u32[]{:S(2)}, u32[]{:S(2)}) collective-permute-start(bf16[64,4096]{1,0:T(8,128)(2,1)S(1)} %slice.137), channel_id=1, source_target_pairs={{0,256},{128,384},{256,512},{384,640},{512,768},{640,896},{768,0},... | collective-permute-start | bytes 1572872 | tf_op jit(solution)/shard_map/ppermute | solution.py:38
  165.7 51.3 %collective-permute-start.6 = (bf16[512,4096]{1,0:T(8,128)(2,1)}, bf16[512,4096]{1,0:T(8,128)(2,1)}, u32[]{:S(2)}, u32[]{:S(2)}) collective-permute-start(bf16[512,4096]{1,0:T(8,128)(2,1)} %constant_dynamic-update-slice_fusion), channel_id=1, source_target_pairs={{0,128},{128,0},{256,384},{384,256},{512,640},{640,512},{768,896},... | collective-permute-start | bytes 12582920 | tf_op jit(solution)/shard_map/ppermute | solution.py:42
  190.8 2.1 copy-start.3
  194.4 14.6 %all-to-all-start.1 = ((bf16[8,40,128]{2,1,0:T(8,128)(2,1)}), bf16[8,40,128]{2,1,0:T(8,128)(2,1)S(1)}, u32[]{:S(2)}, u32[]{:S(2)}) async-start(bf16[8,40,128]{2,1,0:T(8,128)(2,1)} %bitcast.29), calls=%async_computation.1 | async-start | bytes 163840 | tf_op jit(solution)/shard_map/all_to_all | solution.py:120
  209.0 8.0 %all-to-all-start.3 = ((bf16[8,40,128]{2,1,0:T(8,128)(2,1)}), bf16[8,40,128]{2,1,0:T(8,128)(2,1)S(1)}, u32[]{:S(2)}, u32[]{:S(2)}) async-start(bf16[8,40,128]{2,1,0:T(8,128)(2,1)} %bitcast.60), calls=%async_computation.3 | async-start | bytes 163840 | tf_op jit(solution)/shard_map/all_to_all | solution.py:120
  217.0 3.4 %copy-start.1 = (bf16[512,4096]{1,0:T(8,128)(2,1)S(1)}, bf16[512,4096]{1,0:T(8,128)(2,1)}, u32[]{:S(2)}) copy-start(bf16[512,4096]{1,0:T(8,128)(2,1)} %constant_dynamic-update-slice_fusion) | copy-start | bytes 12582916
  221.5 18.1 %copy-start.2 = (bf16[512,4096]{1,0:T(8,128)(2,1)S(1)}, bf16[512,4096]{1,0:T(8,128)(2,1)}, u32[]{:S(2)}) copy-start(bf16[512,4096]{1,0:T(8,128)(2,1)} %constant_dynamic-update-slice_fusion) | copy-start | bytes 12582916
  221.6 32.3 %collective-permute-start.8 = (bf16[5,4,4096]{2,1,0:T(4,128)(2,1)S(1)}, bf16[5,4,4096]{2,1,0:T(4,128)(2,1)S(1)}, u32[]{:S(2)}, u32[]{:S(2)}) collective-permute-start(bf16[5,4,4096]{2,1,0:T(4,128)(2,1)S(1)} %squeeze.154), channel_id=1, source_target_pairs={{0,31},{1,0},{2,1},{3,2},{4,3},{5,4},{6,5},{7,6},{8,7},{9,8},{10,9... | collective-permute-start | bytes 491528 | tf_op jit(solution)/shard_map/ppermute | solution.py:33
  223.7 45.3 %collective-permute-start.7 = (bf16[5,4,4096]{2,1,0:T(4,128)(2,1)S(1)}, bf16[5,4,4096]{2,1,0:T(4,128)(2,1)S(1)}, u32[]{:S(2)}, u32[]{:S(2)}) collective-permute-start(bf16[5,4,4096]{2,1,0:T(4,128)(2,1)S(1)} %squeeze.153), channel_id=1, source_target_pairs={{0,16},{1,17},{2,18},{3,19},{4,20},{5,21},{6,22},{7,23},{8,24},{9,... | collective-permute-start | bytes 491528 | tf_op jit(solution)/shard_map/ppermute | solution.py:33
  240.7 33.2 %collective-permute-start.12 = (bf16[5,4,4096]{2,1,0:T(4,128)(2,1)S(1)}, bf16[5,4,4096]{2,1,0:T(4,128)(2,1)S(1)}, u32[]{:S(2)}, u32[]{:S(2)}) collective-permute-start(bf16[5,4,4096]{2,1,0:T(4,128)(2,1)S(1)} %squeeze.167), channel_id=1, source_target_pairs={{0,24},{1,25},{2,26},{3,27},{4,28},{5,29},{6,30},{7,31},{8,0},{9,1... | collective-permute-start | bytes 491528 | tf_op jit(solution)/shard_map/ppermute | solution.py:33
  244.7 48.8 %collective-permute-start.11 = (bf16[5,4,4096]{2,1,0:T(4,128)(2,1)S(1)}, bf16[5,4,4096]{2,1,0:T(4,128)(2,1)S(1)}, u32[]{:S(2)}, u32[]{:S(2)}) collective-permute-start(bf16[5,4,4096]{2,1,0:T(4,128)(2,1)S(1)} %squeeze.166), channel_id=1, source_target_pairs={{0,23},{1,24},{2,25},{3,26},{4,27},{5,28},{6,29},{7,30},{8,31},{9,... | collective-permute-start | bytes 491528 | tf_op jit(solution)/shard_map/ppermute | solution.py:33
  270.4 24.5 %all-to-all-start.2 = ((bf16[4,5,2,4096]{3,2,1,0:T(2,128)(2,1)}), bf16[4,5,2,4096]{3,2,1,0:T(2,128)(2,1)S(1)}, u32[]{:S(2)}, u32[]{:S(2)}) async-start(bf16[4,5,2,4096]{3,2,1,0:T(2,128)(2,1)} %copy.84), calls=%async_computation.2 | async-start | bytes 655360 | tf_op jit(solution)/shard_map/all_to_all | solution.py:133
  294.8 9.3 %all-to-all-start.4 = ((bf16[4,5,2,4096]{3,2,1,0:T(2,128)(2,1)}), bf16[4,5,2,4096]{3,2,1,0:T(2,128)(2,1)S(1)}, u32[]{:S(2)}, u32[]{:S(2)}) async-start(bf16[4,5,2,4096]{3,2,1,0:T(2,128)(2,1)} %copy.89), calls=%async_computation.4 | async-start | bytes 655360 | tf_op jit(solution)/shard_map/all_to_all | solution.py:133
Sparse Core Ops, SparseCore 0:
  86.4 47.4 all-gather.2
  147.0 37.5 all-gather.4

commit v4 on v3

--- a/solution.py
+++ b/solution.py
@@ -43,7 +43,7 @@
 
 
 def chip_gather(value, n_blk):
-    half = value.shape[0] // 2
+    half = (value.shape[0] // 2 + 7) // 8 * 8
     below = chip_move(value, 1, n_blk)
     above = chip_move(value, -1, n_blk)
     far_low = chip_move(below[:half], 1, n_blk)
@@ -71,52 +71,56 @@
     own_shifts = lax.dynamic_slice_in_dim(jnp.asarray(shifts), b, 1, 0)[0]
     order = [own_shifts[j] for steps in CHUNKS for j in steps]
     z_of = (z + jnp.stack(order)) % n_dp
+    total = len(order)
     per = len(CHUNKS[0])
     rows = n_uly * CAPACITY * per
-    x_of = jnp.arange(n_uly, dtype=jnp.int32) * n_dp
-    experts = (x_of[None, :, None] + z_of.reshape(len(CHUNKS), 1, per)).reshape(-1)
+    experts = (jnp.arange(n_uly, dtype=jnp.int32)[:, None] * n_dp + z_of[None, :]).reshape(-1)
     hit = expert_ids[:, :, None] == experts[None, None, :]
     chosen = jnp.sum(hit.astype(jnp.float32), axis=1)
     weight = jnp.sum(jnp.where(hit, route_weight[:, :, None], 0.0), axis=1)
     before = jnp.dot(earlier, chosen, preferred_element_type=jnp.float32)
-    shape = (tokens_here, len(CHUNKS), n_uly, 1, per)
-    at = (before.reshape(shape) == places[None, None, None, :, None]).astype(jnp.float32)
-    placing = (at * chosen.reshape(shape)).astype(jnp.bfloat16).reshape(tokens_here, len(CHUNKS), rows)
-    mixing = (at * weight.reshape(shape)).reshape(tokens_here, len(CHUNKS), rows)
+    shape = (tokens_here, n_uly, 1, total)
+    at = (before.reshape(shape) == places[None, None, :, None]).astype(jnp.float32)
+    placing = (at * chosen.reshape(shape)).astype(jnp.bfloat16).reshape(tokens_here, n_uly * CAPACITY * total)
+    mixing = at * weight.reshape(shape)
 
     index_own = (b // 2 + jnp.array(NEAR, jnp.int32)) % (n_blk // 2) * 2 + b % 2
     index_other = index_own + 1 - 2 * (b % 2)
 
-    outgoing = [
-        lax.dot_general(placing[:, n], tokens, (((0,), (0,)), ((), ())), preferred_element_type=jnp.float32)
-        .astype(jnp.bfloat16)
-        .reshape(n_uly, CAPACITY, per, width)
-        for n in range(len(CHUNKS))
-    ]
-    crossed = lax.all_to_all(jnp.stack(outgoing, axis=1), "uly", split_axis=0, concat_axis=0, tiled=True)
+    near_of = jnp.array([0, 2, 3, 1], jnp.int32)
+    chips = n_blk // 2
+    to_all = jnp.arange(n_blk, dtype=jnp.int32)
+    place_of = near_of[(to_all // 2 - b // 2) % chips] + chips * ((to_all + b) % 2)
+
+    outgoing = lax.dot_general(
+        placing, tokens, (((0,), (0,)), ((), ())), preferred_element_type=jnp.float32
+    ).astype(jnp.bfloat16)
+    crossed = lax.all_to_all(
+        outgoing.reshape(n_uly, CAPACITY, total, width), "uly", split_axis=0, concat_axis=0, tiled=True
+    )
     gathered = []
     for n, steps in enumerate(CHUNKS):
         arrived = []
         for i, j in enumerate(steps):
-            chunk = jnp.transpose(crossed[:, n, :, i, :], (1, 0, 2))
+            chunk = jnp.transpose(crossed[:, :, n * per + i, :], (1, 0, 2))
             arrived.append(move(chunk, shifts, j, 1, n_blk, n_dp))
-        mine = jnp.stack(arrived).reshape(rows, n_blk, part)
-        mine = jnp.transpose(mine, (1, 0, 2)).reshape(rows * n_blk, part)
-        gathered.append(lax.all_gather(mine, "blk", axis=1, tiled=True))
+        mine = jnp.stack(arrived).reshape(rows, width)
+        gathered.append(chip_gather(mine, n_blk))
 
     home = []
     answers = []
     for n, steps in enumerate(CHUNKS):
-        everyone = gathered[n]
-        if answers:
-            everyone, _ = lax.optimization_barrier((everyone, answers[-1]))
-        everyone = everyone.reshape(n_blk, rows, n_blk, part)
-        everyone = jnp.transpose(everyone, (2, 1, 0, 3)).reshape(n_blk * rows, width)
-        gate = jnp.dot(everyone, w_gate[0], preferred_element_type=jnp.float32)
-        up = jnp.dot(everyone, w_up[0], preferred_element_type=jnp.float32)
-        hidden = (jax.nn.silu(gate) * up).astype(jnp.bfloat16)
-        units = hidden.shape[1]
-        hidden = hidden.reshape(n_blk, rows, units)
+        halves = gathered[n]
+        hidden = []
+        for half in halves:
+            gate = jnp.dot(half, w_gate[0], preferred_element_type=jnp.float32)
+            up = jnp.dot(half, w_up[0], preferred_element_type=jnp.float32)
+            hidden.append((jax.nn.silu(gate) * up).astype(jnp.bfloat16))
+        units = hidden[0].shape[1]
+        hidden = jnp.concatenate(hidden, axis=0).reshape(n_blk, rows, units)
+        hidden = jnp.stack(
+            [lax.dynamic_index_in_dim(hidden, place_of[i], 0, keepdims=False) for i in range(n_blk)]
+        )
         hidden = lax.all_to_all(hidden, "blk", split_axis=0, concat_axis=0, tiled=True)
 
         def pick(index):
@@ -134,7 +138,7 @@
 
     mixed = 0.0
     for n in range(len(CHUNKS)):
-        mixed = mixed + jnp.dot(mixing[:, n], home[n].astype(jnp.float32), precision=lax.Precision.HIGHEST)
+        mixed = mixed + jnp.dot(mixing[:, :, :, n * per : (n + 1) * per].reshape(tokens_here, rows), home[n].astype(jnp.float32), precision=lax.Precision.HIGHEST)
     mixed = mixed.astype(jnp.bfloat16).reshape(tokens_here, n_blk, part)
     mixed = lax.all_to_all(jnp.transpose(mixed, (1, 0, 2)), "blk", split_axis=0, concat_axis=0, tiled=True)
     return jnp.sum(mixed.astype(jnp.float32), axis=0).astype(jnp.bfloat16)

time: 334 us -> 332 us (level)
  starting transfers between devices: 110 us -> 160 us
  waiting for transfers between devices: 105 us -> 61.4 us
  blocking collectives: 31.7 us -> 13.8 us
  matrix products: 16.5 us -> 22 us
    ppermute x8, waiting for transfers between devices: 87.8 us -> 47.9 us  [move(): return lax.ppermute(value, ('blk', 'dp'), pairs)]
    ppermute x1 -> x3, starting transfers between devices: 3.67 us -> 28.2 us  [core_swap(): return lax.ppermute(value, 'blk', [(b, b ^ 1) for b in range(n_blk)])]
    ppermute x4 -> x12, starting transfers between devices: 13 us -> 36.4 us  [chip_move(): lax.ppermute(value, 'blk', [(b, (b // 2 + step) % chips * 2 + b % 2) for...]
    all_to_all x1 -> x0, blocking collectives: 13.8 us -> none  [block(): lax.all_to_all(jnp.stack(outgoing, axis=1), 'uly', split_axis=0, concat_a...]
    ppermute x4 -> x12, waiting for transfers between devices: 8.43 us -> 0.03 us  [chip_move(): lax.ppermute(value, 'blk', [(b, (b // 2 + step) % chips * 2 + b % 2) for...]
    all_to_all x0 -> x1, waiting for transfers between devices: none -> 5.24 us  [block(): lax.all_to_all(outgoing.reshape(n_uly, CAPACITY, total, width), 'uly', sp...]
    dot_general x2, matrix products: 1.69 us -> 6.1 us  [block(): jnp.dot(pick(index_own), down_own, preferred_element_type=jnp.float32)]
    all_to_all x0 -> x1, starting transfers between devices: none -> 4.02 us  [block(): lax.all_to_all(outgoing.reshape(n_uly, CAPACITY, total, width), 'uly', sp...]
  transfers between devices with their start and end apart: 19 -> 28, of which waited for: 8 -> 5; matrix products, arithmetic and copies ran while one was open for 11% -> 16% of each run, Pallas kernels for 0% -> 0%
where the time goes in v4:
time: 332 us; the launch traced here: 327 us
  starting transfers between devices  160 us (48%)
  waiting for transfers between devices  61.4 us (18%)
  local copies, waits for them, and re-layouts  34.2 us (10%)
  between operations  30.7 us (9%)
  matrix products  22 us (7%)
  blocking collectives  13.8 us (4%)
  other arithmetic  5.56 us (2%)
    ppermute x8, starting transfers between devices, move(): return lax.ppermute(value, ('blk', 'dp'), pairs)  72.9 us
    ppermute x8, waiting for transfers between devices, move(): return lax.ppermute(value, ('blk', 'dp'), pairs)  47.9 us
    ppermute x12, starting transfers between devices, chip_move(): lax.ppermute(value, 'blk', [(b, (b // 2 + step) % chips * 2 + b % 2) for...  36.4 us
    ppermute x3, starting transfers between devices, core_swap(): return lax.ppermute(value, 'blk', [(b, b ^ 1) for b in range(n_blk)])  28.2 us
    unnamed x36, local copies, waits for them, and re-layouts  18.1 us
    all_to_all x1, blocking collectives, block(): lax.all_to_all(jnp.transpose(mixed, (1, 0, 2)), 'blk', split_axis=0, conc...  13.8 us
    all_to_all x2, starting transfers between devices, block(): lax.all_to_all(hidden, 'blk', split_axis=0, concat_axis=0, tiled=True)  11.4 us
    all_to_all x2, starting transfers between devices, block(): lax.all_to_all(back, 'uly', split_axis=0, concat_axis=0, tiled=True)  6.91 us
  transfers between devices with their start and end apart: 28, of which 5 were waited for; matrix products, arithmetic and copies ran while one was open for 16% of the time, Pallas kernels for 0%

profile of v4, /device:TPU:25, one launch (start us, length us, event | category | flops | bytes accessed | tf_op | source)
XLA Modules:
  0.0 327.5 jit_solution(16843266365254395399)
XLA Ops:
  0.0 2.5 collective-permute-start.8
  2.5 4.1 %collective-permute-start.7 = (bf16[128,4096]{1,0:T(8,128)(2,1)}, bf16[128,4096]{1,0:T(8,128)(2,1)}, u32[]{:S(2)}, u32[]{:S(2)}) collective-permute-start(bf16[128,4096]{1,0:T(8,128)(2,1)} %bitcast.161), channel_id=1, source_target_pairs={{0,256},{128,384},{256,512},{384,640},{512,768},{640,896},{768,0},... | collective-permute-start | bytes 3145736 | tf_op jit(solution)/shard_map/ppermute | solution.py:38
  8.0 2.0 add_subtract_fusion
  10.2 0.8 fusion.25
  11.3 1.4 convolution_convert_fusion
  12.7 1.1 reshape.188
  13.8 4.0 %all-to-all-start = ((bf16[4,5,4,4096]{3,2,1,0:T(4,128)(2,1)}), bf16[4,5,4,4096]{3,2,1,0:T(4,128)(2,1)S(1)}, u32[]{:S(2)}, u32[]{:S(2)}) async-start(bf16[4,5,4,4096]{3,2,1,0:T(4,128)(2,1)} %reshape.188), calls=%async_computation | async-start | bytes 1310720 | tf_op jit(solution)/shard_map/all_to_all | solution.py:98
  17.8 1.1 constant_dynamic-update-slice_fusion.17
  20.2 5.2 %all-to-all-done = bf16[4,5,4,4096]{3,2,1,0:T(4,128)(2,1)S(1)} async-done(((bf16[4,5,4,4096]{3,2,1,0:T(4,128)(2,1)}), bf16[4,5,4,4096]{3,2,1,0:T(4,128)(2,1)S(1)}, u32[]{:S(2)}, u32[]{:S(2)}) %all-to-all-start) | async-done | bytes 655392 | tf_op jit(solution)/shard_map/all_to_all | solution.py:98
  25.4 0.9 fusion.85
  26.8 21.3 %collective-permute-start.1 = (bf16[5,4,4096]{2,1,0:T(4,128)(2,1)S(1)}, bf16[5,4,4096]{2,1,0:T(4,128)(2,1)S(1)}, u32[]{:S(2)}, u32[]{:S(2)}) collective-permute-start(bf16[5,4,4096]{2,1,0:T(4,128)(2,1)S(1)} %bitcast.187), channel_id=1, source_target_pairs={{0,1},{1,2},{2,3},{3,4},{4,5},{5,6},{6,7},{7,8},{8,9},{9,10},{10,1... | collective-permute-start | bytes 491528 | tf_op jit(solution)/shard_map/ppermute | solution.py:33
  48.1 10.7 %collective-permute-start = (bf16[5,4,4096]{2,1,0:T(4,128)(2,1)S(1)}, bf16[5,4,4096]{2,1,0:T(4,128)(2,1)S(1)}, u32[]{:S(2)}, u32[]{:S(2)}) collective-permute-start(bf16[5,4,4096]{2,1,0:T(4,128)(2,1)S(1)} %bitcast.186), channel_id=1, source_target_pairs={{0,16},{1,17},{2,18},{3,19},{4,20},{5,21},{6,22},{7,23},{8,24},{9,... | collective-permute-start | bytes 491528 | tf_op jit(solution)/shard_map/ppermute | solution.py:33
  90.0 0.9 copy.95
  90.9 0.9 copy.93
  91.8 2.4 collective-permute-start.14
  94.2 11.9 %collective-permute-start.15 = (bf16[5,4,4096]{2,1,0:T(4,128)(2,1)}, bf16[5,4,4096]{2,1,0:T(4,128)(2,1)}, u32[]{:S(2)}, u32[]{:S(2)}) collective-permute-start(bf16[5,4,4096]{2,1,0:T(4,128)(2,1)} %bitcast.157), channel_id=1, source_target_pairs={{0,8},{1,9},{2,10},{3,11},{4,12},{5,13},{6,14},{7,15},{8,16},{9,17... | collective-permute-start | bytes 491528 | tf_op jit(solution)/shard_map/ppermute | solution.py:33
  106.4 1.9 collective-permute-start.3
  108.4 12.7 %collective-permute-done.14 = bf16[5,4,4096]{2,1,0:T(4,128)(2,1)} collective-permute-done((bf16[5,4,4096]{2,1,0:T(4,128)(2,1)}, bf16[5,4,4096]{2,1,0:T(4,128)(2,1)}, u32[]{:S(2)}, u32[]{:S(2)}) %collective-permute-start.14) | collective-permute-done | bytes 163872 | tf_op jit(solution)/shard_map/ppermute | solution.py:33
  121.1 1.9 collective-permute-start.2
  123.0 1.2 pad_maximum_fusion.1
  124.3 3.4 %collective-permute-start.17 = (bf16[40,4096]{1,0:T(8,128)(2,1)S(1)}, bf16[40,4096]{1,0:T(8,128)(2,1)S(1)}, u32[]{:S(2)}, u32[]{:S(2)}) collective-permute-start(bf16[40,4096]{1,0:T(8,128)(2,1)S(1)} %reshape.191), channel_id=1, source_target_pairs={{0,768},{128,896},{256,0},{384,128},{512,256},{640,384},{768,512},... | collective-permute-start | bytes 983048 | tf_op jit(solution)/shard_map/ppermute | solution.py:38
  127.7 3.1 collective-permute-start.16
  130.9 0.9 slice.171
  131.8 3.4 %collective-permute-start.5 = (bf16[16,4096]{1,0:T(8,128)(2,1)S(1)}, bf16[16,4096]{1,0:T(8,128)(2,1)S(1)}, u32[]{:S(2)}, u32[]{:S(2)}) collective-permute-start(bf16[16,4096]{1,0:T(8,128)(2,1)S(1)} %slice.171), channel_id=1, source_target_pairs={{0,768},{128,896},{256,0},{384,128},{512,256},{640,384},{768,512},... | collective-permute-start | bytes 393224 | tf_op jit(solution)/shard_map/ppermute | solution.py:38
  135.2 1.0 constant_dynamic-update-slice_fusion.3
  136.2 1.0 constant_dynamic-update-slice_fusion.2
  137.2 0.9 slice.170
  138.2 3.1 collective-permute-start.4
  141.3 2.2 collective-permute-start.19
  143.6 4.3 %collective-permute-start.18 = (bf16[24,4096]{1,0:T(8,128)(2,1)S(1)}, bf16[24,4096]{1,0:T(8,128)(2,1)S(1)}, u32[]{:S(2)}, u32[]{:S(2)}) collective-permute-start(bf16[24,4096]{1,0:T(8,128)(2,1)S(1)} %slice.178), channel_id=1, source_target_pairs={{0,256},{128,384},{256,512},{384,640},{512,768},{640,896},{768,0},... | collective-permute-start | bytes 589832 | tf_op jit(solution)/shard_map/ppermute | solution.py:38
  147.9 1.1 slice.173
  149.0 1.9 collective-permute-start.10
  150.9 2.3 constant_dynamic-update-slice_fusion.16
  153.2 2.3 constant_dynamic-update-slice_fusion.15
  155.5 1.1 slice.172
  156.6 4.6 %collective-permute-start.9 = (bf16[64,4096]{1,0:T(8,128)(2,1)S(1)}, bf16[64,4096]{1,0:T(8,128)(2,1)S(1)}, u32[]{:S(2)}, u32[]{:S(2)}) collective-permute-start(bf16[64,4096]{1,0:T(8,128)(2,1)S(1)} %slice.172), channel_id=1, source_target_pairs={{0,256},{128,384},{256,512},{384,640},{512,768},{640,896},{768,0},... | collective-permute-start | bytes 1572872 | tf_op jit(solution)/shard_map/ppermute | solution.py:38
  161.2 22.1 %collective-permute-start.6 = (bf16[160,4096]{1,0:T(8,128)(2,1)S(1)}, bf16[160,4096]{1,0:T(8,128)(2,1)}, u32[]{:S(2)}, u32[]{:S(2)}) collective-permute-start(bf16[160,4096]{1,0:T(8,128)(2,1)S(1)} %constant_dynamic-update-slice_fusion), channel_id=1, source_target_pairs={{0,128},{128,0},{256,384},{384,256},{512,640},{640,512},{768,896},... | collective-permute-start | bytes 3932168 | tf_op jit(solution)/shard_map/ppermute | solution.py:42
  183.9 1.9 collective-permute-start.20
  185.8 0.8 constant_dynamic-update-slice_fusion.14
  186.6 0.8 constant_dynamic-update-slice_fusion.13
  187.5 4.2 %collective-permute-start.11 = (bf16[512,4096]{1,0:T(8,128)(2,1)}, bf16[512,4096]{1,0:T(8,128)(2,1)}, u32[]{:S(2)}, u32[]{:S(2)}) collective-permute-start(bf16[512,4096]{1,0:T(8,128)(2,1)} %constant_dynamic-update-slice_fusion.13), channel_id=1, source_target_pairs={{0,128},{128,0},{256,384},{384,256},{512,640},{640,512},{768,896},... | collective-permute-start | bytes 12582920 | tf_op jit(solution)/shard_map/ppermute | solution.py:42
  199.1 6.6 %all-to-all-start.3 = ((bf16[8,40,128]{2,1,0:T(8,128)(2,1)}), bf16[8,40,128]{2,1,0:T(8,128)(2,1)S(1)}, u32[]{:S(2)}, u32[]{:S(2)}) async-start(bf16[8,40,128]{2,1,0:T(8,128)(2,1)} %constant_dynamic-update-slice_fusion.23), calls=%async_computation.3 | async-start | bytes 163840 | tf_op jit(solution)/shard_map/all_to_all | solution.py:124
  205.7 1.8 fusion.16
  207.5 1.8 multiply_convert_fusion.2
  214.1 4.8 %all-to-all-start.1 = ((bf16[8,40,128]{2,1,0:T(8,128)(2,1)}), bf16[8,40,128]{2,1,0:T(8,128)(2,1)S(1)}, u32[]{:S(2)}, u32[]{:S(2)}) async-start(bf16[8,40,128]{2,1,0:T(8,128)(2,1)} %constant_dynamic-update-slice_fusion.5), calls=%async_computation.1 | async-start | bytes 163840 | tf_op jit(solution)/shard_map/all_to_all | solution.py:124
  218.9 3.2 all-to-all-done.1
  222.1 3.0 fusion.48
  225.1 3.1 fusion.3
  228.4 1.9 collective-permute-start.22
  230.3 6.2 %collective-permute-start.21 = (bf16[5,4,4096]{2,1,0:T(4,128)(2,1)S(1)}, bf16[5,4,4096]{2,1,0:T(4,128)(2,1)S(1)}, u32[]{:S(2)}, u32[]{:S(2)}) collective-permute-start(bf16[5,4,4096]{2,1,0:T(4,128)(2,1)S(1)} %squeeze.210), channel_id=1, source_target_pairs={{0,23},{1,24},{2,25},{3,26},{4,27},{5,28},{6,29},{7,30},{8,31},{9,... | collective-permute-start | bytes 491528 | tf_op jit(solution)/shard_map/ppermute | solution.py:33
  236.6 3.0 fusion.33
  239.6 3.0 fusion.2
  242.8 5.9 %collective-permute-start.13 = (bf16[5,4,4096]{2,1,0:T(4,128)(2,1)S(1)}, bf16[5,4,4096]{2,1,0:T(4,128)(2,1)S(1)}, u32[]{:S(2)}, u32[]{:S(2)}) collective-permute-start(bf16[5,4,4096]{2,1,0:T(4,128)(2,1)S(1)} %squeeze.199), channel_id=1, source_target_pairs={{0,31},{1,0},{2,1},{3,2},{4,3},{5,4},{6,5},{7,6},{8,7},{9,8},{10,9... | collective-permute-start | bytes 491528 | tf_op jit(solution)/shard_map/ppermute | solution.py:33
  248.8 12.7 %collective-permute-start.12 = (bf16[5,4,4096]{2,1,0:T(4,128)(2,1)S(1)}, bf16[5,4,4096]{2,1,0:T(4,128)(2,1)S(1)}, u32[]{:S(2)}, u32[]{:S(2)}) collective-permute-start(bf16[5,4,4096]{2,1,0:T(4,128)(2,1)S(1)} %squeeze.198), channel_id=1, source_target_pairs={{0,16},{1,17},{2,18},{3,19},{4,20},{5,21},{6,22},{7,23},{8,24},{9,... | collective-permute-start | bytes 491528 | tf_op jit(solution)/shard_map/ppermute | solution.py:33
  261.7 1.1 copy.74
  262.8 3.5 %all-to-all-start.4 = ((bf16[4,5,2,4096]{3,2,1,0:T(2,128)(2,1)}), bf16[4,5,2,4096]{3,2,1,0:T(2,128)(2,1)S(1)}, u32[]{:S(2)}, u32[]{:S(2)}) async-start(bf16[4,5,2,4096]{3,2,1,0:T(2,128)(2,1)} %copy.74), calls=%async_computation.4 | async-start | bytes 655360 | tf_op jit(solution)/shard_map/all_to_all | solution.py:137
  266.3 35.1 %collective-permute-done.12 = bf16[5,4,4096]{2,1,0:T(4,128)(2,1)S(1)} collective-permute-done((bf16[5,4,4096]{2,1,0:T(4,128)(2,1)S(1)}, bf16[5,4,4096]{2,1,0:T(4,128)(2,1)S(1)}, u32[]{:S(2)}, u32[]{:S(2)}) %collective-permute-start.12) | collective-permute-done | bytes 163872 | tf_op jit(solution)/shard_map/ppermute | solution.py:33
  301.6 1.1 copy.70
  302.7 3.5 %all-to-all-start.2 = ((bf16[4,5,2,4096]{3,2,1,0:T(2,128)(2,1)}), bf16[4,5,2,4096]{3,2,1,0:T(2,128)(2,1)S(1)}, u32[]{:S(2)}, u32[]{:S(2)}) async-start(bf16[4,5,2,4096]{3,2,1,0:T(2,128)(2,1)} %copy.70), calls=%async_computation.2 | async-start | bytes 655360 | tf_op jit(solution)/shard_map/all_to_all | solution.py:137
  306.2 0.9 convolution_bitcast_fusion
  307.0 5.0 %all-to-all-done.2 = bf16[4,5,2,4096]{3,2,1,0:T(2,128)(2,1)S(1)} async-done(((bf16[4,5,2,4096]{3,2,1,0:T(2,128)(2,1)}), bf16[4,5,2,4096]{3,2,1,0:T(2,128)(2,1)S(1)}, u32[]{:S(2)}, u32[]{:S(2)}) %all-to-all-start.2) | async-done | bytes 327712 | tf_op jit(solution)/shard_map/all_to_all | solution.py:137
  312.0 0.9 fusion.1
  312.9 13.8 %all_to_all.30 = bf16[8,64,512]{2,1,0:T(8,128)(2,1)S(1)} all-to-all(bf16[8,64,512]{2,1,0:T(8,128)(2,1)S(1)} %bitcast.159), channel_id=1, replica_groups=mesh['blk'=8,'uly'=4,'dp'=32] {'blk'}, dimensions={0} | all-to-all | bytes 1048576 | tf_op jit(solution)/shard_map/all_to_all | solution.py:143
  326.8 0.7 reduce_sum.32
  (99 shorter events, 19.0 us)
Async XLA Ops:
  0.0 183.4 %copy-start = (bf16[1,4096,128]{2,1,0:T(8,128)(2,1)S(1)}, bf16[1,4096,128]{2,1,0:T(8,128)(2,1)}, u32[]{:S(2)}) copy-start(bf16[1,4096,128]{2,1,0:T(8,128)(2,1)} %param.12) | copy-start | bytes 3145732
  0.0 143.6 %collective-permute-start.8 = (bf16[128,4096]{1,0:T(8,128)(2,1)}, bf16[128,4096]{1,0:T(8,128)(2,1)}, u32[]{:S(2)}, u32[]{:S(2)}) collective-permute-start(bf16[128,4096]{1,0:T(8,128)(2,1)} %bitcast.160), channel_id=1, source_target_pairs={{0,768},{128,896},{256,0},{384,128},{512,256},{640,384},{768,512},... | collective-permute-start | bytes 3145736 | tf_op jit(solution)/shard_map/ppermute | solution.py:38
  2.5 146.5 %collective-permute-start.7 = (bf16[128,4096]{1,0:T(8,128)(2,1)}, bf16[128,4096]{1,0:T(8,128)(2,1)}, u32[]{:S(2)}, u32[]{:S(2)}) collective-permute-start(bf16[128,4096]{1,0:T(8,128)(2,1)} %bitcast.161), channel_id=1, source_target_pairs={{0,256},{128,384},{256,512},{384,640},{512,768},{640,896},{768,0},... | collective-permute-start | bytes 3145736 | tf_op jit(solution)/shard_map/ppermute | solution.py:38
  12.7 5.1 %copy-start.3 = (bf16[1,128,4096]{2,1,0:T(8,128)(2,1)S(1)}, bf16[1,128,4096]{2,1,0:T(8,128)(2,1)}, u32[]{:S(2)}) copy-start(bf16[1,128,4096]{2,1,0:T(8,128)(2,1)} %param.14) | copy-start | bytes 3145732
  13.8 11.7 %all-to-all-start = ((bf16[4,5,4,4096]{3,2,1,0:T(4,128)(2,1)}), bf16[4,5,4,4096]{3,2,1,0:T(4,128)(2,1)S(1)}, u32[]{:S(2)}, u32[]{:S(2)}) async-start(bf16[4,5,4,4096]{3,2,1,0:T(4,128)(2,1)} %reshape.188), calls=%async_computation | async-start | bytes 1310720 | tf_op jit(solution)/shard_map/all_to_all | solution.py:98
  17.8 1.1 copy-start.1
  26.8 67.4 %collective-permute-start.1 = (bf16[5,4,4096]{2,1,0:T(4,128)(2,1)S(1)}, bf16[5,4,4096]{2,1,0:T(4,128)(2,1)S(1)}, u32[]{:S(2)}, u32[]{:S(2)}) collective-permute-start(bf16[5,4,4096]{2,1,0:T(4,128)(2,1)S(1)} %bitcast.187), channel_id=1, source_target_pairs={{0,1},{1,2},{2,3},{3,4},{4,5},{5,6},{6,7},{7,8},{8,9},{9,10},{10,1... | collective-permute-start | bytes 491528 | tf_op jit(solution)/shard_map/ppermute | solution.py:33
  48.1 58.0 %collective-permute-start = (bf16[5,4,4096]{2,1,0:T(4,128)(2,1)S(1)}, bf16[5,4,4096]{2,1,0:T(4,128)(2,1)S(1)}, u32[]{:S(2)}, u32[]{:S(2)}) collective-permute-start(bf16[5,4,4096]{2,1,0:T(4,128)(2,1)S(1)} %bitcast.186), channel_id=1, source_target_pairs={{0,16},{1,17},{2,18},{3,19},{4,20},{5,21},{6,22},{7,23},{8,24},{9,... | collective-permute-start | bytes 491528 | tf_op jit(solution)/shard_map/ppermute | solution.py:33
  91.8 29.3 %collective-permute-start.14 = (bf16[5,4,4096]{2,1,0:T(4,128)(2,1)}, bf16[5,4,4096]{2,1,0:T(4,128)(2,1)}, u32[]{:S(2)}, u32[]{:S(2)}) collective-permute-start(bf16[5,4,4096]{2,1,0:T(4,128)(2,1)} %bitcast.155), channel_id=1, source_target_pairs={{0,9},{1,10},{2,11},{3,12},{4,13},{5,14},{6,15},{7,16},{8,17},{9,1... | collective-permute-start | bytes 491528 | tf_op jit(solution)/shard_map/ppermute | solution.py:33
  94.2 28.8 %collective-permute-start.15 = (bf16[5,4,4096]{2,1,0:T(4,128)(2,1)}, bf16[5,4,4096]{2,1,0:T(4,128)(2,1)}, u32[]{:S(2)}, u32[]{:S(2)}) collective-permute-start(bf16[5,4,4096]{2,1,0:T(4,128)(2,1)} %bitcast.157), channel_id=1, source_target_pairs={{0,8},{1,9},{2,10},{3,11},{4,12},{5,13},{6,14},{7,15},{8,16},{9,17... | collective-permute-start | bytes 491528 | tf_op jit(solution)/shard_map/ppermute | solution.py:33
  106.4 21.3 %collective-permute-start.3 = (bf16[40,4096]{1,0:T(8,128)(2,1)S(1)}, bf16[40,4096]{1,0:T(8,128)(2,1)}, u32[]{:S(2)}, u32[]{:S(2)}) collective-permute-start(bf16[40,4096]{1,0:T(8,128)(2,1)S(1)} %reshape.189), channel_id=1, source_target_pairs={{0,768},{128,896},{256,0},{384,128},{512,256},{640,384},{768,512},... | collective-permute-start | bytes 983048 | tf_op jit(solution)/shard_map/ppermute | solution.py:38
  121.1 10.7 %collective-permute-start.2 = (bf16[40,4096]{1,0:T(8,128)(2,1)S(1)}, bf16[40,4096]{1,0:T(8,128)(2,1)}, u32[]{:S(2)}, u32[]{:S(2)}) collective-permute-start(bf16[40,4096]{1,0:T(8,128)(2,1)S(1)} %reshape.189), channel_id=1, source_target_pairs={{0,256},{128,384},{256,512},{384,640},{512,768},{640,896},{768,0},... | collective-permute-start | bytes 983048 | tf_op jit(solution)/shard_map/ppermute | solution.py:38
  124.3 13.8 %collective-permute-start.17 = (bf16[40,4096]{1,0:T(8,128)(2,1)S(1)}, bf16[40,4096]{1,0:T(8,128)(2,1)S(1)}, u32[]{:S(2)}, u32[]{:S(2)}) collective-permute-start(bf16[40,4096]{1,0:T(8,128)(2,1)S(1)} %reshape.191), channel_id=1, source_target_pairs={{0,768},{128,896},{256,0},{384,128},{512,256},{640,384},{768,512},... | collective-permute-start | bytes 983048 | tf_op jit(solution)/shard_map/ppermute | solution.py:38
  127.7 13.6 %collective-permute-start.16 = (bf16[40,4096]{1,0:T(8,128)(2,1)S(1)}, bf16[40,4096]{1,0:T(8,128)(2,1)S(1)}, u32[]{:S(2)}, u32[]{:S(2)}) collective-permute-start(bf16[40,4096]{1,0:T(8,128)(2,1)S(1)} %reshape.191), channel_id=1, source_target_pairs={{0,256},{128,384},{256,512},{384,640},{512,768},{640,896},{768,0},... | collective-permute-start | bytes 983048 | tf_op jit(solution)/shard_map/ppermute | solution.py:38
  131.8 29.4 %collective-permute-start.5 = (bf16[16,4096]{1,0:T(8,128)(2,1)S(1)}, bf16[16,4096]{1,0:T(8,128)(2,1)S(1)}, u32[]{:S(2)}, u32[]{:S(2)}) collective-permute-start(bf16[16,4096]{1,0:T(8,128)(2,1)S(1)} %slice.171), channel_id=1, source_target_pairs={{0,768},{128,896},{256,0},{384,128},{512,256},{640,384},{768,512},... | collective-permute-start | bytes 393224 | tf_op jit(solution)/shard_map/ppermute | solution.py:38
  138.2 18.4 %collective-permute-start.4 = (bf16[24,4096]{1,0:T(8,128)(2,1)S(1)}, bf16[24,4096]{1,0:T(8,128)(2,1)S(1)}, u32[]{:S(2)}, u32[]{:S(2)}) collective-permute-start(bf16[24,4096]{1,0:T(8,128)(2,1)S(1)} %slice.170), channel_id=1, source_target_pairs={{0,256},{128,384},{256,512},{384,640},{512,768},{640,896},{768,0},... | collective-permute-start | bytes 589832 | tf_op jit(solution)/shard_map/ppermute | solution.py:38
  141.3 42.0 %collective-permute-start.19 = (bf16[16,4096]{1,0:T(8,128)(2,1)S(1)}, bf16[16,4096]{1,0:T(8,128)(2,1)S(1)}, u32[]{:S(2)}, u32[]{:S(2)}) collective-permute-start(bf16[16,4096]{1,0:T(8,128)(2,1)S(1)} %slice.179), channel_id=1, source_target_pairs={{0,768},{128,896},{256,0},{384,128},{512,256},{640,384},{768,512},... | collective-permute-start | bytes 393224 | tf_op jit(solution)/shard_map/ppermute | solution.py:38
  143.6 39.7 %collective-permute-start.18 = (bf16[24,4096]{1,0:T(8,128)(2,1)S(1)}, bf16[24,4096]{1,0:T(8,128)(2,1)S(1)}, u32[]{:S(2)}, u32[]{:S(2)}) collective-permute-start(bf16[24,4096]{1,0:T(8,128)(2,1)S(1)} %slice.178), channel_id=1, source_target_pairs={{0,256},{128,384},{256,512},{384,640},{512,768},{640,896},{768,0},... | collective-permute-start | bytes 589832 | tf_op jit(solution)/shard_map/ppermute | solution.py:38
  149.0 37.6 %collective-permute-start.10 = (bf16[64,4096]{1,0:T(8,128)(2,1)S(1)}, bf16[64,4096]{1,0:T(8,128)(2,1)S(1)}, u32[]{:S(2)}, u32[]{:S(2)}) collective-permute-start(bf16[64,4096]{1,0:T(8,128)(2,1)S(1)} %slice.173), channel_id=1, source_target_pairs={{0,768},{128,896},{256,0},{384,128},{512,256},{640,384},{768,512},... | collective-permute-start | bytes 1572872 | tf_op jit(solution)/shard_map/ppermute | solution.py:38
  156.6 29.2 %collective-permute-start.9 = (bf16[64,4096]{1,0:T(8,128)(2,1)S(1)}, bf16[64,4096]{1,0:T(8,128)(2,1)S(1)}, u32[]{:S(2)}, u32[]{:S(2)}) collective-permute-start(bf16[64,4096]{1,0:T(8,128)(2,1)S(1)} %slice.172), channel_id=1, source_target_pairs={{0,256},{128,384},{256,512},{384,640},{512,768},{640,896},{768,0},... | collective-permute-start | bytes 1572872 | tf_op jit(solution)/shard_map/ppermute | solution.py:38
  161.2 44.4 %collective-permute-start.6 = (bf16[160,4096]{1,0:T(8,128)(2,1)S(1)}, bf16[160,4096]{1,0:T(8,128)(2,1)}, u32[]{:S(2)}, u32[]{:S(2)}) collective-permute-start(bf16[160,4096]{1,0:T(8,128)(2,1)S(1)} %constant_dynamic-update-slice_fusion), channel_id=1, source_target_pairs={{0,128},{128,0},{256,384},{384,256},{512,640},{640,512},{768,896},... | collective-permute-start | bytes 3932168 | tf_op jit(solution)/shard_map/ppermute | solution.py:42
  183.9 9.3 %collective-permute-start.20 = (bf16[160,4096]{1,0:T(8,128)(2,1)S(1)}, bf16[160,4096]{1,0:T(8,128)(2,1)S(1)}, u32[]{:S(2)}, u32[]{:S(2)}) collective-permute-start(bf16[160,4096]{1,0:T(8,128)(2,1)S(1)} %constant_dynamic-update-slice_fusion.18), channel_id=1, source_target_pairs={{0,128},{128,0},{256,384},{384,256},{512,640},{640,512},{768,896},... | collective-permute-start | bytes 3932168 | tf_op jit(solution)/shard_map/ppermute | solution.py:42
  187.5 4.7 %copy-start.2 = (bf16[1,4096,128]{2,1,0:T(8,128)(2,1)S(1)}, bf16[1,4096,128]{2,1,0:T(8,128)(2,1)}, u32[]{:S(2)}) copy-start(bf16[1,4096,128]{2,1,0:T(8,128)(2,1)} %param.13) | copy-start | bytes 3145732
  187.5 34.7 %collective-permute-start.11 = (bf16[512,4096]{1,0:T(8,128)(2,1)}, bf16[512,4096]{1,0:T(8,128)(2,1)}, u32[]{:S(2)}, u32[]{:S(2)}) collective-permute-start(bf16[512,4096]{1,0:T(8,128)(2,1)} %constant_dynamic-update-slice_fusion.13), channel_id=1, source_target_pairs={{0,128},{128,0},{256,384},{384,256},{512,640},{640,512},{768,896},... | collective-permute-start | bytes 12582920 | tf_op jit(solution)/shard_map/ppermute | solution.py:42
  199.1 15.0 %all-to-all-start.3 = ((bf16[8,40,128]{2,1,0:T(8,128)(2,1)}), bf16[8,40,128]{2,1,0:T(8,128)(2,1)S(1)}, u32[]{:S(2)}, u32[]{:S(2)}) async-start(bf16[8,40,128]{2,1,0:T(8,128)(2,1)} %constant_dynamic-update-slice_fusion.23), calls=%async_computation.3 | async-start | bytes 163840 | tf_op jit(solution)/shard_map/all_to_all | solution.py:124
  214.1 8.0 %all-to-all-start.1 = ((bf16[8,40,128]{2,1,0:T(8,128)(2,1)}), bf16[8,40,128]{2,1,0:T(8,128)(2,1)S(1)}, u32[]{:S(2)}, u32[]{:S(2)}) async-start(bf16[8,40,128]{2,1,0:T(8,128)(2,1)} %constant_dynamic-update-slice_fusion.5), calls=%async_computation.1 | async-start | bytes 163840 | tf_op jit(solution)/shard_map/all_to_all | solution.py:124
  228.4 33.0 %collective-permute-start.22 = (bf16[5,4,4096]{2,1,0:T(4,128)(2,1)S(1)}, bf16[5,4,4096]{2,1,0:T(4,128)(2,1)S(1)}, u32[]{:S(2)}, u32[]{:S(2)}) collective-permute-start(bf16[5,4,4096]{2,1,0:T(4,128)(2,1)S(1)} %squeeze.211), channel_id=1, source_target_pairs={{0,24},{1,25},{2,26},{3,27},{4,28},{5,29},{6,30},{7,31},{8,0},{9,1... | collective-permute-start | bytes 491528 | tf_op jit(solution)/shard_map/ppermute | solution.py:33
  230.3 31.1 %collective-permute-start.21 = (bf16[5,4,4096]{2,1,0:T(4,128)(2,1)S(1)}, bf16[5,4,4096]{2,1,0:T(4,128)(2,1)S(1)}, u32[]{:S(2)}, u32[]{:S(2)}) collective-permute-start(bf16[5,4,4096]{2,1,0:T(4,128)(2,1)S(1)} %squeeze.210), channel_id=1, source_target_pairs={{0,23},{1,24},{2,25},{3,26},{4,27},{5,28},{6,29},{7,30},{8,31},{9,... | collective-permute-start | bytes 491528 | tf_op jit(solution)/shard_map/ppermute | solution.py:33
  242.8 23.4 %collective-permute-start.13 = (bf16[5,4,4096]{2,1,0:T(4,128)(2,1)S(1)}, bf16[5,4,4096]{2,1,0:T(4,128)(2,1)S(1)}, u32[]{:S(2)}, u32[]{:S(2)}) collective-permute-start(bf16[5,4,4096]{2,1,0:T(4,128)(2,1)S(1)} %squeeze.199), channel_id=1, source_target_pairs={{0,31},{1,0},{2,1},{3,2},{4,3},{5,4},{6,5},{7,6},{8,7},{9,8},{10,9... | collective-permute-start | bytes 491528 | tf_op jit(solution)/shard_map/ppermute | solution.py:33
  248.8 52.6 %collective-permute-start.12 = (bf16[5,4,4096]{2,1,0:T(4,128)(2,1)S(1)}, bf16[5,4,4096]{2,1,0:T(4,128)(2,1)S(1)}, u32[]{:S(2)}, u32[]{:S(2)}) collective-permute-start(bf16[5,4,4096]{2,1,0:T(4,128)(2,1)S(1)} %squeeze.198), channel_id=1, source_target_pairs={{0,16},{1,17},{2,18},{3,19},{4,20},{5,21},{6,22},{7,23},{8,24},{9,... | collective-permute-start | bytes 491528 | tf_op jit(solution)/shard_map/ppermute | solution.py:33
  262.8 39.9 %all-to-all-start.4 = ((bf16[4,5,2,4096]{3,2,1,0:T(2,128)(2,1)}), bf16[4,5,2,4096]{3,2,1,0:T(2,128)(2,1)S(1)}, u32[]{:S(2)}, u32[]{:S(2)}) async-start(bf16[4,5,2,4096]{3,2,1,0:T(2,128)(2,1)} %copy.74), calls=%async_computation.4 | async-start | bytes 655360 | tf_op jit(solution)/shard_map/all_to_all | solution.py:137
  302.7 9.3 %all-to-all-start.2 = ((bf16[4,5,2,4096]{3,2,1,0:T(2,128)(2,1)}), bf16[4,5,2,4096]{3,2,1,0:T(2,128)(2,1)S(1)}, u32[]{:S(2)}, u32[]{:S(2)}) async-start(bf16[4,5,2,4096]{3,2,1,0:T(2,128)(2,1)} %copy.70), calls=%async_computation.2 | async-start | bytes 655360 | tf_op jit(solution)/shard_map/all_to_all | solution.py:137

commit v5 on v2

--- a/solution.py
+++ b/solution.py
@@ -2,6 +2,8 @@
 import jax.numpy as jnp
 import numpy as np
 from jax import lax
+from jax.experimental import pallas as pl
+from jax.experimental.pallas import tpu as pltpu
 from jax.sharding import PartitionSpec as P
 
 CAPACITY = 5
@@ -32,7 +34,48 @@
     return lax.ppermute(value, ("blk", "dp"), pairs)
 
 
-def local(tokens, expert_ids, route_weight, w_gate, w_up, w_down):
+def first_layer(blocks, w_gate, w_up, n_blk, rows):
+    part = blocks.shape[1] // n_blk
+    units = w_gate.shape[1]
+    total = n_blk * rows
+
+    def body(x_ref, gate_ref, up_ref, out_ref, sum_ref):
+        step = pl.program_id(0)
+        stacked = jnp.concatenate([x_ref[:, n * part : (n + 1) * part] for n in range(n_blk)], axis=0)
+        both = jnp.concatenate([gate_ref[...], up_ref[...]], axis=1)
+        product = jnp.dot(stacked, both, preferred_element_type=jnp.float32)
+
+        @pl.when(step == 0)
+        def _():
+            sum_ref[...] = product
+
+        @pl.when(step > 0)
+        def _():
+            sum_ref[...] += product
+
+        @pl.when(step == n_blk - 1)
+        def _():
+            gate = sum_ref[:, :units]
+            up = sum_ref[:, units:]
+            out_ref[...] = (gate / (1.0 + jnp.exp(-gate)) * up).astype(jnp.bfloat16)
+
+    return pl.pallas_call(
+        body,
+        grid=(n_blk,),
+        in_specs=[
+            pl.BlockSpec((rows, n_blk * part), lambda h: (h, 0)),
+            pl.BlockSpec((part, units), lambda h: (h, 0)),
+            pl.BlockSpec((part, units), lambda h: (h, 0)),
+        ],
+        out_specs=pl.BlockSpec((total, units), lambda h: (0, 0)),
+        out_shape=jax.ShapeDtypeStruct((total, units), jnp.bfloat16),
+        scratch_shapes=[pltpu.VMEM((total, 2 * units), jnp.float32)],
+        compiler_params=pltpu.CompilerParams(dimension_semantics=("arbitrary",)),
+        name="first_layer",
+    )(blocks, w_gate, w_up)
+
+
+def block(tokens, expert_ids, route_weight, w_gate, w_up, w_down):
     n_uly = lax.axis_size("uly")
     n_dp = lax.axis_size("dp")
     n_blk = lax.axis_size("blk")
@@ -69,18 +112,19 @@
     for j in range(STEPS):
         chunk = jnp.transpose(crossed[:, :, j, :], (1, 0, 2))
         arrived.append(move(chunk, shifts, j, 1, n_blk, n_dp))
-    mine = jnp.stack(arrived).reshape(rows, width)
+    mine = jnp.stack(arrived).reshape(rows, n_blk, part)
+    mine = jnp.transpose(mine, (1, 0, 2)).reshape(n_blk * rows, part)
     mine, w_down_full = lax.optimization_barrier((mine, w_down_full))
-    everyone = lax.all_gather(mine, "blk", axis=0, tiled=True)
-    gate = jnp.dot(everyone, w_gate[0], preferred_element_type=jnp.float32)
-    up = jnp.dot(everyone, w_up[0], preferred_element_type=jnp.float32)
-    hidden = (jax.nn.silu(gate) * up).astype(jnp.bfloat16)
+    everyone = lax.all_gather(mine, "blk", axis=1, tiled=True)
+    hidden = first_layer(everyone, w_gate[0], w_up[0], n_blk, rows)
     hidden = hidden.reshape(n_blk, rows, hidden.shape[1])
     hidden = lax.all_to_all(hidden, "blk", split_axis=0, concat_axis=0, tiled=True)
     hidden = jnp.transpose(hidden, (1, 0, 2)).reshape(rows, -1)
     answer = jnp.dot(hidden, w_down_full, preferred_element_type=jnp.float32).astype(jnp.bfloat16)
     answer = answer.reshape(STEPS, CAPACITY, n_uly, width)
-    back = [move(answer[j], shifts, j, -1, n_blk, n_dp) for j in range(STEPS)]
+    back = []
+    for j in range(STEPS):
+        back.append(move(answer[j], shifts, j, -1, n_blk, n_dp))
     back = jnp.transpose(jnp.stack(back), (2, 1, 0, 3))
     home = lax.all_to_all(back, "uly", split_axis=0, concat_axis=0, tiled=True).reshape(rows, width)
     mixed = jnp.dot(mixing.reshape(tokens_here, rows), home.astype(jnp.float32), precision=lax.Precision.HIGHEST)
@@ -91,7 +135,7 @@
 
 def solution(mesh):
     return jax.shard_map(
-        local,
+        block,
         mesh=mesh,
         in_specs=(
             P(("uly", "dp"), None),

time: 297 us -> 300 us (1.010)
  Pallas kernels: 0 us -> 7.55 us
  matrix products: 12.4 us -> 6.56 us
    pallas_call x0 -> x1, Pallas kernels: none -> 7.55 us  [first_layer(): pl.pallas_call(body, grid=(n_blk,), in_specs=[pl.BlockSpec((rows, n_blk *...]
    dot_general x6 -> x4, matrix products: 12.4 us -> 6.56 us  [the longest x1 5.02 us: block(): jnp.dot(hidden, w_down_full, preferred_element_type=jnp.float32)]
  transfers between devices with their start and end apart: 10 -> 10, of which waited for: 7 -> 7; matrix products, arithmetic and copies ran while one was open for 3% -> 2% of each run, Pallas kernels for 0% -> 0%
where the time goes in v5:
time: 300 us; the launch traced here: 296 us
  waiting for transfers between devices  129 us (43%)
  starting transfers between devices  75.1 us (25%)
  blocking collectives  55.3 us (18%)
  between operations  13.6 us (5%)
  Pallas kernels  7.55 us (3%)
  matrix products  6.56 us (2%)
  local copies, waits for them, and re-layouts  5.24 us (2%)
  other arithmetic  3.47 us (1%)
    ppermute x8, waiting for transfers between devices, move(): return lax.ppermute(value, ('blk', 'dp'), pairs)  75.6 us
    ppermute x8, starting transfers between devices, move(): return lax.ppermute(value, ('blk', 'dp'), pairs)  75.1 us
    all_gather x1, waiting for transfers between devices, block(): everyone = lax.all_gather(mine, 'blk', axis=1, tiled=True)  53 us
    all_to_all x1, blocking collectives, block(): lax.all_to_all(jnp.transpose(mixed, (1, 0, 2)), 'blk', split_axis=0, conc...  21.6 us
    all_to_all x1, blocking collectives, block(): lax.all_to_all(outgoing, 'uly', split_axis=0, concat_axis=0, tiled=True)  13.9 us
    all_to_all x1, blocking collectives, block(): lax.all_to_all(back, 'uly', split_axis=0, concat_axis=0, tiled=True)  10.4 us
    all_to_all x1, blocking collectives, block(): lax.all_to_all(hidden, 'blk', split_axis=0, concat_axis=0, tiled=True)  9.42 us
    pallas_call x1, Pallas kernels, first_layer(): pl.pallas_call(body, grid=(n_blk,), in_specs=[pl.BlockSpec((rows, n_blk *...  7.55 us
  transfers between devices with their start and end apart: 10, of which 7 were waited for; matrix products, arithmetic and copies ran while one was open for 2% of the time, Pallas kernels for 0%

profile of v5, /device:TPU:25, one launch (start us, length us, event | category | flops | bytes accessed | tf_op | source)
XLA Modules:
  0.0 296.1 jit_solution(15882926044713349450)
XLA Ops:
  6.5 0.0 copy-start
  6.5 0.0 all-gather.6.cloned.1.call-start
  6.5 0.7 all-gather.6.cloned.1.call-update
  7.3 0.0 all-gather.4.cloned.1.call-start
  7.3 0.7 fusion.14
  8.0 0.1 broadcast_add_fusion
  8.1 0.1 add.47
  8.2 0.1 eq.47
  8.3 0.8 fusion.4
  9.1 0.1 fusion.7
  9.3 0.0 copy-done
  9.3 0.4 convolution_convert_fusion.1
  9.6 0.2 reshape.67
  9.9 13.9 %all_to_all.20 = bf16[4,5,4,4096]{3,2,1,0:T(4,128)(2,1)S(1)} all-to-all(bf16[4,5,4,4096]{3,2,1,0:T(4,128)(2,1)S(1)} %reshape.67), channel_id=1, replica_groups=mesh['blk'=8,'uly'=4,'dp'=32] {'uly'}, dimensions={0} | all-to-all | bytes 1310720 | tf_op jit(solution)/shard_map/all_to_all | solution.py:110
  23.7 1.4 fusion.19
  25.2 0.2 copy.89
  25.4 0.2 copy.88
  25.6 0.2 copy.90
  25.9 0.2 copy.87
  26.1 21.3 %collective-permute-start.2 = (bf16[5,4,4096]{2,1,0:T(4,128)(2,1)S(1)}, bf16[5,4,4096]{2,1,0:T(4,128)(2,1)S(1)}, u32[]{:S(2)}, u32[]{:S(2)}) collective-permute-start(bf16[5,4,4096]{2,1,0:T(4,128)(2,1)S(1)} %bitcast.93), channel_id=1, source_target_pairs={{0,8},{1,9},{2,10},{3,11},{4,12},{5,13},{6,14},{7,15},{8,16},{9,17... | collective-permute-start | bytes 491528 | tf_op jit(solution)/shard_map/ppermute | solution.py:34
  47.4 5.2 %collective-permute-start.3 = (bf16[5,4,4096]{2,1,0:T(4,128)(2,1)S(1)}, bf16[5,4,4096]{2,1,0:T(4,128)(2,1)S(1)}, u32[]{:S(2)}, u32[]{:S(2)}) collective-permute-start(bf16[5,4,4096]{2,1,0:T(4,128)(2,1)S(1)} %bitcast.92), channel_id=1, source_target_pairs={{0,1},{1,2},{2,3},{3,4},{4,5},{5,6},{6,7},{7,8},{8,9},{9,10},{10,1... | collective-permute-start | bytes 491528 | tf_op jit(solution)/shard_map/ppermute | solution.py:34
  52.7 6.2 %collective-permute-start.1 = (bf16[5,4,4096]{2,1,0:T(4,128)(2,1)S(1)}, bf16[5,4,4096]{2,1,0:T(4,128)(2,1)S(1)}, u32[]{:S(2)}, u32[]{:S(2)}) collective-permute-start(bf16[5,4,4096]{2,1,0:T(4,128)(2,1)S(1)} %bitcast.91), channel_id=1, source_target_pairs={{0,9},{1,10},{2,11},{3,12},{4,13},{5,14},{6,15},{7,16},{8,17},{9,1... | collective-permute-start | bytes 491528 | tf_op jit(solution)/shard_map/ppermute | solution.py:34
  58.9 11.8 %collective-permute-start = (bf16[5,4,4096]{2,1,0:T(4,128)(2,1)S(1)}, bf16[5,4,4096]{2,1,0:T(4,128)(2,1)S(1)}, u32[]{:S(2)}, u32[]{:S(2)}) collective-permute-start(bf16[5,4,4096]{2,1,0:T(4,128)(2,1)S(1)} %bitcast.90), channel_id=1, source_target_pairs={{0,16},{1,17},{2,18},{3,19},{4,20},{5,21},{6,22},{7,23},{8,24},{9,... | collective-permute-start | bytes 491528 | tf_op jit(solution)/shard_map/ppermute | solution.py:34
  70.7 0.0 collective-permute-done.2
  70.7 24.3 %collective-permute-done.3 = bf16[5,4,4096]{2,1,0:T(4,128)(2,1)S(1)} collective-permute-done((bf16[5,4,4096]{2,1,0:T(4,128)(2,1)S(1)}, bf16[5,4,4096]{2,1,0:T(4,128)(2,1)S(1)}, u32[]{:S(2)}, u32[]{:S(2)}) %collective-permute-start.3) | collective-permute-done | bytes 163872 | tf_op jit(solution)/shard_map/ppermute | solution.py:34
  95.0 4.4 %collective-permute-done.1 = bf16[5,4,4096]{2,1,0:T(4,128)(2,1)S(1)} collective-permute-done((bf16[5,4,4096]{2,1,0:T(4,128)(2,1)S(1)}, bf16[5,4,4096]{2,1,0:T(4,128)(2,1)S(1)}, u32[]{:S(2)}, u32[]{:S(2)}) %collective-permute-start.1) | collective-permute-done | bytes 163872 | tf_op jit(solution)/shard_map/ppermute | solution.py:34
  99.4 4.0 %collective-permute-done = bf16[5,4,4096]{2,1,0:T(4,128)(2,1)S(1)} collective-permute-done((bf16[5,4,4096]{2,1,0:T(4,128)(2,1)S(1)}, bf16[5,4,4096]{2,1,0:T(4,128)(2,1)S(1)}, u32[]{:S(2)}, u32[]{:S(2)}) %collective-permute-start) | collective-permute-done | bytes 163872 | tf_op jit(solution)/shard_map/ppermute | solution.py:34
  103.4 0.6 pad_maximum_fusion
  104.0 0.5 reshape.68
  104.5 1.0 copy.67
  105.5 0.0 all-gather.6.cloned.1.call-done
  105.5 0.0 all-gather.4.cloned.1.call-update
  105.6 53.0 %all-gather.4.cloned.1.call-done.x_ref = bf16[640,4096]{1,0:T(8,128)(2,1)} async-done(((bf16[640,512]{1,0:T(8,128)(2,1)}), bf16[640,4096]{1,0:T(8,128)(2,1)}) %all-gather.4.cloned.1.call-update) | async-done | bytes 5242896 | tf_op jit(solution)/shard_map/all_gather | solution.py:118
  158.5 7.6 %first_layer.1 = bf16[640,128]{1,0:T(8,128)(2,1)} custom-call(bf16[640,4096]{1,0:T(8,128)(2,1)} %all-gather.4.cloned.1.call-done.x_ref, bf16[4096,128]{1,0:T(8,128)(2,1)} %bitcast.77, bf16[4096,128]{1,0:T(8,128)(2,1)} %bitcast.78), custom_call_target="tpu_custom_call" | custom-call | tf_op jit(solution)/shard_map/first_layer/pallas_call | solution.py:62
  166.1 9.4 %all_to_all.21 = bf16[8,80,128]{2,1,0:T(8,128)(2,1)S(1)} all-to-all(bf16[8,80,128]{2,1,0:T(8,128)(2,1)} %bitcast.79), channel_id=1, replica_groups=mesh['blk'=8,'uly'=4,'dp'=32] {'blk'}, dimensions={0} | all-to-all | bytes 327680 | tf_op jit(solution)/shard_map/all_to_all | solution.py:121
  175.5 5.0 %convolution_convert_fusion = bf16[80,4096]{1,0:T(8,128)(2,1)S(1)} fusion(bf16[1024,4096]{1,0:T(8,128)(2,1)} %bitcast.73, bf16[8,80,128]{2,1,0:T(8,128)(2,1)S(1)} %all_to_all.21), kind=kOutput, calls=%fused_computation.1 | convolution fusion | flops 671416320 | bytes 9207808 | tf_op jit(solution)/shard_map/dot_general | solution.py:123
  180.5 0.1 fusion.18
  180.6 0.1 squeeze.41
  180.7 0.1 squeeze.44
  180.8 0.1 squeeze.43
  180.9 0.1 squeeze.42
  180.9 17.7 %collective-permute-start.5 = (bf16[5,4,4096]{2,1,0:T(4,128)(2,1)S(1)}, bf16[5,4,4096]{2,1,0:T(4,128)(2,1)S(1)}, u32[]{:S(2)}, u32[]{:S(2)}) collective-permute-start(bf16[5,4,4096]{2,1,0:T(4,128)(2,1)S(1)} %squeeze.42), channel_id=1, source_target_pairs={{0,23},{1,24},{2,25},{3,26},{4,27},{5,28},{6,29},{7,30},{8,31},{9,... | collective-permute-start | bytes 491528 | tf_op jit(solution)/shard_map/ppermute | solution.py:34
  198.7 7.5 %collective-permute-start.6 = (bf16[5,4,4096]{2,1,0:T(4,128)(2,1)S(1)}, bf16[5,4,4096]{2,1,0:T(4,128)(2,1)S(1)}, u32[]{:S(2)}, u32[]{:S(2)}) collective-permute-start(bf16[5,4,4096]{2,1,0:T(4,128)(2,1)S(1)} %squeeze.43), channel_id=1, source_target_pairs={{0,24},{1,25},{2,26},{3,27},{4,28},{5,29},{6,30},{7,31},{8,0},{9,1... | collective-permute-start | bytes 491528 | tf_op jit(solution)/shard_map/ppermute | solution.py:34
  206.1 2.6 collective-permute-start.7
  208.7 2.7 collective-permute-start.4
  211.4 0.0 collective-permute-done.5
  211.4 20.9 %collective-permute-done.6 = bf16[5,4,4096]{2,1,0:T(4,128)(2,1)S(1)} collective-permute-done((bf16[5,4,4096]{2,1,0:T(4,128)(2,1)S(1)}, bf16[5,4,4096]{2,1,0:T(4,128)(2,1)S(1)}, u32[]{:S(2)}, u32[]{:S(2)}) %collective-permute-start.6) | collective-permute-done | bytes 163872 | tf_op jit(solution)/shard_map/ppermute | solution.py:34
  232.3 2.7 collective-permute-done.7
  235.0 19.4 %collective-permute-done.4 = bf16[5,4,4096]{2,1,0:T(4,128)(2,1)S(1)} collective-permute-done((bf16[5,4,4096]{2,1,0:T(4,128)(2,1)S(1)}, bf16[5,4,4096]{2,1,0:T(4,128)(2,1)S(1)}, u32[]{:S(2)}, u32[]{:S(2)}) %collective-permute-start.4) | collective-permute-done | bytes 163872 | tf_op jit(solution)/shard_map/ppermute | solution.py:34
  254.4 0.6 maximum_bitcast_fusion
  255.0 0.5 copy.69
  255.5 10.4 %all_to_all.22 = bf16[4,5,4,4096]{3,2,1,0:T(4,128)(2,1)S(1)} all-to-all(bf16[4,5,4,4096]{3,2,1,0:T(4,128)(2,1)S(1)} %copy.69), channel_id=1, replica_groups=mesh['blk'=8,'uly'=4,'dp'=32] {'uly'}, dimensions={0} | all-to-all | bytes 1310720 | tf_op jit(solution)/shard_map/all_to_all | solution.py:129
  265.9 1.1 fusion
  267.0 21.6 %all_to_all.23 = bf16[8,64,512]{2,1,0:T(8,128)(2,1)S(1)} all-to-all(bf16[8,64,512]{2,1,0:T(8,128)(2,1)S(1)} %bitcast.76), channel_id=1, replica_groups=mesh['blk'=8,'uly'=4,'dp'=32] {'blk'}, dimensions={0} | all-to-all | bytes 1048576 | tf_op jit(solution)/shard_map/all_to_all | solution.py:132
  288.6 0.7 reduce_sum.32
  (5 shorter events, 0.1 us)
Async XLA Ops:
  6.5 2.7 copy-start
  6.5 99.0 %all-gather.6.cloned.1.call-start = ((), (), s32[]{:S(2)}) async-start(), calls=%async_computation.5 | async-start | bytes 9437184 | tf_op jit(solution)/shard_map/all_gather | solution.py:88
  7.3 151.3 %all-gather.4.cloned.1.call-start = ((), (), s32[]{:S(2)}) async-start(), calls=%async_computation.4 | async-start | bytes 5898240 | tf_op jit(solution)/shard_map/all_gather | solution.py:118
  26.1 44.6 %collective-permute-start.2 = (bf16[5,4,4096]{2,1,0:T(4,128)(2,1)S(1)}, bf16[5,4,4096]{2,1,0:T(4,128)(2,1)S(1)}, u32[]{:S(2)}, u32[]{:S(2)}) collective-permute-start(bf16[5,4,4096]{2,1,0:T(4,128)(2,1)S(1)} %bitcast.93), channel_id=1, source_target_pairs={{0,8},{1,9},{2,10},{3,11},{4,12},{5,13},{6,14},{7,15},{8,16},{9,17... | collective-permute-start | bytes 491528 | tf_op jit(solution)/shard_map/ppermute | solution.py:34
  47.4 47.6 %collective-permute-start.3 = (bf16[5,4,4096]{2,1,0:T(4,128)(2,1)S(1)}, bf16[5,4,4096]{2,1,0:T(4,128)(2,1)S(1)}, u32[]{:S(2)}, u32[]{:S(2)}) collective-permute-start(bf16[5,4,4096]{2,1,0:T(4,128)(2,1)S(1)} %bitcast.92), channel_id=1, source_target_pairs={{0,1},{1,2},{2,3},{3,4},{4,5},{5,6},{6,7},{7,8},{8,9},{9,10},{10,1... | collective-permute-start | bytes 491528 | tf_op jit(solution)/shard_map/ppermute | solution.py:34
  52.7 46.7 %collective-permute-start.1 = (bf16[5,4,4096]{2,1,0:T(4,128)(2,1)S(1)}, bf16[5,4,4096]{2,1,0:T(4,128)(2,1)S(1)}, u32[]{:S(2)}, u32[]{:S(2)}) collective-permute-start(bf16[5,4,4096]{2,1,0:T(4,128)(2,1)S(1)} %bitcast.91), channel_id=1, source_target_pairs={{0,9},{1,10},{2,11},{3,12},{4,13},{5,14},{6,15},{7,16},{8,17},{9,1... | collective-permute-start | bytes 491528 | tf_op jit(solution)/shard_map/ppermute | solution.py:34
  58.9 44.5 %collective-permute-start = (bf16[5,4,4096]{2,1,0:T(4,128)(2,1)S(1)}, bf16[5,4,4096]{2,1,0:T(4,128)(2,1)S(1)}, u32[]{:S(2)}, u32[]{:S(2)}) collective-permute-start(bf16[5,4,4096]{2,1,0:T(4,128)(2,1)S(1)} %bitcast.90), channel_id=1, source_target_pairs={{0,16},{1,17},{2,18},{3,19},{4,20},{5,21},{6,22},{7,23},{8,24},{9,... | collective-permute-start | bytes 491528 | tf_op jit(solution)/shard_map/ppermute | solution.py:34
  180.9 30.5 %collective-permute-start.5 = (bf16[5,4,4096]{2,1,0:T(4,128)(2,1)S(1)}, bf16[5,4,4096]{2,1,0:T(4,128)(2,1)S(1)}, u32[]{:S(2)}, u32[]{:S(2)}) collective-permute-start(bf16[5,4,4096]{2,1,0:T(4,128)(2,1)S(1)} %squeeze.42), channel_id=1, source_target_pairs={{0,23},{1,24},{2,25},{3,26},{4,27},{5,28},{6,29},{7,30},{8,31},{9,... | collective-permute-start | bytes 491528 | tf_op jit(solution)/shard_map/ppermute | solution.py:34
  198.7 33.7 %collective-permute-start.6 = (bf16[5,4,4096]{2,1,0:T(4,128)(2,1)S(1)}, bf16[5,4,4096]{2,1,0:T(4,128)(2,1)S(1)}, u32[]{:S(2)}, u32[]{:S(2)}) collective-permute-start(bf16[5,4,4096]{2,1,0:T(4,128)(2,1)S(1)} %squeeze.43), channel_id=1, source_target_pairs={{0,24},{1,25},{2,26},{3,27},{4,28},{5,29},{6,30},{7,31},{8,0},{9,1... | collective-permute-start | bytes 491528 | tf_op jit(solution)/shard_map/ppermute | solution.py:34
  206.1 28.9 %collective-permute-start.7 = (bf16[5,4,4096]{2,1,0:T(4,128)(2,1)S(1)}, bf16[5,4,4096]{2,1,0:T(4,128)(2,1)S(1)}, u32[]{:S(2)}, u32[]{:S(2)}) collective-permute-start(bf16[5,4,4096]{2,1,0:T(4,128)(2,1)S(1)} %squeeze.44), channel_id=1, source_target_pairs={{0,31},{1,0},{2,1},{3,2},{4,3},{5,4},{6,5},{7,6},{8,7},{9,8},{10,9... | collective-permute-start | bytes 491528 | tf_op jit(solution)/shard_map/ppermute | solution.py:34
  208.7 45.7 %collective-permute-start.4 = (bf16[5,4,4096]{2,1,0:T(4,128)(2,1)S(1)}, bf16[5,4,4096]{2,1,0:T(4,128)(2,1)S(1)}, u32[]{:S(2)}, u32[]{:S(2)}) collective-permute-start(bf16[5,4,4096]{2,1,0:T(4,128)(2,1)S(1)} %squeeze.41), channel_id=1, source_target_pairs={{0,16},{1,17},{2,18},{3,19},{4,20},{5,21},{6,22},{7,23},{8,24},{9,... | collective-permute-start | bytes 491528 | tf_op jit(solution)/shard_map/ppermute | solution.py:34
Sparse Core Ops, SparseCore 0:
  10.1 73.2 all-gather.5
  105.7 52.8 all-gather.3

commit v6 on v2

--- a/solution.py
+++ b/solution.py
@@ -44,6 +44,18 @@
 
     w_down_full = lax.all_gather(w_down[0], "blk", axis=0, tiled=True)
 
+    same_core = [[2 * y + c for y in range(n_blk // 2)] for c in range(2)]
+
+    def for_chip(weights):
+        other = lax.ppermute(weights, "blk", [(n, n ^ 1) for n in range(n_blk)])
+        first = lax.bitwise_and(b, 1) == 0
+        low = jnp.where(first, weights, other)
+        high = jnp.where(first, other, weights)
+        return jnp.concatenate([low, high], axis=1)
+
+    chip_gate = for_chip(w_gate[0])
+    chip_up = for_chip(w_up[0])
+
     own_shifts = lax.dynamic_slice_in_dim(jnp.asarray(shifts), b, 1, 0)[0]
     z_of = (z + own_shifts) % n_dp
     experts = (jnp.arange(n_uly, dtype=jnp.int32)[:, None] * n_dp + z_of[None, :]).reshape(-1)
@@ -71,12 +83,14 @@
         arrived.append(move(chunk, shifts, j, 1, n_blk, n_dp))
     mine = jnp.stack(arrived).reshape(rows, width)
     mine, w_down_full = lax.optimization_barrier((mine, w_down_full))
-    everyone = lax.all_gather(mine, "blk", axis=0, tiled=True)
-    gate = jnp.dot(everyone, w_gate[0], preferred_element_type=jnp.float32)
-    up = jnp.dot(everyone, w_up[0], preferred_element_type=jnp.float32)
+    everyone = lax.all_gather(mine, "blk", axis=0, tiled=True, axis_index_groups=same_core)
+    gate = jnp.dot(everyone, chip_gate, preferred_element_type=jnp.float32)
+    up = jnp.dot(everyone, chip_up, preferred_element_type=jnp.float32)
     hidden = (jax.nn.silu(gate) * up).astype(jnp.bfloat16)
-    hidden = hidden.reshape(n_blk, rows, hidden.shape[1])
-    hidden = lax.all_to_all(hidden, "blk", split_axis=0, concat_axis=0, tiled=True)
+    hidden = hidden.reshape(n_blk // 2, rows, hidden.shape[1])
+    hidden = lax.all_to_all(
+        hidden, "blk", split_axis=0, concat_axis=0, tiled=True, axis_index_groups=same_core
+    )
     hidden = jnp.transpose(hidden, (1, 0, 2)).reshape(rows, -1)
     answer = jnp.dot(hidden, w_down_full, preferred_element_type=jnp.float32).astype(jnp.bfloat16)
     answer = answer.reshape(STEPS, CAPACITY, n_uly, width)

time: 297 us -> 297 us (level)
  waiting for transfers between devices: 129 us -> 121 us
  other arithmetic: 3.47 us -> 9 us
  starting transfers between devices: 75.1 us -> 79.6 us
  matrix products: 12.4 us -> 8.9 us
    all_gather x1, waiting for transfers between devices: 53.3 us -> 34.3 us  [local(): lax.all_gather(mine, 'blk', axis=0, tiled=True, axis_index_groups=same_core)]
    ppermute x8, waiting for transfers between devices: 74.9 us -> 86.1 us  [move(): return lax.ppermute(value, ('blk', 'dp'), pairs)]
    select_n x0 -> x2, other arithmetic: none -> 5.53 us  [for_chip(): low = jnp.where(first, weights, other)]
    ppermute x0 -> x2, starting transfers between devices: none -> 4.33 us  [for_chip(): other = lax.ppermute(weights, 'blk', [(n, n ^ 1) for n in range(n_blk)])]
  transfers between devices with their start and end apart: 10 -> 12, of which waited for: 7 -> 9; matrix products, arithmetic and copies ran while one was open for 3% -> 4% of each run, Pallas kernels for 0% -> 0%
where the time goes in v6:
time: 297 us; the launch traced here: 293 us
  waiting for transfers between devices  121 us (41%)
  starting transfers between devices  79.6 us (27%)
  blocking collectives  55.9 us (19%)
  between operations  13.7 us (5%)
  other arithmetic  9 us (3%)
  matrix products  8.9 us (3%)
  local copies, waits for them, and re-layouts  4.78 us (2%)
    ppermute x8, waiting for transfers between devices, move(): return lax.ppermute(value, ('blk', 'dp'), pairs)  86.1 us
    ppermute x8, starting transfers between devices, move(): return lax.ppermute(value, ('blk', 'dp'), pairs)  75.3 us
    all_gather x1, waiting for transfers between devices, local(): lax.all_gather(mine, 'blk', axis=0, tiled=True, axis_index_groups=same_core)  34.3 us
    all_to_all x1, blocking collectives, local(): lax.all_to_all(jnp.transpose(mixed, (1, 0, 2)), 'blk', split_axis=0, conc...  22.7 us
    all_to_all x1, blocking collectives, local(): lax.all_to_all(outgoing, 'uly', split_axis=0, concat_axis=0, tiled=True)  13.8 us
    all_to_all x1, blocking collectives, local(): lax.all_to_all(back, 'uly', split_axis=0, concat_axis=0, tiled=True)  11.3 us
    all_to_all x1, blocking collectives, local(): lax.all_to_all(hidden, 'blk', split_axis=0, concat_axis=0, tiled=True, ax...  7.97 us
  transfers between devices with their start and end apart: 12, of which 9 were waited for; matrix products, arithmetic and copies ran while one was open for 4% of the time, Pallas kernels for 0%

profile of v6, /device:TPU:25, one launch (start us, length us, event | category | flops | bytes accessed | tf_op | source)
XLA Modules:
  0.0 293.3 jit_solution(12646586969759213318)
XLA Ops:
  6.5 0.0 copy-start
  6.5 0.7 all-gather.6.cloned.1.call-update
  7.3 0.0 all-gather.4.cloned.1.call-start
  7.3 0.7 fusion.20
  8.0 0.1 broadcast_add_fusion
  8.1 0.1 add.51
  8.2 0.1 eq.51
  8.3 0.8 fusion.10
  9.1 0.1 fusion.13
  9.3 0.4 convolution_convert_fusion.1
  9.6 0.2 reshape.64
  9.9 13.8 %all_to_all.20 = bf16[4,5,4,4096]{3,2,1,0:T(4,128)(2,1)S(1)} all-to-all(bf16[4,5,4,4096]{3,2,1,0:T(4,128)(2,1)S(1)} %reshape.64), channel_id=1, replica_groups=mesh['blk'=8,'uly'=4,'dp'=32] {'uly'}, dimensions={0} | all-to-all | bytes 1310720 | tf_op jit(solution)/shard_map/all_to_all | solution.py:79
  23.7 1.4 fusion.29
  25.2 0.0 copy-start.1
  25.2 0.0 copy-start.2
  25.2 0.2 copy.80
  25.4 27.5 %collective-permute-start = (bf16[5,4,4096]{2,1,0:T(4,128)(2,1)S(1)}, bf16[5,4,4096]{2,1,0:T(4,128)(2,1)S(1)}, u32[]{:S(2)}, u32[]{:S(2)}) collective-permute-start(bf16[5,4,4096]{2,1,0:T(4,128)(2,1)S(1)} %bitcast.92), channel_id=1, source_target_pairs={{0,16},{1,17},{2,18},{3,19},{4,20},{5,21},{6,22},{7,23},{8,24},{9,... | collective-permute-start | bytes 491528 | tf_op jit(solution)/shard_map/ppermute | solution.py:32
  52.9 0.2 copy.79
  53.2 1.9 collective-permute-start.1
  55.1 0.2 copy.78
  55.3 3.0 %collective-permute-start.2 = (bf16[5,4,4096]{2,1,0:T(4,128)(2,1)S(1)}, bf16[5,4,4096]{2,1,0:T(4,128)(2,1)S(1)}, u32[]{:S(2)}, u32[]{:S(2)}) collective-permute-start(bf16[5,4,4096]{2,1,0:T(4,128)(2,1)S(1)} %bitcast.94), channel_id=1, source_target_pairs={{0,8},{1,9},{2,10},{3,11},{4,12},{5,13},{6,14},{7,15},{8,16},{9,17... | collective-permute-start | bytes 491528 | tf_op jit(solution)/shard_map/ppermute | solution.py:32
  58.4 0.2 copy.81
  58.6 12.3 %collective-permute-start.3 = (bf16[5,4,4096]{2,1,0:T(4,128)(2,1)S(1)}, bf16[5,4,4096]{2,1,0:T(4,128)(2,1)S(1)}, u32[]{:S(2)}, u32[]{:S(2)}) collective-permute-start(bf16[5,4,4096]{2,1,0:T(4,128)(2,1)S(1)} %bitcast.95), channel_id=1, source_target_pairs={{0,1},{1,2},{2,3},{3,4},{4,5},{5,6},{6,7},{7,8},{8,9},{9,10},{10,1... | collective-permute-start | bytes 491528 | tf_op jit(solution)/shard_map/ppermute | solution.py:32
  70.9 14.0 %collective-permute-done = bf16[5,4,4096]{2,1,0:T(4,128)(2,1)S(1)} collective-permute-done((bf16[5,4,4096]{2,1,0:T(4,128)(2,1)S(1)}, bf16[5,4,4096]{2,1,0:T(4,128)(2,1)S(1)}, u32[]{:S(2)}, u32[]{:S(2)}) %collective-permute-start) | collective-permute-done | bytes 163872 | tf_op jit(solution)/shard_map/ppermute | solution.py:32
  84.9 9.2 %collective-permute-done.1 = bf16[5,4,4096]{2,1,0:T(4,128)(2,1)S(1)} collective-permute-done((bf16[5,4,4096]{2,1,0:T(4,128)(2,1)S(1)}, bf16[5,4,4096]{2,1,0:T(4,128)(2,1)S(1)}, u32[]{:S(2)}, u32[]{:S(2)}) %collective-permute-start.1) | collective-permute-done | bytes 163872 | tf_op jit(solution)/shard_map/ppermute | solution.py:32
  94.1 12.2 %collective-permute-done.2 = bf16[5,4,4096]{2,1,0:T(4,128)(2,1)S(1)} collective-permute-done((bf16[5,4,4096]{2,1,0:T(4,128)(2,1)S(1)}, bf16[5,4,4096]{2,1,0:T(4,128)(2,1)S(1)}, u32[]{:S(2)}, u32[]{:S(2)}) %collective-permute-start.2) | collective-permute-done | bytes 163872 | tf_op jit(solution)/shard_map/ppermute | solution.py:32
  106.3 6.4 %collective-permute-done.3 = bf16[5,4,4096]{2,1,0:T(4,128)(2,1)S(1)} collective-permute-done((bf16[5,4,4096]{2,1,0:T(4,128)(2,1)S(1)}, bf16[5,4,4096]{2,1,0:T(4,128)(2,1)S(1)}, u32[]{:S(2)}, u32[]{:S(2)}) %collective-permute-start.3) | collective-permute-done | bytes 163872 | tf_op jit(solution)/shard_map/ppermute | solution.py:32
  112.7 0.6 pad_maximum_fusion
  113.3 1.0 reshape.65
  114.3 0.0 all-gather.4.cloned.1.call-update
  114.3 1.9 collective-permute-start.4
  116.3 2.4 collective-permute-start.5
  118.7 0.3 collective-permute-done.4
  119.0 2.8 broadcast_select_fusion.3
  121.8 0.0 collective-permute-done.5
  121.8 2.8 broadcast_select_fusion.1
  124.6 34.3 %all-gather.4.cloned.1.call-done = bf16[320,4096]{1,0:T(8,128)(2,1)} async-done(((bf16[80,4096]{1,0:T(8,128)(2,1)}), bf16[320,4096]{1,0:T(8,128)(2,1)}) %all-gather.4.cloned.1.call-update) | async-done | bytes 2621456 | tf_op jit(solution)/shard_map/all_gather | solution.py:86
  158.9 0.0 copy-done.3
  158.9 3.0 %fusion.1 = f32[320,256]{1,0:T(8,128)S(1)} fusion(bf16[320,4096]{1,0:T(8,128)(2,1)} %all-gather.4.cloned.1.call-done, bf16[4096,128]{1,0:T(8,128)(2,1)} %get-tuple-element.14, bf16[4096,128]{1,0:T(8,128)(2,1)S(1)} %copy-done.3), kind=kOutput, calls=%fused_computation.4 | convolution fusion | flops 675282944 | bytes 5046272 | tf_op jit(solution)/shard_map/dot_general | solution.py:87
  161.9 0.0 slice-start.1
  161.9 2.8 multiply_convert_fusion
  164.7 8.0 %all_to_all.21 = bf16[4,80,256]{2,1,0:T(8,128)(2,1)S(1)} all-to-all(bf16[4,80,256]{2,1,0:T(8,128)(2,1)S(1)} %bitcast.91), channel_id=1, replica_groups={{0,256,512,768},{128,384,640,896},{1,257,513,769},{129,385,641,897},{2,..., dimensions={0} | all-to-all | bytes 327680 | tf_op jit(solution)/shard_map/all_to_all | solution.py:91
  172.7 0.0 slice-done
  172.7 0.0 slice-done.1
  172.7 1.6 convolution_convert_fusion
  174.3 0.1 fusion.28
  174.4 0.1 squeeze.41
  174.5 18.7 %collective-permute-start.6 = (bf16[5,4,4096]{2,1,0:T(4,128)(2,1)S(1)}, bf16[5,4,4096]{2,1,0:T(4,128)(2,1)S(1)}, u32[]{:S(2)}, u32[]{:S(2)}) collective-permute-start(bf16[5,4,4096]{2,1,0:T(4,128)(2,1)S(1)} %squeeze.41), channel_id=1, source_target_pairs={{0,16},{1,17},{2,18},{3,19},{4,20},{5,21},{6,22},{7,23},{8,24},{9,... | collective-permute-start | bytes 491528 | tf_op jit(solution)/shard_map/ppermute | solution.py:32
  193.2 0.1 squeeze.42
  193.3 7.2 %collective-permute-start.7 = (bf16[5,4,4096]{2,1,0:T(4,128)(2,1)S(1)}, bf16[5,4,4096]{2,1,0:T(4,128)(2,1)S(1)}, u32[]{:S(2)}, u32[]{:S(2)}) collective-permute-start(bf16[5,4,4096]{2,1,0:T(4,128)(2,1)S(1)} %squeeze.42), channel_id=1, source_target_pairs={{0,23},{1,24},{2,25},{3,26},{4,27},{5,28},{6,29},{7,30},{8,31},{9,... | collective-permute-start | bytes 491528 | tf_op jit(solution)/shard_map/ppermute | solution.py:32
  200.5 0.1 squeeze.43
  200.5 2.6 collective-permute-start.8
  203.2 0.1 squeeze.44
  203.3 1.9 collective-permute-start.9
  205.2 0.0 collective-permute-done.6
  205.2 20.2 %collective-permute-done.7 = bf16[5,4,4096]{2,1,0:T(4,128)(2,1)S(1)} collective-permute-done((bf16[5,4,4096]{2,1,0:T(4,128)(2,1)S(1)}, bf16[5,4,4096]{2,1,0:T(4,128)(2,1)S(1)}, u32[]{:S(2)}, u32[]{:S(2)}) %collective-permute-start.7) | collective-permute-done | bytes 163872 | tf_op jit(solution)/shard_map/ppermute | solution.py:32
  225.4 23.9 %collective-permute-done.8 = bf16[5,4,4096]{2,1,0:T(4,128)(2,1)S(1)} collective-permute-done((bf16[5,4,4096]{2,1,0:T(4,128)(2,1)S(1)}, bf16[5,4,4096]{2,1,0:T(4,128)(2,1)S(1)}, u32[]{:S(2)}, u32[]{:S(2)}) %collective-permute-start.8) | collective-permute-done | bytes 163872 | tf_op jit(solution)/shard_map/ppermute | solution.py:32
  249.2 0.3 collective-permute-done.9
  249.5 0.6 maximum_bitcast_fusion
  250.1 0.5 copy.64
  250.6 11.3 %all_to_all.22 = bf16[4,5,4,4096]{3,2,1,0:T(4,128)(2,1)S(1)} all-to-all(bf16[4,5,4,4096]{3,2,1,0:T(4,128)(2,1)S(1)} %copy.64), channel_id=1, replica_groups=mesh['blk'=8,'uly'=4,'dp'=32] {'uly'}, dimensions={0} | all-to-all | bytes 1310720 | tf_op jit(solution)/shard_map/all_to_all | solution.py:99
  261.9 1.1 fusion
  263.0 22.7 %all_to_all.23 = bf16[8,64,512]{2,1,0:T(8,128)(2,1)S(1)} all-to-all(bf16[8,64,512]{2,1,0:T(8,128)(2,1)S(1)} %bitcast.76), channel_id=1, replica_groups=mesh['blk'=8,'uly'=4,'dp'=32] {'blk'}, dimensions={0} | all-to-all | bytes 1048576 | tf_op jit(solution)/shard_map/all_to_all | solution.py:102
  285.8 0.7 reduce_sum.32
  (18 shorter events, 0.1 us)
Async XLA Ops:
  6.5 2.7 copy-start
  6.5 107.8 %all-gather.6.cloned.1.call-start = ((), (), s32[]{:S(2)}) async-start(), calls=%async_computation.5 | async-start | bytes 9437184 | tf_op jit(solution)/shard_map/all_gather | solution.py:45
  7.3 151.6 %all-gather.4.cloned.1.call-start = ((), (), s32[]{:S(2)}) async-start(), calls=%async_computation.4 | async-start | bytes 3276800 | tf_op jit(solution)/shard_map/all_gather | solution.py:86
  25.2 89.2 %copy-start.1 = (bf16[1,4096,128]{2,1,0:T(8,128)(2,1)S(1)}, bf16[1,4096,128]{2,1,0:T(8,128)(2,1)}, u32[]{:S(2)}) copy-start(bf16[1,4096,128]{2,1,0:T(8,128)(2,1)} %param.10) | copy-start | bytes 3145732
  25.2 91.1 %copy-start.2 = (bf16[1,4096,128]{2,1,0:T(8,128)(2,1)S(1)}, bf16[1,4096,128]{2,1,0:T(8,128)(2,1)}, u32[]{:S(2)}) copy-start(bf16[1,4096,128]{2,1,0:T(8,128)(2,1)} %param.11) | copy-start | bytes 3145732
  25.4 59.5 %collective-permute-start = (bf16[5,4,4096]{2,1,0:T(4,128)(2,1)S(1)}, bf16[5,4,4096]{2,1,0:T(4,128)(2,1)S(1)}, u32[]{:S(2)}, u32[]{:S(2)}) collective-permute-start(bf16[5,4,4096]{2,1,0:T(4,128)(2,1)S(1)} %bitcast.92), channel_id=1, source_target_pairs={{0,16},{1,17},{2,18},{3,19},{4,20},{5,21},{6,22},{7,23},{8,24},{9,... | collective-permute-start | bytes 491528 | tf_op jit(solution)/shard_map/ppermute | solution.py:32
  53.2 40.9 %collective-permute-start.1 = (bf16[5,4,4096]{2,1,0:T(4,128)(2,1)S(1)}, bf16[5,4,4096]{2,1,0:T(4,128)(2,1)S(1)}, u32[]{:S(2)}, u32[]{:S(2)}) collective-permute-start(bf16[5,4,4096]{2,1,0:T(4,128)(2,1)S(1)} %bitcast.93), channel_id=1, source_target_pairs={{0,9},{1,10},{2,11},{3,12},{4,13},{5,14},{6,15},{7,16},{8,17},{9,1... | collective-permute-start | bytes 491528 | tf_op jit(solution)/shard_map/ppermute | solution.py:32
  55.3 51.0 %collective-permute-start.2 = (bf16[5,4,4096]{2,1,0:T(4,128)(2,1)S(1)}, bf16[5,4,4096]{2,1,0:T(4,128)(2,1)S(1)}, u32[]{:S(2)}, u32[]{:S(2)}) collective-permute-start(bf16[5,4,4096]{2,1,0:T(4,128)(2,1)S(1)} %bitcast.94), channel_id=1, source_target_pairs={{0,8},{1,9},{2,10},{3,11},{4,12},{5,13},{6,14},{7,15},{8,16},{9,17... | collective-permute-start | bytes 491528 | tf_op jit(solution)/shard_map/ppermute | solution.py:32
  58.6 54.1 %collective-permute-start.3 = (bf16[5,4,4096]{2,1,0:T(4,128)(2,1)S(1)}, bf16[5,4,4096]{2,1,0:T(4,128)(2,1)S(1)}, u32[]{:S(2)}, u32[]{:S(2)}) collective-permute-start(bf16[5,4,4096]{2,1,0:T(4,128)(2,1)S(1)} %bitcast.95), channel_id=1, source_target_pairs={{0,1},{1,2},{2,3},{3,4},{4,5},{5,6},{6,7},{7,8},{8,9},{9,10},{10,1... | collective-permute-start | bytes 491528 | tf_op jit(solution)/shard_map/ppermute | solution.py:32
  114.3 4.7 %collective-permute-start.4 = (bf16[4096,128]{1,0:T(8,128)(2,1)S(1)}, bf16[4096,128]{1,0:T(8,128)(2,1)}, u32[]{:S(2)}, u32[]{:S(2)}) collective-permute-start(bf16[4096,128]{1,0:T(8,128)(2,1)S(1)} %bitcast.77), channel_id=1, source_target_pairs={{0,128},{128,0},{256,384},{384,256},{512,640},{640,512},{768,896},... | collective-permute-start | bytes 3145736 | tf_op jit(solution)/shard_map/ppermute | solution.py:50
  116.3 5.5 %collective-permute-start.5 = (bf16[4096,128]{1,0:T(8,128)(2,1)S(1)}, bf16[4096,128]{1,0:T(8,128)(2,1)}, u32[]{:S(2)}, u32[]{:S(2)}) collective-permute-start(bf16[4096,128]{1,0:T(8,128)(2,1)S(1)} %bitcast.78), channel_id=1, source_target_pairs={{0,128},{128,0},{256,384},{384,256},{512,640},{640,512},{768,896},... | collective-permute-start | bytes 3145736 | tf_op jit(solution)/shard_map/ppermute | solution.py:50
  121.8 37.1 %copy-start.3 = (bf16[4096,128]{1,0:T(8,128)(2,1)S(1)}, bf16[4096,128]{1,0:T(8,128)(2,1)}, u32[]{:S(2)}) copy-start(bf16[4096,128]{1,0:T(8,128)(2,1)} %get-tuple-element.13) | copy-start | bytes 3145732
  158.9 3.0 %copy-start.4 = (bf16[4096,128]{1,0:T(8,128)(2,1)S(1)}, bf16[4096,128]{1,0:T(8,128)(2,1)}, u32[]{:S(2)}) copy-start(bf16[4096,128]{1,0:T(8,128)(2,1)} %get-tuple-element.11) | copy-start | bytes 3145732
  158.9 3.0 %copy-start.5 = (bf16[4096,128]{1,0:T(8,128)(2,1)S(1)}, bf16[4096,128]{1,0:T(8,128)(2,1)}, u32[]{:S(2)}) copy-start(bf16[4096,128]{1,0:T(8,128)(2,1)} %get-tuple-element.12) | copy-start | bytes 3145732
  158.9 13.8 %slice-start = ((s8[8388608]{0:T(1024)(128)(4,1)}), s8[4194304]{0:T(1024)(128)(4,1)S(1)}, s32[]{:S(2)}) async-start(s8[8388608]{0:T(1024)(128)(4,1)} %bitcast.73), calls=%async_computation.6 | async-start | bytes 8388608
  161.9 10.8 %slice-start.1 = ((s8[8388608]{0:T(1024)(128)(4,1)}), s8[4194304]{0:T(1024)(128)(4,1)S(1)}, s32[]{:S(2)}) async-start(s8[8388608]{0:T(1024)(128)(4,1)} %bitcast.73), calls=%async_computation.7 | async-start | bytes 8388608
  174.5 30.7 %collective-permute-start.6 = (bf16[5,4,4096]{2,1,0:T(4,128)(2,1)S(1)}, bf16[5,4,4096]{2,1,0:T(4,128)(2,1)S(1)}, u32[]{:S(2)}, u32[]{:S(2)}) collective-permute-start(bf16[5,4,4096]{2,1,0:T(4,128)(2,1)S(1)} %squeeze.41), channel_id=1, source_target_pairs={{0,16},{1,17},{2,18},{3,19},{4,20},{5,21},{6,22},{7,23},{8,24},{9,... | collective-permute-start | bytes 491528 | tf_op jit(solution)/shard_map/ppermute | solution.py:32
  193.3 32.1 %collective-permute-start.7 = (bf16[5,4,4096]{2,1,0:T(4,128)(2,1)S(1)}, bf16[5,4,4096]{2,1,0:T(4,128)(2,1)S(1)}, u32[]{:S(2)}, u32[]{:S(2)}) collective-permute-start(bf16[5,4,4096]{2,1,0:T(4,128)(2,1)S(1)} %squeeze.42), channel_id=1, source_target_pairs={{0,23},{1,24},{2,25},{3,26},{4,27},{5,28},{6,29},{7,30},{8,31},{9,... | collective-permute-start | bytes 491528 | tf_op jit(solution)/shard_map/ppermute | solution.py:32
  200.5 48.7 %collective-permute-start.8 = (bf16[5,4,4096]{2,1,0:T(4,128)(2,1)S(1)}, bf16[5,4,4096]{2,1,0:T(4,128)(2,1)S(1)}, u32[]{:S(2)}, u32[]{:S(2)}) collective-permute-start(bf16[5,4,4096]{2,1,0:T(4,128)(2,1)S(1)} %squeeze.43), channel_id=1, source_target_pairs={{0,24},{1,25},{2,26},{3,27},{4,28},{5,29},{6,30},{7,31},{8,0},{9,1... | collective-permute-start | bytes 491528 | tf_op jit(solution)/shard_map/ppermute | solution.py:32
  203.3 46.2 %collective-permute-start.9 = (bf16[5,4,4096]{2,1,0:T(4,128)(2,1)S(1)}, bf16[5,4,4096]{2,1,0:T(4,128)(2,1)S(1)}, u32[]{:S(2)}, u32[]{:S(2)}) collective-permute-start(bf16[5,4,4096]{2,1,0:T(4,128)(2,1)S(1)} %squeeze.44), channel_id=1, source_target_pairs={{0,31},{1,0},{2,1},{3,2},{4,3},{5,4},{6,5},{7,6},{8,7},{9,8},{10,9... | collective-permute-start | bytes 491528 | tf_op jit(solution)/shard_map/ppermute | solution.py:32
Sparse Core Ops, SparseCore 0:
  10.1 73.2 all-gather.5
  114.4 44.3 all-gather.3

commit v7 on v6

--- a/solution.py
+++ b/solution.py
@@ -6,7 +6,7 @@
 
 CAPACITY = 5
 STEPS = 4
-DISTANCES = ((9, 8, 1), (15, 10, 7, 2), (14, 11, 6, 3), (13, 12, 5, 4))
+DISTANCES = ((13, 9, 2), (15, 12, 4, 1), (14, 10, 5, 3), (11, 8, 7, 6))
 
 
 def shift_table(n_blk, n_dp):
@@ -32,7 +32,7 @@
     return lax.ppermute(value, ("blk", "dp"), pairs)
 
 
-def local(tokens, expert_ids, route_weight, w_gate, w_up, w_down):
+def block(tokens, expert_ids, route_weight, w_gate, w_up, w_down):
     n_uly = lax.axis_size("uly")
     n_dp = lax.axis_size("dp")
     n_blk = lax.axis_size("blk")
@@ -94,7 +94,9 @@
     hidden = jnp.transpose(hidden, (1, 0, 2)).reshape(rows, -1)
     answer = jnp.dot(hidden, w_down_full, preferred_element_type=jnp.float32).astype(jnp.bfloat16)
     answer = answer.reshape(STEPS, CAPACITY, n_uly, width)
-    back = [move(answer[j], shifts, j, -1, n_blk, n_dp) for j in range(STEPS)]
+    back = []
+    for j in range(STEPS):
+        back.append(move(answer[j], shifts, j, -1, n_blk, n_dp))
     back = jnp.transpose(jnp.stack(back), (2, 1, 0, 3))
     home = lax.all_to_all(back, "uly", split_axis=0, concat_axis=0, tiled=True).reshape(rows, width)
     mixed = jnp.dot(mixing.reshape(tokens_here, rows), home.astype(jnp.float32), precision=lax.Precision.HIGHEST)
@@ -105,7 +107,7 @@
 
 def solution(mesh):
     return jax.shard_map(
-        local,
+        block,
         mesh=mesh,
         in_specs=(
             P(("uly", "dp"), None),

time: 297 us -> 292 us (0.983)
  starting transfers between devices: 79.6 us -> 68.9 us
  waiting for transfers between devices: 121 us -> 126 us
    ppermute x8, starting transfers between devices: 75.3 us -> 64.5 us  [move(): return lax.ppermute(value, ('blk', 'dp'), pairs)]
    ppermute x8, waiting for transfers between devices: 86.1 us -> 89.3 us  [move(): return lax.ppermute(value, ('blk', 'dp'), pairs)]
where the time goes in v7:
time: 292 us; the launch traced here: 289 us
  waiting for transfers between devices  126 us (43%)
  starting transfers between devices  68.9 us (24%)
  blocking collectives  57.3 us (20%)
  between operations  13.7 us (5%)
  other arithmetic  9 us (3%)
  matrix products  8.89 us (3%)
  local copies, waits for them, and re-layouts  4.78 us (2%)
    ppermute x8, waiting for transfers between devices, move(): return lax.ppermute(value, ('blk', 'dp'), pairs)  89.3 us
    ppermute x8, starting transfers between devices, move(): return lax.ppermute(value, ('blk', 'dp'), pairs)  64.5 us
    all_gather x1, waiting for transfers between devices, block(): lax.all_gather(mine, 'blk', axis=0, tiled=True, axis_index_groups=same_core)  35.9 us
    all_to_all x1, blocking collectives, block(): lax.all_to_all(jnp.transpose(mixed, (1, 0, 2)), 'blk', split_axis=0, conc...  24.1 us
    all_to_all x1, blocking collectives, block(): lax.all_to_all(outgoing, 'uly', split_axis=0, concat_axis=0, tiled=True)  13.8 us
    all_to_all x1, blocking collectives, block(): lax.all_to_all(back, 'uly', split_axis=0, concat_axis=0, tiled=True)  11.4 us
    all_to_all x1, blocking collectives, block(): lax.all_to_all(hidden, 'blk', split_axis=0, concat_axis=0, tiled=True, ax...  7.97 us
  transfers between devices with their start and end apart: 12, of which 9 were waited for; matrix products, arithmetic and copies ran while one was open for 4% of the time, Pallas kernels for 0%

profile of v7, /device:TPU:25, one launch (start us, length us, event | category | flops | bytes accessed | tf_op | source)
XLA Modules:
  0.0 288.9 jit_solution(1341878396714682499)
XLA Ops:
  6.5 0.0 copy-start
  6.5 0.0 all-gather.6.cloned.1.call-start
  6.5 0.7 all-gather.6.cloned.1.call-update
  7.3 0.0 all-gather.4.cloned.1.call-start
  7.3 0.7 fusion.20
  8.0 0.1 broadcast_add_fusion
  8.1 0.1 add.51
  8.2 0.1 eq.51
  8.3 0.8 fusion.10
  9.1 0.1 fusion.13
  9.3 0.4 convolution_convert_fusion.1
  9.6 0.2 reshape.64
  9.9 13.8 %all_to_all.20 = bf16[4,5,4,4096]{3,2,1,0:T(4,128)(2,1)S(1)} all-to-all(bf16[4,5,4,4096]{3,2,1,0:T(4,128)(2,1)S(1)} %reshape.64), channel_id=1, replica_groups=mesh['blk'=8,'uly'=4,'dp'=32] {'uly'}, dimensions={0} | all-to-all | bytes 1310720 | tf_op jit(solution)/shard_map/all_to_all | solution.py:79
  23.7 1.4 fusion.29
  25.2 0.0 copy-start.1
  25.2 0.0 copy-start.2
  25.2 0.2 copy.80
  25.4 25.4 %collective-permute-start = (bf16[5,4,4096]{2,1,0:T(4,128)(2,1)S(1)}, bf16[5,4,4096]{2,1,0:T(4,128)(2,1)S(1)}, u32[]{:S(2)}, u32[]{:S(2)}) collective-permute-start(bf16[5,4,4096]{2,1,0:T(4,128)(2,1)S(1)} %bitcast.92), channel_id=1, source_target_pairs={{0,16},{1,17},{2,18},{3,19},{4,20},{5,21},{6,22},{7,23},{8,24},{9,... | collective-permute-start | bytes 491528 | tf_op jit(solution)/shard_map/ppermute | solution.py:32
  50.8 0.2 copy.79
  51.0 4.3 %collective-permute-start.1 = (bf16[5,4,4096]{2,1,0:T(4,128)(2,1)S(1)}, bf16[5,4,4096]{2,1,0:T(4,128)(2,1)S(1)}, u32[]{:S(2)}, u32[]{:S(2)}) collective-permute-start(bf16[5,4,4096]{2,1,0:T(4,128)(2,1)S(1)} %bitcast.93), channel_id=1, source_target_pairs={{0,13},{1,14},{2,15},{3,16},{4,17},{5,18},{6,19},{7,20},{8,21},{9,... | collective-permute-start | bytes 491528 | tf_op jit(solution)/shard_map/ppermute | solution.py:32
  55.3 0.2 copy.78
  55.5 2.8 collective-permute-start.2
  58.4 0.2 copy.81
  58.6 1.9 collective-permute-start.3
  60.5 13.2 %collective-permute-done = bf16[5,4,4096]{2,1,0:T(4,128)(2,1)S(1)} collective-permute-done((bf16[5,4,4096]{2,1,0:T(4,128)(2,1)S(1)}, bf16[5,4,4096]{2,1,0:T(4,128)(2,1)S(1)}, u32[]{:S(2)}, u32[]{:S(2)}) %collective-permute-start) | collective-permute-done | bytes 163872 | tf_op jit(solution)/shard_map/ppermute | solution.py:32
  73.8 17.2 %collective-permute-done.1 = bf16[5,4,4096]{2,1,0:T(4,128)(2,1)S(1)} collective-permute-done((bf16[5,4,4096]{2,1,0:T(4,128)(2,1)S(1)}, bf16[5,4,4096]{2,1,0:T(4,128)(2,1)S(1)}, u32[]{:S(2)}, u32[]{:S(2)}) %collective-permute-start.1) | collective-permute-done | bytes 163872 | tf_op jit(solution)/shard_map/ppermute | solution.py:32
  90.9 11.4 %collective-permute-done.2 = bf16[5,4,4096]{2,1,0:T(4,128)(2,1)S(1)} collective-permute-done((bf16[5,4,4096]{2,1,0:T(4,128)(2,1)S(1)}, bf16[5,4,4096]{2,1,0:T(4,128)(2,1)S(1)}, u32[]{:S(2)}, u32[]{:S(2)}) %collective-permute-start.2) | collective-permute-done | bytes 163872 | tf_op jit(solution)/shard_map/ppermute | solution.py:32
  102.3 5.5 %collective-permute-done.3 = bf16[5,4,4096]{2,1,0:T(4,128)(2,1)S(1)} collective-permute-done((bf16[5,4,4096]{2,1,0:T(4,128)(2,1)S(1)}, bf16[5,4,4096]{2,1,0:T(4,128)(2,1)S(1)}, u32[]{:S(2)}, u32[]{:S(2)}) %collective-permute-start.3) | collective-permute-done | bytes 163872 | tf_op jit(solution)/shard_map/ppermute | solution.py:32
  107.8 0.6 pad_maximum_fusion
  108.4 1.0 reshape.65
  109.4 0.0 all-gather.4.cloned.1.call-update
  109.4 1.9 collective-permute-start.4
  111.4 2.4 collective-permute-start.5
  113.8 0.3 collective-permute-done.4
  114.1 2.8 broadcast_select_fusion.3
  116.9 0.0 collective-permute-done.5
  116.9 2.8 broadcast_select_fusion.1
  119.7 35.9 %all-gather.4.cloned.1.call-done = bf16[320,4096]{1,0:T(8,128)(2,1)} async-done(((bf16[80,4096]{1,0:T(8,128)(2,1)}), bf16[320,4096]{1,0:T(8,128)(2,1)}) %all-gather.4.cloned.1.call-update) | async-done | bytes 2621456 | tf_op jit(solution)/shard_map/all_gather | solution.py:86
  155.6 3.0 %fusion.1 = f32[320,256]{1,0:T(8,128)S(1)} fusion(bf16[320,4096]{1,0:T(8,128)(2,1)} %all-gather.4.cloned.1.call-done, bf16[4096,128]{1,0:T(8,128)(2,1)} %get-tuple-element.14, bf16[4096,128]{1,0:T(8,128)(2,1)S(1)} %copy-done.3), kind=kOutput, calls=%fused_computation.4 | convolution fusion | flops 675282944 | bytes 5046272 | tf_op jit(solution)/shard_map/dot_general | solution.py:87
  158.6 0.0 copy-done.4
  158.6 0.0 copy-done.5
  158.6 0.0 slice-start.1
  158.6 2.8 multiply_convert_fusion
  161.4 8.0 %all_to_all.21 = bf16[4,80,256]{2,1,0:T(8,128)(2,1)S(1)} all-to-all(bf16[4,80,256]{2,1,0:T(8,128)(2,1)S(1)} %bitcast.91), channel_id=1, replica_groups={{0,256,512,768},{128,384,640,896},{1,257,513,769},{129,385,641,897},{2,..., dimensions={0} | all-to-all | bytes 327680 | tf_op jit(solution)/shard_map/all_to_all | solution.py:91
  169.4 1.6 convolution_convert_fusion
  171.0 0.1 fusion.28
  171.1 0.1 squeeze.41
  171.2 15.5 %collective-permute-start.6 = (bf16[5,4,4096]{2,1,0:T(4,128)(2,1)S(1)}, bf16[5,4,4096]{2,1,0:T(4,128)(2,1)S(1)}, u32[]{:S(2)}, u32[]{:S(2)}) collective-permute-start(bf16[5,4,4096]{2,1,0:T(4,128)(2,1)S(1)} %squeeze.41), channel_id=1, source_target_pairs={{0,16},{1,17},{2,18},{3,19},{4,20},{5,21},{6,22},{7,23},{8,24},{9,... | collective-permute-start | bytes 491528 | tf_op jit(solution)/shard_map/ppermute | solution.py:32
  186.7 0.1 squeeze.42
  186.8 9.8 %collective-permute-start.7 = (bf16[5,4,4096]{2,1,0:T(4,128)(2,1)S(1)}, bf16[5,4,4096]{2,1,0:T(4,128)(2,1)S(1)}, u32[]{:S(2)}, u32[]{:S(2)}) collective-permute-start(bf16[5,4,4096]{2,1,0:T(4,128)(2,1)S(1)} %squeeze.42), channel_id=1, source_target_pairs={{0,19},{1,20},{2,21},{3,22},{4,23},{5,24},{6,25},{7,26},{8,27},{9,... | collective-permute-start | bytes 491528 | tf_op jit(solution)/shard_map/ppermute | solution.py:32
  196.6 0.1 squeeze.43
  196.7 2.8 collective-permute-start.8
  199.5 0.1 squeeze.44
  199.6 1.9 collective-permute-start.9
  201.5 0.0 collective-permute-done.6
  201.5 17.9 %collective-permute-done.7 = bf16[5,4,4096]{2,1,0:T(4,128)(2,1)S(1)} collective-permute-done((bf16[5,4,4096]{2,1,0:T(4,128)(2,1)S(1)}, bf16[5,4,4096]{2,1,0:T(4,128)(2,1)S(1)}, u32[]{:S(2)}, u32[]{:S(2)}) %collective-permute-start.7) | collective-permute-done | bytes 163872 | tf_op jit(solution)/shard_map/ppermute | solution.py:32
  219.5 18.3 %collective-permute-done.8 = bf16[5,4,4096]{2,1,0:T(4,128)(2,1)S(1)} collective-permute-done((bf16[5,4,4096]{2,1,0:T(4,128)(2,1)S(1)}, bf16[5,4,4096]{2,1,0:T(4,128)(2,1)S(1)}, u32[]{:S(2)}, u32[]{:S(2)}) %collective-permute-start.8) | collective-permute-done | bytes 163872 | tf_op jit(solution)/shard_map/ppermute | solution.py:32
  237.8 5.8 %collective-permute-done.9 = bf16[5,4,4096]{2,1,0:T(4,128)(2,1)S(1)} collective-permute-done((bf16[5,4,4096]{2,1,0:T(4,128)(2,1)S(1)}, bf16[5,4,4096]{2,1,0:T(4,128)(2,1)S(1)}, u32[]{:S(2)}, u32[]{:S(2)}) %collective-permute-start.9) | collective-permute-done | bytes 163872 | tf_op jit(solution)/shard_map/ppermute | solution.py:32
  243.6 0.6 maximum_bitcast_fusion
  244.2 0.5 copy.64
  244.7 11.4 %all_to_all.22 = bf16[4,5,4,4096]{3,2,1,0:T(4,128)(2,1)S(1)} all-to-all(bf16[4,5,4,4096]{3,2,1,0:T(4,128)(2,1)S(1)} %copy.64), channel_id=1, replica_groups=mesh['blk'=8,'uly'=4,'dp'=32] {'uly'}, dimensions={0} | all-to-all | bytes 1310720 | tf_op jit(solution)/shard_map/all_to_all | solution.py:101
  256.1 1.0 fusion
  257.2 24.1 %all_to_all.23 = bf16[8,64,512]{2,1,0:T(8,128)(2,1)S(1)} all-to-all(bf16[8,64,512]{2,1,0:T(8,128)(2,1)S(1)} %bitcast.76), channel_id=1, replica_groups=mesh['blk'=8,'uly'=4,'dp'=32] {'blk'}, dimensions={0} | all-to-all | bytes 1048576 | tf_op jit(solution)/shard_map/all_to_all | solution.py:104
  281.3 0.7 reduce_sum.32
  (18 shorter events, 0.1 us)
Async XLA Ops:
  6.5 2.7 copy-start
  6.5 102.9 %all-gather.6.cloned.1.call-start = ((), (), s32[]{:S(2)}) async-start(), calls=%async_computation.5 | async-start | bytes 9437184 | tf_op jit(solution)/shard_map/all_gather | solution.py:45
  7.3 148.3 %all-gather.4.cloned.1.call-start = ((), (), s32[]{:S(2)}) async-start(), calls=%async_computation.4 | async-start | bytes 3276800 | tf_op jit(solution)/shard_map/all_gather | solution.py:86
  25.2 84.3 %copy-start.1 = (bf16[1,4096,128]{2,1,0:T(8,128)(2,1)S(1)}, bf16[1,4096,128]{2,1,0:T(8,128)(2,1)}, u32[]{:S(2)}) copy-start(bf16[1,4096,128]{2,1,0:T(8,128)(2,1)} %param.10) | copy-start | bytes 3145732
  25.2 86.2 %copy-start.2 = (bf16[1,4096,128]{2,1,0:T(8,128)(2,1)S(1)}, bf16[1,4096,128]{2,1,0:T(8,128)(2,1)}, u32[]{:S(2)}) copy-start(bf16[1,4096,128]{2,1,0:T(8,128)(2,1)} %param.11) | copy-start | bytes 3145732
  25.4 48.4 %collective-permute-start = (bf16[5,4,4096]{2,1,0:T(4,128)(2,1)S(1)}, bf16[5,4,4096]{2,1,0:T(4,128)(2,1)S(1)}, u32[]{:S(2)}, u32[]{:S(2)}) collective-permute-start(bf16[5,4,4096]{2,1,0:T(4,128)(2,1)S(1)} %bitcast.92), channel_id=1, source_target_pairs={{0,16},{1,17},{2,18},{3,19},{4,20},{5,21},{6,22},{7,23},{8,24},{9,... | collective-permute-start | bytes 491528 | tf_op jit(solution)/shard_map/ppermute | solution.py:32
  51.0 39.9 %collective-permute-start.1 = (bf16[5,4,4096]{2,1,0:T(4,128)(2,1)S(1)}, bf16[5,4,4096]{2,1,0:T(4,128)(2,1)S(1)}, u32[]{:S(2)}, u32[]{:S(2)}) collective-permute-start(bf16[5,4,4096]{2,1,0:T(4,128)(2,1)S(1)} %bitcast.93), channel_id=1, source_target_pairs={{0,13},{1,14},{2,15},{3,16},{4,17},{5,18},{6,19},{7,20},{8,21},{9,... | collective-permute-start | bytes 491528 | tf_op jit(solution)/shard_map/ppermute | solution.py:32
  55.5 46.8 %collective-permute-start.2 = (bf16[5,4,4096]{2,1,0:T(4,128)(2,1)S(1)}, bf16[5,4,4096]{2,1,0:T(4,128)(2,1)S(1)}, u32[]{:S(2)}, u32[]{:S(2)}) collective-permute-start(bf16[5,4,4096]{2,1,0:T(4,128)(2,1)S(1)} %bitcast.94), channel_id=1, source_target_pairs={{0,9},{1,10},{2,11},{3,12},{4,13},{5,14},{6,15},{7,16},{8,17},{9,1... | collective-permute-start | bytes 491528 | tf_op jit(solution)/shard_map/ppermute | solution.py:32
  58.6 49.2 %collective-permute-start.3 = (bf16[5,4,4096]{2,1,0:T(4,128)(2,1)S(1)}, bf16[5,4,4096]{2,1,0:T(4,128)(2,1)S(1)}, u32[]{:S(2)}, u32[]{:S(2)}) collective-permute-start(bf16[5,4,4096]{2,1,0:T(4,128)(2,1)S(1)} %bitcast.95), channel_id=1, source_target_pairs={{0,2},{1,3},{2,4},{3,5},{4,6},{5,7},{6,8},{7,9},{8,10},{9,11},{10,... | collective-permute-start | bytes 491528 | tf_op jit(solution)/shard_map/ppermute | solution.py:32
  109.4 4.7 %collective-permute-start.4 = (bf16[4096,128]{1,0:T(8,128)(2,1)S(1)}, bf16[4096,128]{1,0:T(8,128)(2,1)}, u32[]{:S(2)}, u32[]{:S(2)}) collective-permute-start(bf16[4096,128]{1,0:T(8,128)(2,1)S(1)} %bitcast.77), channel_id=1, source_target_pairs={{0,128},{128,0},{256,384},{384,256},{512,640},{640,512},{768,896},... | collective-permute-start | bytes 3145736 | tf_op jit(solution)/shard_map/ppermute | solution.py:50
  111.4 5.5 %collective-permute-start.5 = (bf16[4096,128]{1,0:T(8,128)(2,1)S(1)}, bf16[4096,128]{1,0:T(8,128)(2,1)}, u32[]{:S(2)}, u32[]{:S(2)}) collective-permute-start(bf16[4096,128]{1,0:T(8,128)(2,1)S(1)} %bitcast.78), channel_id=1, source_target_pairs={{0,128},{128,0},{256,384},{384,256},{512,640},{640,512},{768,896},... | collective-permute-start | bytes 3145736 | tf_op jit(solution)/shard_map/ppermute | solution.py:50
  116.9 38.7 %copy-start.3 = (bf16[4096,128]{1,0:T(8,128)(2,1)S(1)}, bf16[4096,128]{1,0:T(8,128)(2,1)}, u32[]{:S(2)}) copy-start(bf16[4096,128]{1,0:T(8,128)(2,1)} %get-tuple-element.13) | copy-start | bytes 3145732
  155.6 3.0 %copy-start.4 = (bf16[4096,128]{1,0:T(8,128)(2,1)S(1)}, bf16[4096,128]{1,0:T(8,128)(2,1)}, u32[]{:S(2)}) copy-start(bf16[4096,128]{1,0:T(8,128)(2,1)} %get-tuple-element.11) | copy-start | bytes 3145732
  155.6 3.0 %copy-start.5 = (bf16[4096,128]{1,0:T(8,128)(2,1)S(1)}, bf16[4096,128]{1,0:T(8,128)(2,1)}, u32[]{:S(2)}) copy-start(bf16[4096,128]{1,0:T(8,128)(2,1)} %get-tuple-element.12) | copy-start | bytes 3145732
  155.6 13.8 %slice-start = ((s8[8388608]{0:T(1024)(128)(4,1)}), s8[4194304]{0:T(1024)(128)(4,1)S(1)}, s32[]{:S(2)}) async-start(s8[8388608]{0:T(1024)(128)(4,1)} %bitcast.73), calls=%async_computation.6 | async-start | bytes 8388608
  158.6 10.8 %slice-start.1 = ((s8[8388608]{0:T(1024)(128)(4,1)}), s8[4194304]{0:T(1024)(128)(4,1)S(1)}, s32[]{:S(2)}) async-start(s8[8388608]{0:T(1024)(128)(4,1)} %bitcast.73), calls=%async_computation.7 | async-start | bytes 8388608
  171.2 30.4 %collective-permute-start.6 = (bf16[5,4,4096]{2,1,0:T(4,128)(2,1)S(1)}, bf16[5,4,4096]{2,1,0:T(4,128)(2,1)S(1)}, u32[]{:S(2)}, u32[]{:S(2)}) collective-permute-start(bf16[5,4,4096]{2,1,0:T(4,128)(2,1)S(1)} %squeeze.41), channel_id=1, source_target_pairs={{0,16},{1,17},{2,18},{3,19},{4,20},{5,21},{6,22},{7,23},{8,24},{9,... | collective-permute-start | bytes 491528 | tf_op jit(solution)/shard_map/ppermute | solution.py:32
  186.8 32.7 %collective-permute-start.7 = (bf16[5,4,4096]{2,1,0:T(4,128)(2,1)S(1)}, bf16[5,4,4096]{2,1,0:T(4,128)(2,1)S(1)}, u32[]{:S(2)}, u32[]{:S(2)}) collective-permute-start(bf16[5,4,4096]{2,1,0:T(4,128)(2,1)S(1)} %squeeze.42), channel_id=1, source_target_pairs={{0,19},{1,20},{2,21},{3,22},{4,23},{5,24},{6,25},{7,26},{8,27},{9,... | collective-permute-start | bytes 491528 | tf_op jit(solution)/shard_map/ppermute | solution.py:32
  196.7 41.1 %collective-permute-start.8 = (bf16[5,4,4096]{2,1,0:T(4,128)(2,1)S(1)}, bf16[5,4,4096]{2,1,0:T(4,128)(2,1)S(1)}, u32[]{:S(2)}, u32[]{:S(2)}) collective-permute-start(bf16[5,4,4096]{2,1,0:T(4,128)(2,1)S(1)} %squeeze.43), channel_id=1, source_target_pairs={{0,23},{1,24},{2,25},{3,26},{4,27},{5,28},{6,29},{7,30},{8,31},{9,... | collective-permute-start | bytes 491528 | tf_op jit(solution)/shard_map/ppermute | solution.py:32
  199.6 44.0 %collective-permute-start.9 = (bf16[5,4,4096]{2,1,0:T(4,128)(2,1)S(1)}, bf16[5,4,4096]{2,1,0:T(4,128)(2,1)S(1)}, u32[]{:S(2)}, u32[]{:S(2)}) collective-permute-start(bf16[5,4,4096]{2,1,0:T(4,128)(2,1)S(1)} %squeeze.44), channel_id=1, source_target_pairs={{0,30},{1,31},{2,0},{3,1},{4,2},{5,3},{6,4},{7,5},{8,6},{9,7},{10,... | collective-permute-start | bytes 491528 | tf_op jit(solution)/shard_map/ppermute | solution.py:32
Sparse Core Ops, SparseCore 0:
  10.1 73.2 all-gather.5
  109.6 45.9 all-gather.3
